TPU v7x, 256 devices: a 2x2x32 block of a 4x8x32 slice. The times are simulated.
256 devices in a mesh: groups: 4 (over y, x), row: 64 (over z, core).
Axes of the slice: x: 2, y: 2, z: 32, core: 2. Of those that a mesh axis runs over, the one named last changes fastest.
The devices are a block of a 4x8x32 slice.
Arguments:
- elevation: float32 [4096, 8192], P(('groups', 'row')), parts along dimension 0, may hold values from -2048 to 4096
- bin_index: int32 [4096, 8192], P(('groups', 'row')), parts along dimension 0, may hold values from 0 to 1023, as said below
- ranks: int32 [8], P('groups'), parts along dimension 0, may hold values from 83886 to 8304713, as said below
Outputs:
- shaded: float32 [4096, 8192], P(('groups', 'row')), parts along dimension 0
There are 4 independent parts, one for each index of `groups`. A program takes and returns all parts, laid end to end along the dimension named above; each array names one. Nothing has to cross between parts.
Inputs may be any that keep to these rules, and one draw needn't show every extreme that they name: The bins have fixed edges: a cell with 0 < bin_index < 1023 has an elevation at or above 2 bin_index and below 2 bin_index + 2; bin 0 holds every elevation below 2 and bin 1024 - 1 every elevation at or above 2046. `ranks`: the first entry lies below 419430 and the second at or above 7969170.
All inputs are finite; a program needn't handle non-finite values.
Results may differ from a plain program's by a relative error of at most 0.0049.
Values sent between devices are 32-bit elements; how exact they have to be, the bound alone decides.
No kernel may reach another device: no remote copies, remote signals or barrier semaphores. Data moves between devices by JAX's collectives and lax.ppermute only.
A program may use at most 64 MiB of HBM per device.

v0:
```python
import jax
import jax.numpy as jnp
from jax import lax
from jax.sharding import PartitionSpec as P

BINS = 1024


binomial = (1.0 / 64, 6.0 / 64, 15.0 / 64, 20.0 / 64, 15.0 / 64, 6.0 / 64, 1.0 / 64)
zfactor = 200.0
cos_zenith = 0.70710678
sin_zenith = 0.70710678
light_x = -0.70710678
light_y = 0.70710678
low_bins = 32


def total_of_pieces(x, axis):
    pieces = lax.all_gather(x, axis)
    return pieces.sum(axis=0)


def sent_to_all(x, axis):
    size = lax.axis_size(axis)
    return lax.all_to_all(jnp.broadcast_to(x[None], (size, *x.shape)), axis, 0, 0, tiled=True)


def taken_together(x, axis):
    everything = sent_to_all(x, axis)
    return jnp.max(everything, axis=0)


def together(arrays, axis):
    ends = [0]
    for a in arrays:
        ends.append(ends[-1] + a.size)
    total = taken_together(jnp.concatenate([a.ravel() for a in arrays]), axis)
    return tuple((total[b:e].reshape(a.shape) for a, b, e in zip(arrays, ends, ends[1:])))


def padded_2(cells, sides, width):
    for axis, dim in sides:
        count = lax.axis_size(axis)
        ends = count - 1
        head = lax.slice_in_dim(cells, 0, width, axis=dim)
        tail = lax.slice_in_dim(cells, cells.shape[dim] - width, cells.shape[dim], axis=dim)
        cells = jnp.concatenate(
            [
                lax.ppermute(tail, axis, [(i, (i + 1) % count) for i in range(ends)]),
                cells,
                lax.ppermute(head, axis, [((i + 1) % count, i) for i in range(ends)]),
            ],
            axis=dim,
        )
    return cells


def filter_cols(padded):
    width = padded.shape[1] - 6
    total = binomial[0] * padded[:, 0:width]
    for offset in range(1, 7):
        total = total + binomial[offset] * padded[:, offset : offset + width]
    return total


def filter_rows(padded):
    height = padded.shape[0] - 6
    total = binomial[0] * padded[0:height, :]
    for offset in range(1, 7):
        total = total + binomial[offset] * padded[offset : offset + height, :]
    return total


def shade(smooth, span):
    height = smooth.shape[0] - 2
    width = smooth.shape[1] - 2

    def window(drow, dcol):
        return smooth[drow : drow + height, dcol : dcol + width]

    east = window(0, 2) + 2.0 * window(1, 2) + window(2, 2)
    west = window(0, 0) + 2.0 * window(1, 0) + window(2, 0)
    south = window(2, 0) + 2.0 * window(2, 1) + window(2, 2)
    north = window(0, 0) + 2.0 * window(0, 1) + window(0, 2)
    scale = zfactor / (8.0 * span)
    grad_x = (east - west) * scale
    grad_y = (south - north) * scale
    light = (cos_zenith - sin_zenith * (light_x * grad_x + light_y * grad_y)) * lax.rsqrt(
        1.0 + grad_x * grad_x + grad_y * grad_y
    )
    return jnp.maximum(light, 0.0)


def one_hots(block, upper_count):
    upper_idx = block // low_bins
    lower_idx = block % low_bins
    upper_hot = (upper_idx[None, :] == lax.broadcasted_iota(jnp.int32, (upper_count, 1), 0)).astype(
        jnp.bfloat16
    )
    lower_hot = (lower_idx[None, :] == lax.broadcasted_iota(jnp.int32, (low_bins, 1), 0)).astype(
        jnp.bfloat16
    )
    return (upper_hot, lower_hot)


def body(elevation, bin_index, ranks):
    height = elevation.shape[0]
    width = elevation.shape[1]
    upper_count = BINS // low_bins
    blocked = bin_index.reshape(height // 4, 4 * width)

    def count_block(carry, block):
        upper_hot, lower_hot = one_hots(block, upper_count)
        part_counts = lax.dot_general(
            upper_hot, lower_hot, (((1,), (1,)), ((), ())), preferred_element_type=jnp.float32
        )
        return (carry + part_counts, None)

    local_counts, unused = lax.scan(
        count_block, jnp.zeros((upper_count, low_bins), jnp.float32), blocked
    )
    local_counts = local_counts.reshape(BINS)
    local_max = jnp.max(elevation)
    local_min = jnp.min(elevation)
    counts = total_of_pieces(local_counts, "row")
    highest, neg_lowest = together((local_max, -local_min), "row")
    lowest = -neg_lowest
    span = highest - lowest
    cumulative = jnp.cumsum(counts.astype(jnp.int32), dtype=jnp.int32)
    table = jnp.clip(
        (cumulative - ranks[0]).astype(jnp.float32) / (ranks[1] - ranks[0]).astype(jnp.float32),
        0.0,
        1.0,
    ).astype(jnp.bfloat16)
    stretch = jnp.take(table.astype(jnp.float32), bin_index, axis=0)
    extended = padded_2(elevation, (("row", 0),), 4)
    smooth = filter_rows(filter_cols(jnp.pad(extended, ((0, 0), (4, 4)))))
    light = shade(smooth, span)
    return stretch * (0.5 + light)


def solution(mesh):
    in_specs = (P(("groups", "row"), None), P(("groups", "row"), None), P("groups"))
    out_specs = P(("groups", "row"), None)
    return jax.shard_map(body, mesh=mesh, in_specs=in_specs, out_specs=out_specs, check_vma=False)
```

profile of v0, /device:TPU:37, one launch (start us, length us, event | category | flops | bytes accessed | tf_op | source)
XLA Modules:
  0.0 648.0 jit_solution(2977505616675468371)
XLA Ops:
  0.0 1.9 fusion.30
  2.6 0.7 pad_maximum_fusion
  3.3 0.6 broadcast_in_dim.22
  4.0 34.4 %all-to-all-start = ((f32[64,1,2]{2,1,0:T(1,128)}), f32[64,1,2]{2,1,0:T(1,128)}, u32[]{:S(2)}, u32[]{:S(2)}) async-start(f32[64,1,2]{2,1,0:T(1,128)} %broadcast_in_dim.22), calls=%async_computation | async-start | bytes 65536 | tf_op jit(solution)/shard_map/all_to_all | solution.py:25
  38.3 1.8 fusion.31
  40.1 3.6 collective-permute-start
  43.7 2.0 collective-permute-start.1
  45.6 0.0 copy-start.3
  45.7 0.3 reshape.47
  46.0 0.1 fusion.29
  46.1 0.2 copy-done.3
  46.3 0.6 fusion.33
  48.2 10.7 %while.13 = (s32[]{:T(128)}, f32[32,32]{1,0:T(8,128)S(1)}, s32[4,32768]{1,0:T(4,128)S(1)}, s32[]{:T(128)}, s32[]{:T(128)}) while((s32[]{:T(128)}, f32[32,32]{1,0:T(8,128)S(1)}, s32[4,32768]{1,0:T(4,128)S(1)}, s32[]{:T(128)}, s32[]{:T(128)}) %tuple.37), condition=%wide.region_1.2_spmd.clone, body=%wide.region_0.1_spmd.clone.sunk | while | flops 69863424 | bytes 3022931 | solution.py:119
  48.2 0.6 and_select_fusion.4
  48.9 0.2 and_select_fusion.5
  49.1 0.5 iota_compare_fusion.20
  49.6 1.3 fusion.38
  50.9 0.6 and_select_fusion.4
  51.6 0.2 and_select_fusion.5
  51.8 0.5 iota_compare_fusion.20
  52.3 1.3 fusion.38
  53.6 0.6 and_select_fusion.4
  54.2 0.2 and_select_fusion.5
  54.4 0.5 iota_compare_fusion.20
  55.0 1.3 fusion.38
  56.3 0.6 and_select_fusion.4
  56.9 0.2 and_select_fusion.5
  57.1 0.5 iota_compare_fusion.20
  57.7 1.3 fusion.38
  58.9 0.1 reshape.66
  59.0 58.1 %all-gather = f32[64,1,1024]{2,1,0:T(1,128)S(1)} all-gather(f32[1,1,1024]{2,1,0:T(1,128)S(1)} %reshape.66), channel_id=1, replica_groups=mesh['groups'=4,'row'=64] {'row'}, dimensions={0}, use_global_device_ids=true | all-gather | bytes 266240 | tf_op jit(solution)/shard_map/all_gather | solution.py:19
  117.1 0.2 reduce_sum.9
  117.3 0.3 reduce-window.9
  117.6 0.1 slice.96
  117.7 0.1 slice_reduce_fusion
  117.8 0.1 copy.8
  117.9 0.1 broadcast_clamp_fusion
  118.0 0.7 bitcast_convert_fusion
  118.7 520.8 %gather_fusion = f32[131072]{0:T(1024)S(1)} fusion(f32[1024]{0:T(1024)S(1)} %bitcast_convert_fusion, s32[131072]{0:T(1024)S(1)} %broadcast_clamp_fusion), kind=kCustom, calls=%fused_computation | custom fusion | bytes 1572864 | tf_op jit(solution)/shard_map/jit(_take)/gather | solution.py:135
  639.6 0.0 copy-start.2
  639.6 0.1 reshape.57
  639.7 0.9 reduce_max.19
  640.6 0.6 fusion.32
  642.6 1.4 select_maximum_fusion
  643.9 1.3 fusion.10
  645.2 0.6 fusion.4
  645.9 0.4 copy-done.1
  646.3 1.7 add_multiply_fusion
  (10 shorter events, 0.1 us)
Async XLA Ops:
  0.0 45.6 %copy-start = (s32[16,8192]{1,0:T(8,128)S(1)}, s32[16,8192]{1,0:T(8,128)}, u32[]{:S(2)}) copy-start(s32[16,8192]{1,0:T(8,128)} %param.6) | copy-start | bytes 1572868
  4.0 635.7 %all-to-all-start = ((f32[64,1,2]{2,1,0:T(1,128)}), f32[64,1,2]{2,1,0:T(1,128)}, u32[]{:S(2)}, u32[]{:S(2)}) async-start(f32[64,1,2]{2,1,0:T(1,128)} %broadcast_in_dim.22), calls=%async_computation | async-start | bytes 65536 | tf_op jit(solution)/shard_map/all_to_all | solution.py:25
  40.1 602.4 %collective-permute-start = (f32[4,8192]{1,0:T(4,128)}, f32[4,8192]{1,0:T(4,128)}, u32[]{:S(2)}, u32[]{:S(2)}) collective-permute-start(f32[4,8192]{1,0:T(4,128)} %get-tuple-element.72), channel_id=1, source_target_pairs={{0,1},{1,2},{2,3},{3,4},{4,5},{5,6},{6,7},{7,8},{8,9},{9,10},{10,1... | collective-permute-start | bytes 393224 | tf_op jit(solution)/shard_map/ppermute | solution.py:49
  43.7 598.9 %collective-permute-start.1 = (f32[4,8192]{1,0:T(4,128)}, f32[4,8192]{1,0:T(4,128)}, u32[]{:S(2)}, u32[]{:S(2)}) collective-permute-start(f32[4,8192]{1,0:T(4,128)} %get-tuple-element.73), channel_id=1, source_target_pairs={{1,0},{2,1},{3,2},{4,3},{5,4},{6,5},{7,6},{8,7},{9,8},{10,9},{11,1... | collective-permute-start | bytes 393224 | tf_op jit(solution)/shard_map/ppermute | solution.py:51
  45.6 0.7 copy-start.3
  639.6 3.0 copy-start.2
  645.2 1.0 copy-start.1
where the time goes:
time: 648 us
  local copies, waits for them, and re-layouts  526 us (81%)
  blocking collectives  58.1 us (9%)
  starting transfers between devices  39.9 us (6%)
  other arithmetic  15.4 us (2%)
    gather x2, local copies, waits for them, and re-layouts, body(): stretch = jnp.take(table.astype(jnp.float32), bin_index, axis=0)  521 us
    all_gather x1, blocking collectives, total_of_pieces(): pieces = lax.all_gather(x, axis)  58.1 us
    all_to_all x1, starting transfers between devices, sent_to_all(): lax.all_to_all(jnp.broadcast_to(x[None], (size, *x.shape)), axis, 0, 0, t...  34.4 us
  transfers between devices with their start and end apart: 3, of which 0 were waited for; matrix products, arithmetic and copies ran while one was open for 83% of the time, Pallas kernels for 0%

commit v1 on v0

v1 whole, which is shorter than its diff:
```python
import functools

import jax
import jax.numpy as jnp
from jax import lax
from jax.experimental import pallas as pl
from jax.experimental.pallas import tpu as pltpu
from jax.sharding import PartitionSpec as P

BINS = 1024
HALF = BINS // 2
LANES = 128
LOW = 32
WIRE = HALF + LANES

zfactor = 200.0
cos_zenith = 0.70710678
sin_zenith = 0.70710678
light_x = -0.70710678
light_y = 0.70710678
HIGHEST = lax.Precision.HIGHEST


def bin_of(height):
    return jnp.clip(jnp.floor(height * 0.5), 0.0, BINS - 1.0)


def iota(shape, dim):
    return lax.broadcasted_iota(jnp.int32, shape, dim)


def count_kernel(heights, core_ref, keep_ref, send_ref, upper, lower):
    rows, width = heights.shape
    high_count = BINS // LOW
    bins = bin_of(heights[...])
    up = jnp.floor(bins * (1.0 / LOW))
    upper[...] = up
    lower[...] = bins - up * LOW
    row_ids = iota((LOW, width), 0).astype(jnp.float32)
    one = jnp.float32(1.0)
    zero = jnp.float32(0.0)

    def step(r, total):
        up_hot = jnp.where(upper[pl.ds(r, 1), :] == row_ids, one, zero).astype(jnp.bfloat16)
        low_hot = jnp.where(lower[pl.ds(r, 1), :] == row_ids, one, zero).astype(jnp.bfloat16)
        return total + lax.dot_general(
            up_hot, low_hot, (((1,), (1,)), ((), ())), preferred_element_type=jnp.float32
        )

    grid = lax.fori_loop(0, rows, step, jnp.zeros((high_count, LOW), jnp.float32))
    spread = (iota((LOW, LANES), 1) % LOW == iota((LOW, LANES), 0)).astype(jnp.float32)
    tiled = jnp.dot(grid, spread, precision=HIGHEST, preferred_element_type=jnp.float32)
    quarter = iota((high_count, LANES), 1) // LOW == iota((high_count, LANES), 0) % 4
    fold = (iota((8, high_count), 1) // 4 == iota((8, high_count), 0)).astype(jnp.float32)
    flat = jnp.dot(
        fold, jnp.where(quarter, tiled, 0.0), precision=HIGHEST, preferred_element_type=jnp.float32
    )
    highest = jnp.max(heights[...])
    neg_lowest = -jnp.min(heights[...])
    first = core_ref[0] == 0
    for i in range(4):
        cols = slice(i * LANES, (i + 1) * LANES)
        keep_ref[:, cols] = jnp.where(first, flat[i : i + 1], flat[4 + i : 5 + i])
        send_ref[:, cols] = jnp.where(first, flat[4 + i : 5 + i], flat[i : i + 1])
    keep_ref[:, HALF:] = jnp.full((1, LANES), jnp.where(first, highest, neg_lowest))
    send_ref[:, HALF:] = jnp.full((1, LANES), jnp.where(first, neg_lowest, highest))


def count(elevation, core):
    shape = jax.ShapeDtypeStruct((1, WIRE), jnp.float32)
    return pl.pallas_call(
        count_kernel,
        out_shape=(shape, shape),
        in_specs=[
            pl.BlockSpec(memory_space=pltpu.VMEM),
            pl.BlockSpec(memory_space=pltpu.SMEM),
        ],
        out_specs=(pl.BlockSpec(memory_space=pltpu.VMEM),) * 2,
        scratch_shapes=[pltpu.VMEM(elevation.shape, jnp.float32)] * 2,
    )(elevation, core)


def spread_kernel(a_ref, b_ref, out_ref):
    a, b = a_ref[...], b_ref[...]
    both = jnp.where(iota(a.shape, 1) < HALF, a + b, jnp.maximum(a, b))
    out_ref[...] = jnp.broadcast_to(both, out_ref.shape)


def gather_kernel(x_ref, out_ref):
    out_ref[:, :HALF] = jnp.sum(x_ref[:, :HALF], axis=0, keepdims=True)
    out_ref[:, HALF:] = jnp.max(x_ref[:, HALF:], axis=0, keepdims=True)


def shade_kernel(mine, theirs, core_ref, ranks, heights, gx_ref, gy_ref, out_ref):
    first = core_ref[0] == 0
    a, b = mine[...], theirs[...]
    lower = jnp.where(first, a, b)
    upper = jnp.where(first, b, a)
    span = lower[:, HALF : HALF + 1] + upper[:, HALF : HALF + 1]
    parts = [lower[:, i * LANES : (i + 1) * LANES] for i in range(4)]
    parts += [upper[:, i * LANES : (i + 1) * LANES] for i in range(4)]
    counts = jnp.concatenate(parts, axis=0)
    upto = (iota((LANES, LANES), 0) <= iota((LANES, LANES), 1)).astype(jnp.float32)
    inside = jnp.dot(counts, upto, precision=HIGHEST, preferred_element_type=jnp.float32)
    ones = jnp.ones((LANES, LANES), jnp.float32)
    totals = jnp.dot(counts, ones, precision=HIGHEST, preferred_element_type=jnp.float32)
    before = (iota((8, 8), 1) < iota((8, 8), 0)).astype(jnp.float32)
    ahead = jnp.dot(before, totals, precision=HIGHEST, preferred_element_type=jnp.float32)
    cumulative = (inside + ahead).astype(jnp.int32)
    table = jnp.clip(
        (cumulative - ranks[0]).astype(jnp.float32)
        / jnp.full(cumulative.shape, ranks[1] - ranks[0]).astype(jnp.float32),
        0.0,
        1.0,
    )
    table = table.astype(jnp.bfloat16).astype(jnp.float32)
    rows, width = heights.shape
    scale = zfactor / (8.0 * span)
    tables = [jnp.broadcast_to(table[r : r + 1], (rows, LANES)) for r in range(8)]
    for c in range(width // LANES):
        cols = slice(c * LANES, (c + 1) * LANES)
        bins = bin_of(heights[:, cols]).astype(jnp.int32)
        low = bins & (LANES - 1)
        high = bins >> 7
        found = [
            jnp.take_along_axis(t, low, axis=1, mode="promise_in_bounds") for t in tables
        ]
        for bit in range(3):
            odd = (high & (1 << bit)) != 0
            found = [jnp.where(odd, found[2 * i + 1], found[2 * i]) for i in range(len(found) // 2)]
        gx = gx_ref[:, cols] * scale
        gy = gy_ref[:, cols] * scale
        light = (cos_zenith - sin_zenith * (light_x * gx + light_y * gy)) * lax.rsqrt(
            1.0 + gx * gx + gy * gy
        )
        out_ref[:, cols] = found[0] * (0.5 + jnp.maximum(light, 0.0))


def shade(mine, theirs, core, ranks, elevation, gx, gy):
    vmem = pl.BlockSpec(memory_space=pltpu.VMEM)
    smem = pl.BlockSpec(memory_space=pltpu.SMEM)
    return pl.pallas_call(
        shade_kernel,
        out_shape=jax.ShapeDtypeStruct(elevation.shape, jnp.float32),
        in_specs=[vmem, vmem, smem, smem, vmem, vmem, vmem],
        out_specs=vmem,
    )(mine, theirs, core, ranks, elevation, gx, gy)


def pairs_added(x, times, dim):
    for _ in range(times):
        n = x.shape[dim] - 1
        x = lax.slice_in_dim(x, 0, n, axis=dim) + lax.slice_in_dim(x, 1, n + 1, axis=dim)
    return x


def gradients(extended):
    common = pairs_added(extended, 7, 0)
    common = pairs_added(jnp.pad(common, ((0, 0), (4, 4))), 7, 1) * (1.0 / 4096)
    east = common[:, 1:] - common[:, :-1]
    south = common[:, 1:] + common[:, :-1]
    return east[1:] + east[:-1], south[1:] - south[:-1]


def body(elevation, ranks):
    size = lax.axis_size("row")
    core = (lax.axis_index("row") % 2).astype(jnp.int32).reshape(1)
    partner = [(i, i ^ 1) for i in range(size)]
    same_core = [list(range(c, size, 2)) for c in range(2)]
    keep, send = count(elevation, core)
    received = lax.ppermute(send, "row", partner)
    spread = pl.pallas_call(
        spread_kernel, out_shape=jax.ShapeDtypeStruct((size // 2, WIRE), jnp.float32)
    )(keep, received)
    everyone = lax.all_to_all(spread, "row", 0, 0, axis_index_groups=same_core, tiled=True)

    head = elevation[:4]
    tail = elevation[-4:]
    above = lax.ppermute(tail, "row", [(i, i + 1) for i in range(size - 1)])
    below = lax.ppermute(head, "row", [(i + 1, i) for i in range(size - 1)])
    gx, gy = gradients(jnp.concatenate([above, elevation, below], axis=0))

    mine = pl.pallas_call(
        gather_kernel, out_shape=jax.ShapeDtypeStruct((1, WIRE), jnp.float32)
    )(everyone)
    theirs = lax.ppermute(mine, "row", partner)
    return shade(mine, theirs, core, ranks, elevation, gx, gy)


def solution(mesh):
    whole = P(("groups", "row"), None)
    mapped = jax.shard_map(
        body, mesh=mesh, in_specs=(whole, P("groups")), out_specs=whole, check_vma=False
    )

    def run(elevation, bin_index, ranks):
        return mapped(elevation, ranks)

    return run
```

time: 648 us -> 89.9 us (0.14)
  local copies, waits for them, and re-layouts: 526 us -> 4.5 us
  blocking collectives: 58.1 us -> 0 us
  waiting for transfers between devices: 0.01 us -> 23.5 us
  Pallas kernels: 0 us -> 14.4 us
  other arithmetic: 15.4 us -> 4.14 us
    gather x2 -> x0, local copies, waits for them, and re-layouts: 521 us -> none  [body(): stretch = jnp.take(table.astype(jnp.float32), bin_index, axis=0)]
    all_gather x1 -> x0, blocking collectives: 58.1 us -> none  [total_of_pieces(): pieces = lax.all_gather(x, axis)]
    all_to_all x1, waiting for transfers between devices: 0.01 us -> 22.1 us  [body(): lax.all_to_all(spread, 'row', 0, 0, axis_index_groups=same_core, tiled=True)]
    ppermute x2 -> x4, starting transfers between devices: 5.51 us -> 26.1 us  [the longest x1 18.6 us: body(): below = lax.ppermute(head, 'row', [(i + 1, i) for i in range(size - 1)])]
    all_to_all x1, starting transfers between devices: 34.4 us -> 16.6 us  [body(): lax.all_to_all(spread, 'row', 0, 0, axis_index_groups=same_core, tiled=True)]
    pallas_call x0 -> x4, Pallas kernels: none -> 14.4 us  [the longest x1 6.76 us: count(): pl.pallas_call(count_kernel, out_shape=(shape, shape), in_specs=[pl.Block...]
  transfers between devices with their start and end apart: 3 -> 5, of which waited for: 0 -> 2; matrix products, arithmetic and copies ran while one was open for 83% -> 6% of each run, Pallas kernels for 0% -> 9%
where the time goes in v1:
time: 89.9 us; the launch traced here: 89.5 us
  starting transfers between devices  42.8 us (48%)
  waiting for transfers between devices  23.5 us (26%)
  Pallas kernels  14.4 us (16%)
  local copies, waits for them, and re-layouts  4.5 us (5%)
  other arithmetic  4.14 us (5%)
    all_to_all x1, waiting for transfers between devices, body(): lax.all_to_all(spread, 'row', 0, 0, axis_index_groups=same_core, tiled=True)  22.1 us
    ppermute x1, starting transfers between devices, body(): below = lax.ppermute(head, 'row', [(i + 1, i) for i in range(size - 1)])  18.6 us
    all_to_all x1, starting transfers between devices, body(): lax.all_to_all(spread, 'row', 0, 0, axis_index_groups=same_core, tiled=True)  16.6 us
    pallas_call x1, Pallas kernels, count(): pl.pallas_call(count_kernel, out_shape=(shape, shape), in_specs=[pl.Block...  6.76 us
    ppermute x1, starting transfers between devices, body(): above = lax.ppermute(tail, 'row', [(i, i + 1) for i in range(size - 1)])  5.22 us
    pallas_call x1, Pallas kernels, shade(): pl.pallas_call(shade_kernel, out_shape=jax.ShapeDtypeStruct(elevation.sha...  4.85 us
    add x13, other arithmetic, pairs_added(): lax.slice_in_dim(x, 0, n, axis=dim)  2.41 us
    ppermute x1, starting transfers between devices, body(): theirs = lax.ppermute(mine, 'row', partner)  2.33 us
  transfers between devices with their start and end apart: 5, of which 2 were waited for; matrix products, arithmetic and copies ran while one was open for 6% of the time, Pallas kernels for 9%

profile of v1, /device:TPU:37, one launch (start us, length us, event | category | flops | bytes accessed | tf_op | source)
XLA Modules:
  0.0 89.5 jit_solution(14822049317690631635)
XLA Ops:
  0.0 1.1 %fusion.1 = (f32[4,8192]{1,0:T(4,128)S(1)}, f32[4,8192]{1,0:T(4,128)S(1)}) fusion(f32[16,8192]{1,0:T(8,128)} %heights.3), kind=kLoop, calls=%fused_computation.21 | loop fusion | bytes 524288 | tf_op jit(solution)/shard_map/slice | solution.py:178
  1.1 0.0 copy-start
  1.1 5.2 %collective-permute-start.2 = (f32[4,8192]{1,0:T(4,128)S(1)}, f32[4,8192]{1,0:T(4,128)S(1)}, u32[]{:S(2)}, u32[]{:S(2)}) collective-permute-start(f32[4,8192]{1,0:T(4,128)S(1)} %get-tuple-element.11), channel_id=1, source_target_pairs={{0,1},{1,2},{2,3},{3,4},{4,5},{5,6},{6,7},{7,8},{8,9},{9,10},{10,1... | collective-permute-start | bytes 393224 | tf_op jit(solution)/shard_map/ppermute | solution.py:179
  6.3 18.6 %collective-permute-start.3 = (f32[4,8192]{1,0:T(4,128)S(1)}, f32[4,8192]{1,0:T(4,128)S(1)}, u32[]{:S(2)}, u32[]{:S(2)}) collective-permute-start(f32[4,8192]{1,0:T(4,128)S(1)} %get-tuple-element.12), channel_id=1, source_target_pairs={{1,0},{2,1},{3,2},{4,3},{5,4},{6,5},{7,6},{8,7},{9,8},{10,9},{11,1... | collective-permute-start | bytes 393224 | tf_op jit(solution)/shard_map/ppermute | solution.py:180
  24.9 6.8 %shard_map.28 = (f32[1,640]{1,0:T(1,128)}, f32[1,640]{1,0:T(1,128)}) custom-call(f32[16,8192]{1,0:T(8,128)} %heights.3, s32[1]{0:T(128)} %bitcast.core_ref), custom_call_target="tpu_custom_call" | custom-call | tf_op jit(solution)/shard_map/pallas_call | solution.py:71
  31.7 0.0 collective-permute-start
  31.7 1.4 %collective-permute-done.b_ref = f32[1,640]{1,0:T(1,128)S(1)} collective-permute-done((f32[1,640]{1,0:T(1,128)}, f32[1,640]{1,0:T(1,128)S(1)}, u32[]{:S(2)}, u32[]{:S(2)}) %collective-permute-start) | collective-permute-done | bytes 2592 | tf_op jit(solution)/shard_map/ppermute | solution.py:171
  33.0 0.0 copy-start.2
  33.1 0.6 copy-done.2
  33.6 1.3 %shard_map.29 = f32[32,640]{1,0:T(8,128)} custom-call(f32[1,640]{1,0:T(1,128)} %get-tuple-element.7.a_ref, f32[1,640]{1,0:T(1,128)} %copy-done.2), custom_call_target="tpu_custom_call" | custom-call | tf_op jit(solution)/shard_map/pallas_call | solution.py:172
  35.0 1.6 %copy.3 = f32[32,1,640]{2,1,0:T(1,128)} copy(f32[32,1,640]{2,0,1:T(8,128)} %bitcast.5) | data formatting | bytes 163840 | tf_op jit(solution)/shard_map/all_to_all | solution.py:175
  36.6 16.6 %all-to-all-start = ((f32[32,1,640]{2,1,0:T(1,128)}), f32[32,1,640]{2,1,0:T(1,128)S(1)}, u32[]{:S(2)}, u32[]{:S(2)}) async-start(f32[32,1,640]{2,1,0:T(1,128)} %copy.3), calls=%async_computation | async-start | bytes 163840 | tf_op jit(solution)/shard_map/all_to_all | solution.py:175
  53.2 0.0 collective-permute-done.2
  53.2 0.0 collective-permute-done.3
  53.2 0.0 copy-done
  53.2 0.1 pad_maximum_fusion
  53.4 0.1 slice_add_fusion.13
  53.4 0.1 slice_add_fusion.12
  53.5 0.1 slice_add_fusion.11
  53.6 0.1 slice_add_fusion.10
  53.7 0.1 slice_add_fusion.9
  53.8 0.1 slice_add_fusion.8
  53.9 0.1 slice_add_fusion.7
  54.0 0.5 slice_add_fusion.6
  54.5 0.3 slice_add_fusion.5
  54.7 0.3 slice_add_fusion.4
  55.0 0.3 slice_add_fusion.3
  55.3 0.3 slice_add_fusion.2
  55.6 0.3 slice_add_fusion.1
  55.8 0.3 fusion
  56.1 0.3 slice_add_fusion.14
  56.4 22.1 %all-to-all-done = f32[32,1,640]{2,1,0:T(1,128)S(1)} async-done(((f32[32,1,640]{2,1,0:T(1,128)}), f32[32,1,640]{2,1,0:T(1,128)S(1)}, u32[]{:S(2)}, u32[]{:S(2)}) %all-to-all-start) | async-done | bytes 81952 | tf_op jit(solution)/shard_map/all_to_all | solution.py:175
  78.5 0.6 copy.6
  79.1 1.5 %shard_map.30.mine = f32[1,640]{1,0:T(1,128)} custom-call(f32[32,640]{1,0:T(8,128)} %bitcast.6), custom_call_target="tpu_custom_call" | custom-call | tf_op jit(solution)/shard_map/pallas_call | solution.py:183
  80.6 2.3 %collective-permute-start.1 = (f32[1,640]{1,0:T(1,128)}, f32[1,640]{1,0:T(1,128)S(1)}, u32[]{:S(2)}, u32[]{:S(2)}) collective-permute-start(f32[1,640]{1,0:T(1,128)} %shard_map.30.mine), channel_id=1, source_target_pairs={{0,1},{1,0},{2,3},{3,2},{4,5},{5,4},{6,7},{7,6},{8,9},{9,8},{10,11... | collective-permute-start | bytes 7688 | tf_op jit(solution)/shard_map/ppermute | solution.py:186
  82.9 1.1 %slice_subtract_fusion.1 = (f32[16,8192]{1,0:T(8,128)}, f32[16,8192]{1,0:T(8,128)}) fusion(f32[17,8192]{1,0:T(8,128)S(1)} %get-tuple-element.9, f32[17,8192]{1,0:T(8,128)S(1)} %get-tuple-element.10), kind=kLoop, calls=%fused_computation.18 | loop fusion | flops 262144 | bytes 3145728 | tf_op jit(solution)/shard_map/sub | solution.py:162
  84.0 0.0 collective-permute-done.1.theirs
  84.0 0.0 copy-start.1
  84.0 0.6 copy-done.1
  84.6 4.8 %shard_map.31 = f32[16,8192]{1,0:T(8,128)} custom-call(f32[1,640]{1,0:T(1,128)} %shard_map.30.mine, f32[1,640]{1,0:T(1,128)} %copy-done.1, s32[1]{0:T(128)} %bitcast.core_ref, s32[2]{0:T(128)} %ranks.1, f32[16,8192]{1,0:T(8,128)} %heights.3, f32[16,8192]{1,0:T(8,128)} %get-tuple-element.14.gx_ref, f32[16,8192]{1,0:T(8,128)} %get-tuple-element.13.gy_ref), custom_call_target="tpu_custom_call" | custom-call | tf_op jit(solution)/shard_map/pallas_call | solution.py:142
Async XLA Ops:
  1.1 52.2 %copy-start = (f32[16,8192]{1,0:T(8,128)S(1)}, f32[16,8192]{1,0:T(8,128)}, u32[]{:S(2)}) copy-start(f32[16,8192]{1,0:T(8,128)} %heights.3) | copy-start | bytes 1572868
  1.1 52.1 %collective-permute-start.2 = (f32[4,8192]{1,0:T(4,128)S(1)}, f32[4,8192]{1,0:T(4,128)S(1)}, u32[]{:S(2)}, u32[]{:S(2)}) collective-permute-start(f32[4,8192]{1,0:T(4,128)S(1)} %get-tuple-element.11), channel_id=1, source_target_pairs={{0,1},{1,2},{2,3},{3,4},{4,5},{5,6},{6,7},{7,8},{8,9},{9,10},{10,1... | collective-permute-start | bytes 393224 | tf_op jit(solution)/shard_map/ppermute | solution.py:179
  6.3 46.9 %collective-permute-start.3 = (f32[4,8192]{1,0:T(4,128)S(1)}, f32[4,8192]{1,0:T(4,128)S(1)}, u32[]{:S(2)}, u32[]{:S(2)}) collective-permute-start(f32[4,8192]{1,0:T(4,128)S(1)} %get-tuple-element.12), channel_id=1, source_target_pairs={{1,0},{2,1},{3,2},{4,3},{5,4},{6,5},{7,6},{8,7},{9,8},{10,9},{11,1... | collective-permute-start | bytes 393224 | tf_op jit(solution)/shard_map/ppermute | solution.py:180
  31.7 1.4 %collective-permute-start = (f32[1,640]{1,0:T(1,128)}, f32[1,640]{1,0:T(1,128)S(1)}, u32[]{:S(2)}, u32[]{:S(2)}) collective-permute-start(f32[1,640]{1,0:T(1,128)} %get-tuple-element.8), channel_id=1, source_target_pairs={{0,1},{1,0},{2,3},{3,2},{4,5},{5,4},{6,7},{7,6},{8,9},{9,8},{10,11... | collective-permute-start | bytes 7688 | tf_op jit(solution)/shard_map/ppermute | solution.py:171
  33.0 0.6 copy-start.2
  36.6 41.9 %all-to-all-start = ((f32[32,1,640]{2,1,0:T(1,128)}), f32[32,1,640]{2,1,0:T(1,128)S(1)}, u32[]{:S(2)}, u32[]{:S(2)}) async-start(f32[32,1,640]{2,1,0:T(1,128)} %copy.3), calls=%async_computation | async-start | bytes 163840 | tf_op jit(solution)/shard_map/all_to_all | solution.py:175
  80.6 3.4 %collective-permute-start.1 = (f32[1,640]{1,0:T(1,128)}, f32[1,640]{1,0:T(1,128)S(1)}, u32[]{:S(2)}, u32[]{:S(2)}) collective-permute-start(f32[1,640]{1,0:T(1,128)} %shard_map.30.mine), channel_id=1, source_target_pairs={{0,1},{1,0},{2,3},{3,2},{4,5},{5,4},{6,7},{7,6},{8,9},{9,8},{10,11... | collective-permute-start | bytes 7688 | tf_op jit(solution)/shard_map/ppermute | solution.py:186
  84.0 0.6 copy-start.1

commit v2 on v1

v2 whole, which is shorter than its diff:
```python
import jax
import jax.numpy as jnp
from jax import lax
from jax.experimental import pallas as pl
from jax.experimental.pallas import tpu as pltpu
from jax.sharding import PartitionSpec as P

BINS = 1024
HALF = BINS // 2
LANES = 128
LOW = 32
WIRE = HALF + LANES

zfactor = 200.0
cos_zenith = 0.70710678
sin_zenith = 0.70710678
light_x = -0.70710678
light_y = 0.70710678
HIGHEST = lax.Precision.HIGHEST


def bin_of(height):
    return jnp.clip(jnp.floor(height * 0.5), 0.0, BINS - 1.0)


def iota(shape, dim):
    return lax.broadcasted_iota(jnp.int32, shape, dim)


def in_vmem(x):
    return pltpu.with_memory_space_constraint(x, pltpu.VMEM)


def count_kernel(heights, core_ref, keep_ref, send_ref, upper, lower):
    rows, width = heights.shape
    high_count = BINS // LOW
    bins = bin_of(heights[...])
    up = jnp.floor(bins * (1.0 / LOW))
    upper[...] = up
    lower[...] = bins - up * LOW
    row_ids = iota((LOW, width), 0).astype(jnp.float32)
    one = jnp.float32(1.0)
    zero = jnp.float32(0.0)
    grid = jnp.zeros((high_count, LOW), jnp.float32)
    for r in range(rows):
        up_hot = jnp.where(upper[r : r + 1, :] == row_ids, one, zero).astype(jnp.bfloat16)
        low_hot = jnp.where(lower[r : r + 1, :] == row_ids, one, zero).astype(jnp.bfloat16)
        grid = grid + lax.dot_general(
            up_hot, low_hot, (((1,), (1,)), ((), ())), preferred_element_type=jnp.float32
        )
    spread = (iota((LOW, LANES), 1) % LOW == iota((LOW, LANES), 0)).astype(jnp.float32)
    tiled = jnp.dot(grid, spread, precision=HIGHEST, preferred_element_type=jnp.float32)
    quarter = iota((high_count, LANES), 1) // LOW == iota((high_count, LANES), 0) % 4
    fold = (iota((8, high_count), 1) // 4 == iota((8, high_count), 0)).astype(jnp.float32)
    flat = jnp.dot(
        fold, jnp.where(quarter, tiled, 0.0), precision=HIGHEST, preferred_element_type=jnp.float32
    )
    highest = jnp.max(heights[...])
    neg_lowest = -jnp.min(heights[...])
    first = core_ref[0] == 0
    for i in range(4):
        cols = slice(i * LANES, (i + 1) * LANES)
        keep_ref[:, cols] = jnp.where(first, flat[i : i + 1], flat[4 + i : 5 + i])
        send_ref[:, cols] = jnp.where(first, flat[4 + i : 5 + i], flat[i : i + 1])
    keep_ref[:, HALF:] = jnp.full((1, LANES), jnp.where(first, highest, neg_lowest))
    send_ref[:, HALF:] = jnp.full((1, LANES), jnp.where(first, neg_lowest, highest))


VMEM_SPEC = pl.BlockSpec(memory_space=pltpu.VMEM)
SMEM_SPEC = pl.BlockSpec(memory_space=pltpu.SMEM)


def count(elevation, core):
    shape = pltpu.VMEM((1, WIRE), jnp.float32)
    return pl.pallas_call(
        count_kernel,
        out_shape=(shape, shape),
        in_specs=[VMEM_SPEC, SMEM_SPEC],
        out_specs=(VMEM_SPEC,) * 2,
        scratch_shapes=[pltpu.VMEM(elevation.shape, jnp.float32)] * 2,
        name="count",
    )(elevation, core)


def join_kernel(a_ref, b_ref, out_ref):
    a, b = a_ref[...], b_ref[...]
    both = jnp.where(iota(a.shape, 1) < HALF, a + b, jnp.maximum(a, b))
    out_ref[...] = jnp.broadcast_to(both[None], out_ref.shape)


def join(a, b, copies):
    return pl.pallas_call(
        join_kernel,
        out_shape=pltpu.VMEM((copies, *a.shape), jnp.float32),
        in_specs=[VMEM_SPEC] * 2,
        out_specs=VMEM_SPEC,
        name="join",
    )(a, b)


def gather_kernel(x_ref, out_ref):
    x = x_ref[...]
    out_ref[:, :HALF] = jnp.sum(x[:, :, :HALF], axis=0)
    out_ref[:, HALF:] = jnp.max(x[:, :, HALF:], axis=0)


def gather(everyone):
    return pl.pallas_call(
        gather_kernel,
        out_shape=pltpu.VMEM((1, WIRE), jnp.float32),
        in_specs=[VMEM_SPEC],
        out_specs=VMEM_SPEC,
        name="gather",
    )(everyone)


def gradient_kernel(above, middle, below, gx_ref, gy_ref, wide):
    rows, width = middle.shape
    halo = above.shape[0]
    edge = jnp.zeros((rows + 2 * halo, LANES), jnp.float32)
    wide[:, :LANES] = edge
    wide[:, LANES + width :] = edge
    wide[:halo, LANES : LANES + width] = above[...]
    wide[halo : halo + rows, LANES : LANES + width] = middle[...]
    wide[halo + rows :, LANES : LANES + width] = below[...]
    chunk = 4 * LANES
    for c in range(0, width, chunk):
        x = wide[:, c : c + chunk + 2 * LANES]
        tall, across = x.shape
        for _ in range(7):
            x = x + pltpu.roll(x, tall - 1, 0)
        for _ in range(4):
            x = x + pltpu.roll(x, 1, 1)
        for _ in range(3):
            x = x + pltpu.roll(x, across - 1, 1)
        x = x * (1.0 / 4096)
        ahead = pltpu.roll(x, across - 1, 1)
        east = ahead - x
        both = ahead + x
        gx = east + pltpu.roll(east, tall - 1, 0)
        gy = pltpu.roll(both, tall - 1, 0) - both
        gx_ref[:, c : c + chunk] = gx[:rows, LANES : LANES + chunk]
        gy_ref[:, c : c + chunk] = gy[:rows, LANES : LANES + chunk]


def gradients(above, middle, below):
    rows, width = middle.shape
    shape = pltpu.VMEM(middle.shape, jnp.float32)
    return pl.pallas_call(
        gradient_kernel,
        out_shape=(shape, shape),
        in_specs=[VMEM_SPEC] * 3,
        out_specs=(VMEM_SPEC,) * 2,
        scratch_shapes=[
            pltpu.VMEM((rows + 2 * above.shape[0], width + 2 * LANES), jnp.float32)
        ],
        name="gradients",
    )(above, middle, below)


def shade_kernel(mine, theirs, core_ref, ranks, heights, gx_ref, gy_ref, out_ref, held, scale_ref):
    step = pl.program_id(0)

    @pl.when(step == 0)
    def _():
        first = core_ref[0] == 0
        a, b = mine[...], theirs[...]
        lower = jnp.where(first, a, b)
        upper = jnp.where(first, b, a)
        span = lower[:, HALF:] + upper[:, HALF:]
        scale_ref[...] = zfactor / (8.0 * span)
        parts = [lower[:, i * LANES : (i + 1) * LANES] for i in range(4)]
        parts += [upper[:, i * LANES : (i + 1) * LANES] for i in range(4)]
        counts = jnp.concatenate(parts, axis=0)
        upto = (iota((LANES, LANES), 0) <= iota((LANES, LANES), 1)).astype(jnp.float32)
        inside = jnp.dot(counts, upto, precision=HIGHEST, preferred_element_type=jnp.float32)
        totals = jnp.broadcast_to(jnp.sum(counts, axis=1, keepdims=True), counts.shape)
        rows = iota(counts.shape, 0)
        ahead = jnp.zeros(counts.shape, jnp.float32)
        for r in range(7):
            ahead = ahead + jnp.where(rows > r, totals[r : r + 1], 0.0)
        cumulative = (inside + ahead).astype(jnp.int32)
        table = jnp.clip(
            (cumulative - ranks[0]).astype(jnp.float32)
            / jnp.full(cumulative.shape, ranks[1] - ranks[0]).astype(jnp.float32),
            0.0,
            1.0,
        )
        held[...] = table.astype(jnp.bfloat16).astype(jnp.float32)

    rows, width = out_ref.shape
    tables = [jnp.broadcast_to(held[r : r + 1], (rows, LANES)) for r in range(8)]
    scale = scale_ref[...]
    for c in range(width // LANES):
        cols = pl.ds(pl.multiple_of(step * width + c * LANES, LANES), LANES)
        bins = bin_of(heights[:, cols]).astype(jnp.int32)
        low = bins & (LANES - 1)
        high = bins >> 7
        found = [
            jnp.take_along_axis(t, low, axis=1, mode="promise_in_bounds") for t in tables
        ]
        for bit in range(3):
            odd = (high & (1 << bit)) != 0
            found = [jnp.where(odd, found[2 * i + 1], found[2 * i]) for i in range(len(found) // 2)]
        gx = gx_ref[:, cols] * scale
        gy = gy_ref[:, cols] * scale
        light = (cos_zenith - sin_zenith * (light_x * gx + light_y * gy)) * lax.rsqrt(
            1.0 + gx * gx + gy * gy
        )
        out_ref[:, c * LANES : (c + 1) * LANES] = found[0] * (0.5 + jnp.maximum(light, 0.0))


def shade(mine, theirs, core, ranks, elevation, gx, gy):
    rows, width = elevation.shape
    steps = 4
    return pl.pallas_call(
        shade_kernel,
        grid=(steps,),
        out_shape=jax.ShapeDtypeStruct(elevation.shape, jnp.float32),
        in_specs=[VMEM_SPEC, VMEM_SPEC, SMEM_SPEC, SMEM_SPEC, VMEM_SPEC, VMEM_SPEC, VMEM_SPEC],
        out_specs=pl.BlockSpec((rows, width // steps), lambda i: (0, i)),
        scratch_shapes=[pltpu.VMEM((8, LANES), jnp.float32), pltpu.VMEM((1, LANES), jnp.float32)],
        name="shade",
    )(mine, theirs, core, ranks, elevation, gx, gy)


def body(elevation, ranks):
    size = lax.axis_size("row")
    core = lax.axis_index("row") & 1
    core = core.astype(jnp.int32).reshape(1)
    partner = [(i, i ^ 1) for i in range(size)]
    chips = size // 2
    begin = chips * 5 // 8
    order = [(i + begin) % chips for i in range(chips)]
    same_core = [[2 * i + c for i in order] for c in range(2)]
    local = in_vmem(elevation)
    keep, send = count(local, core)
    received = lax.ppermute(send, "row", partner)
    spread = join(in_vmem(keep), in_vmem(received), chips)
    everyone = lax.all_to_all(spread, "row", 0, 0, axis_index_groups=same_core, tiled=True)

    above = lax.ppermute(elevation[-4:], "row", [(i, i + 1) for i in range(size - 1)])
    below = lax.ppermute(elevation[:4], "row", [(i + 1, i) for i in range(size - 1)])
    gx, gy = gradients(in_vmem(above), local, in_vmem(below))

    mine = gather(in_vmem(everyone))
    theirs = lax.ppermute(mine, "row", partner)
    return shade(
        in_vmem(mine), in_vmem(theirs), core, ranks, local, in_vmem(gx), in_vmem(gy)
    )


def solution(mesh):
    whole = P(("groups", "row"), None)
    mapped = jax.shard_map(
        body, mesh=mesh, in_specs=(whole, P("groups")), out_specs=whole, check_vma=False
    )

    def run(elevation, bin_index, ranks):
        return mapped(elevation, ranks)

    return run
```

time: 89.9 us -> 69.6 us (0.77)
  waiting for transfers between devices: 23.5 us -> 7.39 us
  other arithmetic: 4.14 us -> 0 us
  local copies, waits for them, and re-layouts: 4.5 us -> 1.09 us
  starting transfers between devices: 42.8 us -> 45.7 us
    ppermute x1, starting transfers between devices: 0.01 us -> 20.5 us  [body(): received = lax.ppermute(send, 'row', partner)]
    ppermute x2, starting transfers between devices: 23.8 us -> 5.86 us  [the longest x1 3.02 us: body(): lax.ppermute(elevation[-4:], 'row', [(i, i + 1) for i in range(size - 1)])]
    all_to_all x1, waiting for transfers between devices: 22.1 us -> 6.56 us  [body(): lax.all_to_all(spread, 'row', 0, 0, axis_index_groups=same_core, tiled=True)]
    add x14 -> x0, other arithmetic: 2.68 us -> none  [the longest x13 2.41 us: pairs_added(): lax.slice_in_dim(x, 0, n, axis=dim)]
    all_to_all x1 -> x0, local copies, waits for them, and re-layouts: 1.6 us -> none  [body(): lax.all_to_all(spread, 'row', 0, 0, axis_index_groups=same_core, tiled=True)]
    all_to_all x1, starting transfers between devices: 16.6 us -> 18 us  [body(): lax.all_to_all(spread, 'row', 0, 0, axis_index_groups=same_core, tiled=True)]
    sub x1 -> x0, other arithmetic: 1.08 us -> none  [gradients(): return (east[1:] + east[:-1], south[1:] - south[:-1])]
    ppermute x1, starting transfers between devices: 2.33 us -> 1.28 us  [body(): theirs = lax.ppermute(mine, 'row', partner)]
  transfers between devices with their start and end apart: 5 -> 5, of which waited for: 2 -> 2; matrix products, arithmetic and copies ran while one was open for 6% -> 0% of each run, Pallas kernels for 9% -> 11%
where the time goes in v2:
time: 69.6 us; the launch traced here: 69.3 us
  starting transfers between devices  45.7 us (66%)
  Pallas kernels  15.1 us (22%)
  waiting for transfers between devices  7.39 us (11%)
  local copies, waits for them, and re-layouts  1.09 us (2%)
    ppermute x1, starting transfers between devices, body(): received = lax.ppermute(send, 'row', partner)  20.5 us
    all_to_all x1, starting transfers between devices, body(): lax.all_to_all(spread, 'row', 0, 0, axis_index_groups=same_core, tiled=True)  18 us
    pallas_call x1, Pallas kernels, gradients(): pl.pallas_call(gradient_kernel, out_shape=(shape, shape), in_specs=[VMEM_...  7.58 us
    all_to_all x1, waiting for transfers between devices, body(): lax.all_to_all(spread, 'row', 0, 0, axis_index_groups=same_core, tiled=True)  6.56 us
    pallas_call x1, Pallas kernels, shade(): pl.pallas_call(shade_kernel, grid=(steps,), out_shape=jax.ShapeDtypeStruc...  4.1 us
    ppermute x1, starting transfers between devices, body(): lax.ppermute(elevation[-4:], 'row', [(i, i + 1) for i in range(size - 1)])  3.02 us
    ppermute x1, starting transfers between devices, body(): lax.ppermute(elevation[:4], 'row', [(i + 1, i) for i in range(size - 1)])  2.84 us
    pallas_call x1, Pallas kernels, count(): pl.pallas_call(count_kernel, out_shape=(shape, shape), in_specs=[VMEM_SPE...  2.74 us
  transfers between devices with their start and end apart: 5, of which 2 were waited for; matrix products, arithmetic and copies ran while one was open for 0% of the time, Pallas kernels for 11%

profile of v2, /device:TPU:37, one launch (start us, length us, event | category | flops | bytes accessed | tf_op | source)
XLA Modules:
  0.0 69.3 jit_solution(16313213928124189461)
XLA Ops:
  0.0 0.0 copy-start
  0.0 1.0 %copy-done = f32[16,8192]{1,0:T(8,128)S(1)} copy-done((f32[16,8192]{1,0:T(8,128)S(1)}, f32[16,8192]{1,0:T(8,128)}, u32[]{:S(2)}) %copy-start) | copy-done | bytes 524312
  1.0 0.0 copy-start.1
  1.0 2.7 %count.1 = (f32[1,640]{1,0:T(1,128)S(1)}, f32[1,640]{1,0:T(1,128)S(1)}) custom-call(f32[16,8192]{1,0:T(8,128)S(1)} %copy-done, s32[1]{0:T(128)} %bitcast.core_ref), custom_call_target="tpu_custom_call" | custom-call | tf_op jit(solution)/shard_map/count/pallas_call | solution.py:75
  3.8 20.5 %collective-permute-start = (f32[1,640]{1,0:T(1,128)S(1)}, f32[1,640]{1,0:T(1,128)S(1)}, u32[]{:S(2)}, u32[]{:S(2)}) collective-permute-start(f32[1,640]{1,0:T(1,128)S(1)} %get-tuple-element.10), channel_id=1, source_target_pairs={{0,1},{1,0},{2,3},{3,2},{4,5},{5,4},{6,7},{7,6},{8,9},{9,8},{10,11... | collective-permute-start | bytes 7688 | tf_op jit(solution)/shard_map/ppermute | solution.py:238
  24.3 0.8 %collective-permute-done.b_ref = f32[1,640]{1,0:T(1,128)S(1)} collective-permute-done((f32[1,640]{1,0:T(1,128)S(1)}, f32[1,640]{1,0:T(1,128)S(1)}, u32[]{:S(2)}, u32[]{:S(2)}) %collective-permute-start) | collective-permute-done | bytes 2592 | tf_op jit(solution)/shard_map/ppermute | solution.py:238
  25.1 0.7 join.1
  25.7 18.0 %all-to-all-start = ((f32[32,1,640]{2,1,0:T(1,128)}), f32[32,1,640]{2,1,0:T(1,128)S(1)}, u32[]{:S(2)}, u32[]{:S(2)}) async-start(f32[32,1,640]{2,1,0:T(1,128)} %join.1), calls=%async_computation | async-start | bytes 163840 | tf_op jit(solution)/shard_map/all_to_all | solution.py:240
  43.8 0.0 copy-done.1
  43.8 2.8 %collective-permute-start.3 = (f32[4,8192]{1,0:T(4,128)S(1)}, f32[4,8192]{1,0:T(4,128)S(1)}, u32[]{:S(2)}, u32[]{:S(2)}) collective-permute-start(f32[4,8192]{1,0:T(4,128)S(1)} %get-tuple-element.13), channel_id=1, source_target_pairs={{1,0},{2,1},{3,2},{4,3},{5,4},{6,5},{7,6},{8,7},{9,8},{10,9},{11,1... | collective-permute-start | bytes 393224 | tf_op jit(solution)/shard_map/ppermute | solution.py:243
  46.7 3.0 %collective-permute-start.2 = (f32[4,8192]{1,0:T(4,128)S(1)}, f32[4,8192]{1,0:T(4,128)S(1)}, u32[]{:S(2)}, u32[]{:S(2)}) collective-permute-start(f32[4,8192]{1,0:T(4,128)S(1)} %get-tuple-element.14), channel_id=1, source_target_pairs={{0,1},{1,2},{2,3},{3,4},{4,5},{5,6},{6,7},{7,8},{8,9},{9,10},{10,1... | collective-permute-start | bytes 393224 | tf_op jit(solution)/shard_map/ppermute | solution.py:242
  49.7 6.6 %all-to-all-done.x_ref = f32[32,1,640]{2,1,0:T(1,128)S(1)} async-done(((f32[32,1,640]{2,1,0:T(1,128)}), f32[32,1,640]{2,1,0:T(1,128)S(1)}, u32[]{:S(2)}, u32[]{:S(2)}) %all-to-all-start) | async-done | bytes 81952 | tf_op jit(solution)/shard_map/all_to_all | solution.py:240
  56.3 0.1 gather.1.mine
  56.3 1.3 %collective-permute-start.1 = (f32[1,640]{1,0:T(1,128)S(1)}, f32[1,640]{1,0:T(1,128)S(1)}, u32[]{:S(2)}, u32[]{:S(2)}) collective-permute-start(f32[1,640]{1,0:T(1,128)S(1)} %gather.1.mine), channel_id=1, source_target_pairs={{0,1},{1,0},{2,3},{3,2},{4,5},{5,4},{6,7},{7,6},{8,9},{9,8},{10,11... | collective-permute-start | bytes 7688 | tf_op jit(solution)/shard_map/ppermute | solution.py:247
  57.6 0.0 collective-permute-done.3.below
  57.6 0.0 collective-permute-done.2.above
  57.6 7.6 %gradients.1 = (f32[16,8192]{1,0:T(8,128)S(1)}, f32[16,8192]{1,0:T(8,128)S(1)}) custom-call(f32[4,8192]{1,0:T(4,128)S(1)} %collective-permute-done.2.above, f32[16,8192]{1,0:T(8,128)S(1)} %copy-done.1, f32[4,8192]{1,0:T(4,128)S(1)} %collective-permute-done.3.below), custom_call_target="tpu_custom_call" | custom-call | tf_op jit(solution)/shard_map/gradients/pallas_call | solution.py:149
  65.2 0.0 collective-permute-done.1.theirs
  65.2 4.1 %shade.1 = f32[16,8192]{1,0:T(8,128)} custom-call(f32[1,640]{1,0:T(1,128)S(1)} %gather.1.mine, f32[1,640]{1,0:T(1,128)S(1)} %collective-permute-done.1.theirs, s32[1]{0:T(128)} %bitcast.core_ref, s32[2]{0:T(128)} %ranks.1, f32[16,8192]{1,0:T(8,128)S(1)} %copy-done.1, f32[16,8192]{1,0:T(8,128)S(1)} %get-tuple-element.11.gx_ref, ...), custom_call_target="tpu_custom_call" | custom-call | tf_op jit(solution)/shard_map/shade/pallas_call | solution.py:216
  (1 shorter events, 0.0 us)
Async XLA Ops:
  0.0 1.0 %copy-start = (f32[16,8192]{1,0:T(8,128)S(1)}, f32[16,8192]{1,0:T(8,128)}, u32[]{:S(2)}) copy-start(f32[16,8192]{1,0:T(8,128)} %heights.3) | copy-start | bytes 1572868
  1.0 42.7 %copy-start.1 = (f32[16,8192]{1,0:T(8,128)S(1)}, f32[16,8192]{1,0:T(8,128)}, u32[]{:S(2)}) copy-start(f32[16,8192]{1,0:T(8,128)} %heights.3) | copy-start | bytes 1572868
  3.8 21.3 %collective-permute-start = (f32[1,640]{1,0:T(1,128)S(1)}, f32[1,640]{1,0:T(1,128)S(1)}, u32[]{:S(2)}, u32[]{:S(2)}) collective-permute-start(f32[1,640]{1,0:T(1,128)S(1)} %get-tuple-element.10), channel_id=1, source_target_pairs={{0,1},{1,0},{2,3},{3,2},{4,5},{5,4},{6,7},{7,6},{8,9},{9,8},{10,11... | collective-permute-start | bytes 7688 | tf_op jit(solution)/shard_map/ppermute | solution.py:238
  25.7 30.5 %all-to-all-start = ((f32[32,1,640]{2,1,0:T(1,128)}), f32[32,1,640]{2,1,0:T(1,128)S(1)}, u32[]{:S(2)}, u32[]{:S(2)}) async-start(f32[32,1,640]{2,1,0:T(1,128)} %join.1), calls=%async_computation | async-start | bytes 163840 | tf_op jit(solution)/shard_map/all_to_all | solution.py:240
  43.8 13.8 %collective-permute-start.3 = (f32[4,8192]{1,0:T(4,128)S(1)}, f32[4,8192]{1,0:T(4,128)S(1)}, u32[]{:S(2)}, u32[]{:S(2)}) collective-permute-start(f32[4,8192]{1,0:T(4,128)S(1)} %get-tuple-element.13), channel_id=1, source_target_pairs={{1,0},{2,1},{3,2},{4,3},{5,4},{6,5},{7,6},{8,7},{9,8},{10,9},{11,1... | collective-permute-start | bytes 393224 | tf_op jit(solution)/shard_map/ppermute | solution.py:243
  46.7 10.9 %collective-permute-start.2 = (f32[4,8192]{1,0:T(4,128)S(1)}, f32[4,8192]{1,0:T(4,128)S(1)}, u32[]{:S(2)}, u32[]{:S(2)}) collective-permute-start(f32[4,8192]{1,0:T(4,128)S(1)} %get-tuple-element.14), channel_id=1, source_target_pairs={{0,1},{1,2},{2,3},{3,4},{4,5},{5,6},{6,7},{7,8},{8,9},{9,10},{10,1... | collective-permute-start | bytes 393224 | tf_op jit(solution)/shard_map/ppermute | solution.py:242
  56.3 8.9 %collective-permute-start.1 = (f32[1,640]{1,0:T(1,128)S(1)}, f32[1,640]{1,0:T(1,128)S(1)}, u32[]{:S(2)}, u32[]{:S(2)}) collective-permute-start(f32[1,640]{1,0:T(1,128)S(1)} %gather.1.mine), channel_id=1, source_target_pairs={{0,1},{1,0},{2,3},{3,2},{4,5},{5,4},{6,7},{7,6},{8,9},{9,8},{10,11... | collective-permute-start | bytes 7688 | tf_op jit(solution)/shard_map/ppermute | solution.py:247

commit v3 on v2

--- a/solution.py
+++ b/solution.py
@@ -124,23 +124,29 @@
     wide[halo : halo + rows, LANES : LANES + width] = middle[...]
     wide[halo + rows :, LANES : LANES + width] = below[...]
     chunk = 4 * LANES
+    tall = rows + 2 * halo
+    for c in range(0, width, chunk):
+        x = wide[:, LANES + c : LANES + c + chunk]
+        for _ in range(7):
+            x = x + pltpu.roll(x, tall - 1, 0)
+        wide[:, LANES + c : LANES + c + chunk] = x * (1.0 / 4096)
     for c in range(0, width, chunk):
         x = wide[:, c : c + chunk + 2 * LANES]
-        tall, across = x.shape
-        for _ in range(7):
-            x = x + pltpu.roll(x, tall - 1, 0)
-        for _ in range(4):
-            x = x + pltpu.roll(x, 1, 1)
-        for _ in range(3):
-            x = x + pltpu.roll(x, across - 1, 1)
-        x = x * (1.0 / 4096)
-        ahead = pltpu.roll(x, across - 1, 1)
-        east = ahead - x
-        both = ahead + x
+        across = x.shape[1]
+
+        def moved(k):
+            return pltpu.roll(x, (-k) % across, 1)[:, LANES : LANES + chunk]
+
+        right = [moved(k) for k in range(1, 5)]
+        left = [moved(-k) for k in range(1, 5)]
+        d1, d2, d3, d4 = (r - l for r, l in zip(right, left))
+        s1, s2, s3, s4 = (r + l for r, l in zip(right, left))
+        east = d4 + 6.0 * d3 + 14.0 * (d2 + d1)
+        both = s4 + 8.0 * s3 + 28.0 * s2 + 56.0 * s1 + 70.0 * x[:, LANES : LANES + chunk]
         gx = east + pltpu.roll(east, tall - 1, 0)
         gy = pltpu.roll(both, tall - 1, 0) - both
-        gx_ref[:, c : c + chunk] = gx[:rows, LANES : LANES + chunk]
-        gy_ref[:, c : c + chunk] = gy[:rows, LANES : LANES + chunk]
+        gx_ref[:, c : c + chunk] = gx[:rows]
+        gy_ref[:, c : c + chunk] = gy[:rows]
 
 
 def gradients(above, middle, below):
@@ -158,41 +164,39 @@
     )(above, middle, below)
 
 
-def shade_kernel(mine, theirs, core_ref, ranks, heights, gx_ref, gy_ref, out_ref, held, scale_ref):
-    step = pl.program_id(0)
-
-    @pl.when(step == 0)
-    def _():
-        first = core_ref[0] == 0
-        a, b = mine[...], theirs[...]
-        lower = jnp.where(first, a, b)
-        upper = jnp.where(first, b, a)
-        span = lower[:, HALF:] + upper[:, HALF:]
-        scale_ref[...] = zfactor / (8.0 * span)
-        parts = [lower[:, i * LANES : (i + 1) * LANES] for i in range(4)]
-        parts += [upper[:, i * LANES : (i + 1) * LANES] for i in range(4)]
-        counts = jnp.concatenate(parts, axis=0)
-        upto = (iota((LANES, LANES), 0) <= iota((LANES, LANES), 1)).astype(jnp.float32)
-        inside = jnp.dot(counts, upto, precision=HIGHEST, preferred_element_type=jnp.float32)
-        totals = jnp.broadcast_to(jnp.sum(counts, axis=1, keepdims=True), counts.shape)
-        rows = iota(counts.shape, 0)
-        ahead = jnp.zeros(counts.shape, jnp.float32)
-        for r in range(7):
-            ahead = ahead + jnp.where(rows > r, totals[r : r + 1], 0.0)
-        cumulative = (inside + ahead).astype(jnp.int32)
-        table = jnp.clip(
-            (cumulative - ranks[0]).astype(jnp.float32)
-            / jnp.full(cumulative.shape, ranks[1] - ranks[0]).astype(jnp.float32),
-            0.0,
-            1.0,
-        )
-        held[...] = table.astype(jnp.bfloat16).astype(jnp.float32)
-
-    rows, width = out_ref.shape
-    tables = [jnp.broadcast_to(held[r : r + 1], (rows, LANES)) for r in range(8)]
-    scale = scale_ref[...]
+def shade_kernel(mine, theirs, core_ref, ranks, heights, gx_ref, gy_ref, out_ref, done, sems):
+    first = core_ref[0] == 0
+    a, b = mine[...], theirs[...]
+    lower = jnp.where(first, a, b)
+    upper = jnp.where(first, b, a)
+    span = lower[:, HALF:] + upper[:, HALF:]
+    scale = zfactor / (8.0 * span)
+    parts = [lower[:, i * LANES : (i + 1) * LANES] for i in range(4)]
+    parts += [upper[:, i * LANES : (i + 1) * LANES] for i in range(4)]
+    counts = jnp.concatenate(parts, axis=0)
+    upto = (iota((LANES, LANES), 0) <= iota((LANES, LANES), 1)).astype(jnp.float32)
+    inside = jnp.dot(counts, upto, precision=HIGHEST, preferred_element_type=jnp.float32)
+    totals = jnp.broadcast_to(jnp.sum(counts, axis=1, keepdims=True), counts.shape)
+    row_ids = iota(counts.shape, 0)
+    ahead = jnp.zeros(counts.shape, jnp.float32)
+    for r in range(7):
+        ahead = ahead + jnp.where(row_ids > r, totals[r : r + 1], 0.0)
+    cumulative = (inside + ahead).astype(jnp.int32)
+    table = jnp.clip(
+        (cumulative - ranks[0]).astype(jnp.float32)
+        / jnp.full(cumulative.shape, ranks[1] - ranks[0]).astype(jnp.float32),
+        0.0,
+        1.0,
+    )
+    table = table.astype(jnp.bfloat16).astype(jnp.float32)
+
+    rows, width = heights.shape
+    tables = [jnp.broadcast_to(table[r : r + 1], (rows, LANES)) for r in range(8)]
+    pieces = sems.shape[0]
+    piece = width // pieces
+    copies = []
     for c in range(width // LANES):
-        cols = pl.ds(pl.multiple_of(step * width + c * LANES, LANES), LANES)
+        cols = slice(c * LANES, (c + 1) * LANES)
         bins = bin_of(heights[:, cols]).astype(jnp.int32)
         low = bins & (LANES - 1)
         high = bins >> 7
@@ -207,19 +211,28 @@
         light = (cos_zenith - sin_zenith * (light_x * gx + light_y * gy)) * lax.rsqrt(
             1.0 + gx * gx + gy * gy
         )
-        out_ref[:, c * LANES : (c + 1) * LANES] = found[0] * (0.5 + jnp.maximum(light, 0.0))
+        done[:, cols] = found[0] * (0.5 + jnp.maximum(light, 0.0))
+        if (c + 1) * LANES % piece == 0:
+            n = len(copies)
+            span_cols = slice(n * piece, (n + 1) * piece)
+            copies.append(
+                pltpu.make_async_copy(done.at[:, span_cols], out_ref.at[:, span_cols], sems.at[n])
+            )
+            copies[-1].start()
+    for copy in copies:
+        copy.wait()
 
 
 def shade(mine, theirs, core, ranks, elevation, gx, gy):
-    rows, width = elevation.shape
-    steps = 4
     return pl.pallas_call(
         shade_kernel,
-        grid=(steps,),
         out_shape=jax.ShapeDtypeStruct(elevation.shape, jnp.float32),
         in_specs=[VMEM_SPEC, VMEM_SPEC, SMEM_SPEC, SMEM_SPEC, VMEM_SPEC, VMEM_SPEC, VMEM_SPEC],
-        out_specs=pl.BlockSpec((rows, width // steps), lambda i: (0, i)),
-        scratch_shapes=[pltpu.VMEM((8, LANES), jnp.float32), pltpu.VMEM((1, LANES), jnp.float32)],
+        out_specs=pl.BlockSpec(memory_space=pl.ANY),
+        scratch_shapes=[
+            pltpu.VMEM(elevation.shape, jnp.float32),
+            pltpu.SemaphoreType.DMA((8,)),
+        ],
         name="shade",
     )(mine, theirs, core, ranks, elevation, gx, gy)
 
@@ -230,7 +243,7 @@
     core = core.astype(jnp.int32).reshape(1)
     partner = [(i, i ^ 1) for i in range(size)]
     chips = size // 2
-    begin = chips * 5 // 8
+    begin = chips * 3 // 4
     order = [(i + begin) % chips for i in range(chips)]
     same_core = [[2 * i + c for i in order] for c in range(2)]
     local = in_vmem(elevation)

time: 69.6 us -> 63.3 us (0.909)
  Pallas kernels: 15.1 us -> 9.66 us
  starting transfers between devices: 45.7 us -> 41.9 us
  waiting for transfers between devices: 7.39 us -> 10.3 us
    pallas_call x1, Pallas kernels: 7.58 us -> 2.34 us  [gradients(): pl.pallas_call(gradient_kernel, out_shape=(shape, shape), in_specs=[VMEM_...]
    all_to_all x1, starting transfers between devices: 18 us -> 13.2 us  [body(): lax.all_to_all(spread, 'row', 0, 0, axis_index_groups=same_core, tiled=True)]
    all_to_all x1, waiting for transfers between devices: 6.56 us -> 9.46 us  [body(): lax.all_to_all(spread, 'row', 0, 0, axis_index_groups=same_core, tiled=True)]
    ppermute x1, starting transfers between devices: 1.28 us -> 2.36 us  [body(): theirs = lax.ppermute(mine, 'row', partner)]
  transfers between devices with their start and end apart: 5 -> 5, of which waited for: 2 -> 2; matrix products, arithmetic and copies ran while one was open for 0% -> 0% of each run, Pallas kernels for 11% -> 4%
where the time goes in v3:
time: 63.3 us; the launch traced here: 63 us
  starting transfers between devices  41.9 us (66%)
  waiting for transfers between devices  10.3 us (16%)
  Pallas kernels  9.66 us (15%)
  local copies, waits for them, and re-layouts  1.09 us (2%)
    ppermute x1, starting transfers between devices, body(): received = lax.ppermute(send, 'row', partner)  20.5 us
    all_to_all x1, starting transfers between devices, body(): lax.all_to_all(spread, 'row', 0, 0, axis_index_groups=same_core, tiled=True)  13.2 us
    all_to_all x1, waiting for transfers between devices, body(): lax.all_to_all(spread, 'row', 0, 0, axis_index_groups=same_core, tiled=True)  9.46 us
    pallas_call x1, Pallas kernels, shade(): pl.pallas_call(shade_kernel, out_shape=jax.ShapeDtypeStruct(elevation.sha...  3.88 us
    ppermute x1, starting transfers between devices, body(): lax.ppermute(elevation[-4:], 'row', [(i, i + 1) for i in range(size - 1)])  3.02 us
    ppermute x1, starting transfers between devices, body(): lax.ppermute(elevation[:4], 'row', [(i + 1, i) for i in range(size - 1)])  2.84 us
    pallas_call x1, Pallas kernels, count(): pl.pallas_call(count_kernel, out_shape=(shape, shape), in_specs=[VMEM_SPE...  2.74 us
    ppermute x1, starting transfers between devices, body(): theirs = lax.ppermute(mine, 'row', partner)  2.36 us
  transfers between devices with their start and end apart: 5, of which 2 were waited for; matrix products, arithmetic and copies ran while one was open for 0% of the time, Pallas kernels for 4%

profile of v3, /device:TPU:37, one launch (start us, length us, event | category | flops | bytes accessed | tf_op | source)
XLA Modules:
  0.0 63.0 jit_solution(16748624997985248876)
XLA Ops:
  0.0 0.0 copy-start
  0.0 1.0 %copy-done = f32[16,8192]{1,0:T(8,128)S(1)} copy-done((f32[16,8192]{1,0:T(8,128)S(1)}, f32[16,8192]{1,0:T(8,128)}, u32[]{:S(2)}) %copy-start) | copy-done | bytes 524312
  1.0 0.0 copy-start.1
  1.0 2.7 %count.1 = (f32[1,640]{1,0:T(1,128)S(1)}, f32[1,640]{1,0:T(1,128)S(1)}) custom-call(f32[16,8192]{1,0:T(8,128)S(1)} %copy-done, s32[1]{0:T(128)} %bitcast.core_ref), custom_call_target="tpu_custom_call" | custom-call | tf_op jit(solution)/shard_map/count/pallas_call | solution.py:75
  3.8 20.5 %collective-permute-start = (f32[1,640]{1,0:T(1,128)S(1)}, f32[1,640]{1,0:T(1,128)S(1)}, u32[]{:S(2)}, u32[]{:S(2)}) collective-permute-start(f32[1,640]{1,0:T(1,128)S(1)} %get-tuple-element.10), channel_id=1, source_target_pairs={{0,1},{1,0},{2,3},{3,2},{4,5},{5,4},{6,7},{7,6},{8,9},{9,8},{10,11... | collective-permute-start | bytes 7688 | tf_op jit(solution)/shard_map/ppermute | solution.py:251
  24.3 0.8 %collective-permute-done.b_ref = f32[1,640]{1,0:T(1,128)S(1)} collective-permute-done((f32[1,640]{1,0:T(1,128)S(1)}, f32[1,640]{1,0:T(1,128)S(1)}, u32[]{:S(2)}, u32[]{:S(2)}) %collective-permute-start) | collective-permute-done | bytes 2592 | tf_op jit(solution)/shard_map/ppermute | solution.py:251
  25.1 0.7 %join.1 = f32[32,1,640]{2,1,0:T(1,128)} custom-call(f32[1,640]{1,0:T(1,128)S(1)} %get-tuple-element.9.a_ref, f32[1,640]{1,0:T(1,128)S(1)} %collective-permute-done.b_ref), custom_call_target="tpu_custom_call" | custom-call | tf_op jit(solution)/shard_map/join/pallas_call | solution.py:92
  25.7 13.2 %all-to-all-start = ((f32[32,1,640]{2,1,0:T(1,128)}), f32[32,1,640]{2,1,0:T(1,128)S(1)}, u32[]{:S(2)}, u32[]{:S(2)}) async-start(f32[32,1,640]{2,1,0:T(1,128)} %join.1), calls=%async_computation | async-start | bytes 163840 | tf_op jit(solution)/shard_map/all_to_all | solution.py:253
  39.0 0.0 copy-done.1
  39.0 2.8 %collective-permute-start.3 = (f32[4,8192]{1,0:T(4,128)S(1)}, f32[4,8192]{1,0:T(4,128)S(1)}, u32[]{:S(2)}, u32[]{:S(2)}) collective-permute-start(f32[4,8192]{1,0:T(4,128)S(1)} %get-tuple-element.13), channel_id=1, source_target_pairs={{1,0},{2,1},{3,2},{4,3},{5,4},{6,5},{7,6},{8,7},{9,8},{10,9},{11,1... | collective-permute-start | bytes 393224 | tf_op jit(solution)/shard_map/ppermute | solution.py:256
  41.9 3.0 %collective-permute-start.2 = (f32[4,8192]{1,0:T(4,128)S(1)}, f32[4,8192]{1,0:T(4,128)S(1)}, u32[]{:S(2)}, u32[]{:S(2)}) collective-permute-start(f32[4,8192]{1,0:T(4,128)S(1)} %get-tuple-element.14), channel_id=1, source_target_pairs={{0,1},{1,2},{2,3},{3,4},{4,5},{5,6},{6,7},{7,8},{8,9},{9,10},{10,1... | collective-permute-start | bytes 393224 | tf_op jit(solution)/shard_map/ppermute | solution.py:255
  44.9 9.5 %all-to-all-done.x_ref = f32[32,1,640]{2,1,0:T(1,128)S(1)} async-done(((f32[32,1,640]{2,1,0:T(1,128)}), f32[32,1,640]{2,1,0:T(1,128)S(1)}, u32[]{:S(2)}, u32[]{:S(2)}) %all-to-all-start) | async-done | bytes 81952 | tf_op jit(solution)/shard_map/all_to_all | solution.py:253
  54.4 0.1 gather.1.mine
  54.4 2.4 %collective-permute-start.1 = (f32[1,640]{1,0:T(1,128)S(1)}, f32[1,640]{1,0:T(1,128)S(1)}, u32[]{:S(2)}, u32[]{:S(2)}) collective-permute-start(f32[1,640]{1,0:T(1,128)S(1)} %gather.1.mine), channel_id=1, source_target_pairs={{0,1},{1,0},{2,3},{3,2},{4,5},{5,4},{6,7},{7,6},{8,9},{9,8},{10,11... | collective-permute-start | bytes 7688 | tf_op jit(solution)/shard_map/ppermute | solution.py:260
  56.8 0.0 collective-permute-done.3.below
  56.8 0.0 collective-permute-done.2.above
  56.8 2.3 %gradients.1 = (f32[16,8192]{1,0:T(8,128)S(1)}, f32[16,8192]{1,0:T(8,128)S(1)}) custom-call(f32[4,8192]{1,0:T(4,128)S(1)} %collective-permute-done.2.above, f32[16,8192]{1,0:T(8,128)S(1)} %copy-done.1, f32[4,8192]{1,0:T(4,128)S(1)} %collective-permute-done.3.below), custom_call_target="tpu_custom_call" | custom-call | tf_op jit(solution)/shard_map/gradients/pallas_call | solution.py:155
  59.1 0.0 collective-permute-done.1.theirs
  59.2 3.9 %shade.1 = f32[16,8192]{1,0:T(8,128)} custom-call(f32[1,640]{1,0:T(1,128)S(1)} %gather.1.mine, f32[1,640]{1,0:T(1,128)S(1)} %collective-permute-done.1.theirs, s32[1]{0:T(128)} %bitcast.core_ref, s32[2]{0:T(128)} %ranks.1, f32[16,8192]{1,0:T(8,128)S(1)} %copy-done.1, f32[16,8192]{1,0:T(8,128)S(1)} %get-tuple-element.11.gx_ref, ...), custom_call_target="tpu_custom_call" | custom-call | tf_op jit(solution)/shard_map/shade/pallas_call | solution.py:227
  (1 shorter events, 0.0 us)
Async XLA Ops:
  0.0 1.0 %copy-start = (f32[16,8192]{1,0:T(8,128)S(1)}, f32[16,8192]{1,0:T(8,128)}, u32[]{:S(2)}) copy-start(f32[16,8192]{1,0:T(8,128)} %heights.3) | copy-start | bytes 1572868
  1.0 37.9 %copy-start.1 = (f32[16,8192]{1,0:T(8,128)S(1)}, f32[16,8192]{1,0:T(8,128)}, u32[]{:S(2)}) copy-start(f32[16,8192]{1,0:T(8,128)} %heights.3) | copy-start | bytes 1572868
  3.8 21.3 %collective-permute-start = (f32[1,640]{1,0:T(1,128)S(1)}, f32[1,640]{1,0:T(1,128)S(1)}, u32[]{:S(2)}, u32[]{:S(2)}) collective-permute-start(f32[1,640]{1,0:T(1,128)S(1)} %get-tuple-element.10), channel_id=1, source_target_pairs={{0,1},{1,0},{2,3},{3,2},{4,5},{5,4},{6,7},{7,6},{8,9},{9,8},{10,11... | collective-permute-start | bytes 7688 | tf_op jit(solution)/shard_map/ppermute | solution.py:251
  25.7 28.6 %all-to-all-start = ((f32[32,1,640]{2,1,0:T(1,128)}), f32[32,1,640]{2,1,0:T(1,128)S(1)}, u32[]{:S(2)}, u32[]{:S(2)}) async-start(f32[32,1,640]{2,1,0:T(1,128)} %join.1), calls=%async_computation | async-start | bytes 163840 | tf_op jit(solution)/shard_map/all_to_all | solution.py:253
  39.0 17.8 %collective-permute-start.3 = (f32[4,8192]{1,0:T(4,128)S(1)}, f32[4,8192]{1,0:T(4,128)S(1)}, u32[]{:S(2)}, u32[]{:S(2)}) collective-permute-start(f32[4,8192]{1,0:T(4,128)S(1)} %get-tuple-element.13), channel_id=1, source_target_pairs={{1,0},{2,1},{3,2},{4,3},{5,4},{6,5},{7,6},{8,7},{9,8},{10,9},{11,1... | collective-permute-start | bytes 393224 | tf_op jit(solution)/shard_map/ppermute | solution.py:256
  41.9 14.9 %collective-permute-start.2 = (f32[4,8192]{1,0:T(4,128)S(1)}, f32[4,8192]{1,0:T(4,128)S(1)}, u32[]{:S(2)}, u32[]{:S(2)}) collective-permute-start(f32[4,8192]{1,0:T(4,128)S(1)} %get-tuple-element.14), channel_id=1, source_target_pairs={{0,1},{1,2},{2,3},{3,4},{4,5},{5,6},{6,7},{7,8},{8,9},{9,10},{10,1... | collective-permute-start | bytes 393224 | tf_op jit(solution)/shard_map/ppermute | solution.py:255
  54.4 4.7 %collective-permute-start.1 = (f32[1,640]{1,0:T(1,128)S(1)}, f32[1,640]{1,0:T(1,128)S(1)}, u32[]{:S(2)}, u32[]{:S(2)}) collective-permute-start(f32[1,640]{1,0:T(1,128)S(1)} %gather.1.mine), channel_id=1, source_target_pairs={{0,1},{1,0},{2,3},{3,2},{4,5},{5,4},{6,7},{7,6},{8,9},{9,8},{10,11... | collective-permute-start | bytes 7688 | tf_op jit(solution)/shard_map/ppermute | solution.py:260

commit v4 on v3

--- a/solution.py
+++ b/solution.py
@@ -14,9 +14,10 @@
 zfactor = 200.0
 cos_zenith = 0.70710678
 sin_zenith = 0.70710678
-light_x = -0.70710678
 light_y = 0.70710678
 HIGHEST = lax.Precision.HIGHEST
+HOT = jnp.float8_e4m3fn
+STEPS = 65535.0
 
 
 def bin_of(height):
@@ -38,15 +39,21 @@
     up = jnp.floor(bins * (1.0 / LOW))
     upper[...] = up
     lower[...] = bins - up * LOW
-    row_ids = iota((LOW, width), 0).astype(jnp.float32)
-    one = jnp.float32(1.0)
-    zero = jnp.float32(0.0)
+    row_ids = iota((LOW, width), 0).astype(jnp.float32).astype(jnp.bfloat16)
+    one = jnp.array(1, HOT)
+    zero = jnp.array(0, HOT)
+
+    def hot(digits, r):
+        again = digits[pl.ds(r, LOW // 2, stride=0), :].astype(jnp.bfloat16)
+        return jnp.where(jnp.concatenate([again, again], axis=0) == row_ids, one, zero)
+
     grid = jnp.zeros((high_count, LOW), jnp.float32)
     for r in range(rows):
-        up_hot = jnp.where(upper[r : r + 1, :] == row_ids, one, zero).astype(jnp.bfloat16)
-        low_hot = jnp.where(lower[r : r + 1, :] == row_ids, one, zero).astype(jnp.bfloat16)
         grid = grid + lax.dot_general(
-            up_hot, low_hot, (((1,), (1,)), ((), ())), preferred_element_type=jnp.float32
+            hot(upper, r),
+            hot(lower, r),
+            (((1,), (1,)), ((), ())),
+            preferred_element_type=jnp.float32,
         )
     spread = (iota((LOW, LANES), 1) % LOW == iota((LOW, LANES), 0)).astype(jnp.float32)
     tiled = jnp.dot(grid, spread, precision=HIGHEST, preferred_element_type=jnp.float32)
@@ -114,7 +121,7 @@
     )(everyone)
 
 
-def gradient_kernel(above, middle, below, gx_ref, gy_ref, wide):
+def gradient_kernel(above, middle, below, gx_ref, gy_ref, bin_ref, wide):
     rows, width = middle.shape
     halo = above.shape[0]
     edge = jnp.zeros((rows + 2 * halo, LANES), jnp.float32)
@@ -145,6 +152,7 @@
         both = s4 + 8.0 * s3 + 28.0 * s2 + 56.0 * s1 + 70.0 * x[:, LANES : LANES + chunk]
         gx = east + pltpu.roll(east, tall - 1, 0)
         gy = pltpu.roll(both, tall - 1, 0) - both
+        bin_ref[:, c : c + chunk] = bin_of(middle[:, c : c + chunk]).astype(jnp.int32)
         gx_ref[:, c : c + chunk] = gx[:rows]
         gy_ref[:, c : c + chunk] = gy[:rows]
 
@@ -154,9 +162,9 @@
     shape = pltpu.VMEM(middle.shape, jnp.float32)
     return pl.pallas_call(
         gradient_kernel,
-        out_shape=(shape, shape),
+        out_shape=(shape, shape, pltpu.VMEM(middle.shape, jnp.int32)),
         in_specs=[VMEM_SPEC] * 3,
-        out_specs=(VMEM_SPEC,) * 2,
+        out_specs=(VMEM_SPEC,) * 3,
         scratch_shapes=[
             pltpu.VMEM((rows + 2 * above.shape[0], width + 2 * LANES), jnp.float32)
         ],
@@ -164,7 +172,22 @@
     )(above, middle, below)
 
 
-def shade_kernel(mine, theirs, core_ref, ranks, heights, gx_ref, gy_ref, out_ref, done, sems):
+def prefix_sums(counts):
+    whole = counts.astype(jnp.int32)
+    parts = [(whole >> shift) & 255 for shift in (0, 8, 16)]
+    parts = jnp.concatenate(parts, axis=0).astype(jnp.float32).astype(jnp.bfloat16)
+    upto = jnp.where(iota((LANES, LANES), 0) <= iota((LANES, LANES), 1), 1.0, 0.0)
+    sums = jnp.dot(parts, upto.astype(jnp.bfloat16), preferred_element_type=jnp.float32)
+    n = counts.shape[0]
+    inside = sums[:n] + 256.0 * sums[n : 2 * n] + 65536.0 * sums[2 * n :]
+    totals = jnp.broadcast_to(jnp.sum(counts, axis=1, keepdims=True), counts.shape)
+    row_ids = iota(counts.shape, 0)
+    for r in range(n - 1):
+        inside = inside + jnp.where(row_ids > r, totals[r : r + 1], 0.0)
+    return inside
+
+
+def shade_kernel(mine, theirs, core_ref, ranks, bins, gx_ref, gy_ref, out_ref, done, sems):
     first = core_ref[0] == 0
     a, b = mine[...], theirs[...]
     lower = jnp.where(first, a, b)
@@ -173,45 +196,35 @@
     scale = zfactor / (8.0 * span)
     parts = [lower[:, i * LANES : (i + 1) * LANES] for i in range(4)]
     parts += [upper[:, i * LANES : (i + 1) * LANES] for i in range(4)]
-    counts = jnp.concatenate(parts, axis=0)
-    upto = (iota((LANES, LANES), 0) <= iota((LANES, LANES), 1)).astype(jnp.float32)
-    inside = jnp.dot(counts, upto, precision=HIGHEST, preferred_element_type=jnp.float32)
-    totals = jnp.broadcast_to(jnp.sum(counts, axis=1, keepdims=True), counts.shape)
-    row_ids = iota(counts.shape, 0)
-    ahead = jnp.zeros(counts.shape, jnp.float32)
-    for r in range(7):
-        ahead = ahead + jnp.where(row_ids > r, totals[r : r + 1], 0.0)
-    cumulative = (inside + ahead).astype(jnp.int32)
+    cumulative = prefix_sums(jnp.concatenate(parts, axis=0)).astype(jnp.int32)
     table = jnp.clip(
         (cumulative - ranks[0]).astype(jnp.float32)
         / jnp.full(cumulative.shape, ranks[1] - ranks[0]).astype(jnp.float32),
         0.0,
         1.0,
     )
-    table = table.astype(jnp.bfloat16).astype(jnp.float32)
-
-    rows, width = heights.shape
-    tables = [jnp.broadcast_to(table[r : r + 1], (rows, LANES)) for r in range(8)]
+    steps = jnp.floor(table * STEPS + 0.5).astype(jnp.int32)
+    words = steps[:4] | (steps[4:] << 16)
+
+    rows, width = bins.shape
+    tables = [jnp.broadcast_to(words[r : r + 1], (rows, LANES)) for r in range(4)]
     pieces = sems.shape[0]
     piece = width // pieces
     copies = []
     for c in range(width // LANES):
         cols = slice(c * LANES, (c + 1) * LANES)
-        bins = bin_of(heights[:, cols]).astype(jnp.int32)
-        low = bins & (LANES - 1)
-        high = bins >> 7
-        found = [
-            jnp.take_along_axis(t, low, axis=1, mode="promise_in_bounds") for t in tables
-        ]
-        for bit in range(3):
-            odd = (high & (1 << bit)) != 0
-            found = [jnp.where(odd, found[2 * i + 1], found[2 * i]) for i in range(len(found) // 2)]
+        code = bins[:, cols]
+        low = code & (LANES - 1)
+        w = [jnp.take_along_axis(t, low, axis=1, mode="promise_in_bounds") for t in tables]
+        odd = (code & 128) != 0
+        word = jnp.where((code & 256) != 0, jnp.where(odd, w[3], w[2]), jnp.where(odd, w[1], w[0]))
+        stretch = ((word >> ((code >> 5) & 16)) & 65535).astype(jnp.float32)
         gx = gx_ref[:, cols] * scale
         gy = gy_ref[:, cols] * scale
-        light = (cos_zenith - sin_zenith * (light_x * gx + light_y * gy)) * lax.rsqrt(
+        light = (cos_zenith - (sin_zenith * light_y) * (gy - gx)) * lax.rsqrt(
             1.0 + gx * gx + gy * gy
         )
-        done[:, cols] = found[0] * (0.5 + jnp.maximum(light, 0.0))
+        done[:, cols] = stretch * (0.5 / STEPS + jnp.maximum(light, 0.0) * (1.0 / STEPS))
         if (c + 1) * LANES % piece == 0:
             n = len(copies)
             span_cols = slice(n * piece, (n + 1) * piece)
@@ -223,18 +236,18 @@
         copy.wait()
 
 
-def shade(mine, theirs, core, ranks, elevation, gx, gy):
+def shade(mine, theirs, core, ranks, bins, gx, gy):
     return pl.pallas_call(
         shade_kernel,
-        out_shape=jax.ShapeDtypeStruct(elevation.shape, jnp.float32),
+        out_shape=jax.ShapeDtypeStruct(gx.shape, jnp.float32),
         in_specs=[VMEM_SPEC, VMEM_SPEC, SMEM_SPEC, SMEM_SPEC, VMEM_SPEC, VMEM_SPEC, VMEM_SPEC],
         out_specs=pl.BlockSpec(memory_space=pl.ANY),
         scratch_shapes=[
-            pltpu.VMEM(elevation.shape, jnp.float32),
+            pltpu.VMEM(gx.shape, jnp.float32),
             pltpu.SemaphoreType.DMA((8,)),
         ],
         name="shade",
-    )(mine, theirs, core, ranks, elevation, gx, gy)
+    )(mine, theirs, core, ranks, bins, gx, gy)
 
 
 def body(elevation, ranks):
@@ -243,7 +256,7 @@
     core = core.astype(jnp.int32).reshape(1)
     partner = [(i, i ^ 1) for i in range(size)]
     chips = size // 2
-    begin = chips * 3 // 4
+    begin = chips * 11 // 16
     order = [(i + begin) % chips for i in range(chips)]
     same_core = [[2 * i + c for i in order] for c in range(2)]
     local = in_vmem(elevation)
@@ -254,12 +267,12 @@
 
     above = lax.ppermute(elevation[-4:], "row", [(i, i + 1) for i in range(size - 1)])
     below = lax.ppermute(elevation[:4], "row", [(i + 1, i) for i in range(size - 1)])
-    gx, gy = gradients(in_vmem(above), local, in_vmem(below))
+    gx, gy, bins = gradients(in_vmem(above), local, in_vmem(below))
 
     mine = gather(in_vmem(everyone))
     theirs = lax.ppermute(mine, "row", partner)
     return shade(
-        in_vmem(mine), in_vmem(theirs), core, ranks, local, in_vmem(gx), in_vmem(gy)
+        in_vmem(mine), in_vmem(theirs), core, ranks, in_vmem(bins), in_vmem(gx), in_vmem(gy)
     )
 
 

time: 63.3 us -> 64.4 us (1.017)
  starting transfers between devices: 41.9 us -> 44.7 us
  waiting for transfers between devices: 10.3 us -> 8.17 us
  local copies, waits for them, and re-layouts: 1.09 us -> 2.92 us
  Pallas kernels: 9.66 us -> 8.27 us
    all_to_all x1, starting transfers between devices: 13.2 us -> 16.2 us  [body(): lax.all_to_all(spread, 'row', 0, 0, axis_index_groups=same_core, tiled=True)]
    all_to_all x1, waiting for transfers between devices: 9.46 us -> 7.34 us  [body(): lax.all_to_all(spread, 'row', 0, 0, axis_index_groups=same_core, tiled=True)]
    unnamed x4 -> x8, local copies, waits for them, and re-layouts: 1.04 us -> 2.87 us
    pallas_call x2, Pallas kernels: 6.22 us -> 5.2 us  [the longest x1 2.79 us: shade(): pl.pallas_call(shade_kernel, out_shape=jax.ShapeDtypeStruct(gx.shape, jnp...]
where the time goes in v4:
time: 64.4 us; the launch traced here: 64.1 us
  starting transfers between devices  44.7 us (69%)
  Pallas kernels  8.27 us (13%)
  waiting for transfers between devices  8.17 us (13%)
  local copies, waits for them, and re-layouts  2.92 us (5%)
    ppermute x1, starting transfers between devices, body(): received = lax.ppermute(send, 'row', partner)  20.5 us
    all_to_all x1, starting transfers between devices, body(): lax.all_to_all(spread, 'row', 0, 0, axis_index_groups=same_core, tiled=True)  16.2 us
    all_to_all x1, waiting for transfers between devices, body(): lax.all_to_all(spread, 'row', 0, 0, axis_index_groups=same_core, tiled=True)  7.34 us
    ppermute x1, starting transfers between devices, body(): lax.ppermute(elevation[-4:], 'row', [(i, i + 1) for i in range(size - 1)])  3.02 us
    unnamed x8, local copies, waits for them, and re-layouts  2.87 us
    ppermute x1, starting transfers between devices, body(): lax.ppermute(elevation[:4], 'row', [(i + 1, i) for i in range(size - 1)])  2.84 us
    pallas_call x1, Pallas kernels, shade(): pl.pallas_call(shade_kernel, out_shape=jax.ShapeDtypeStruct(gx.shape, jnp...  2.79 us
    pallas_call x1, Pallas kernels, gradients(): pl.pallas_call(gradient_kernel, out_shape=(shape, shape, pltpu.VMEM(middl...  2.41 us
  transfers between devices with their start and end apart: 5, of which 2 were waited for; matrix products, arithmetic and copies ran while one was open for 0% of the time, Pallas kernels for 4%

profile of v4, /device:TPU:37, one launch (start us, length us, event | category | flops | bytes accessed | tf_op | source)
XLA Modules:
  0.0 64.1 jit_solution(2943126463778705509)
XLA Ops:
  0.0 0.0 copy-start
  0.0 1.0 %copy-done = f32[16,8192]{1,0:T(8,128)S(1)} copy-done((f32[16,8192]{1,0:T(8,128)S(1)}, f32[16,8192]{1,0:T(8,128)}, u32[]{:S(2)}) %copy-start) | copy-done | bytes 524312
  1.0 0.0 copy-start.1
  1.0 2.4 %count.1 = (f32[1,640]{1,0:T(1,128)S(1)}, f32[1,640]{1,0:T(1,128)S(1)}) custom-call(f32[16,8192]{1,0:T(8,128)S(1)} %copy-done, s32[1]{0:T(128)} %bitcast.core_ref), custom_call_target="tpu_custom_call" | custom-call | tf_op jit(solution)/shard_map/count/pallas_call | solution.py:82
  3.4 20.5 %collective-permute-start = (f32[1,640]{1,0:T(1,128)S(1)}, f32[1,640]{1,0:T(1,128)S(1)}, u32[]{:S(2)}, u32[]{:S(2)}) collective-permute-start(f32[1,640]{1,0:T(1,128)S(1)} %get-tuple-element.11), channel_id=1, source_target_pairs={{0,1},{1,0},{2,3},{3,2},{4,5},{5,4},{6,7},{7,6},{8,9},{9,8},{10,11... | collective-permute-start | bytes 7688 | tf_op jit(solution)/shard_map/ppermute | solution.py:264
  23.9 0.8 %collective-permute-done.b_ref = f32[1,640]{1,0:T(1,128)S(1)} collective-permute-done((f32[1,640]{1,0:T(1,128)S(1)}, f32[1,640]{1,0:T(1,128)S(1)}, u32[]{:S(2)}, u32[]{:S(2)}) %collective-permute-start) | collective-permute-done | bytes 2592 | tf_op jit(solution)/shard_map/ppermute | solution.py:264
  24.7 0.7 %join.1 = f32[32,1,640]{2,1,0:T(1,128)} custom-call(f32[1,640]{1,0:T(1,128)S(1)} %get-tuple-element.10.a_ref, f32[1,640]{1,0:T(1,128)S(1)} %collective-permute-done.b_ref), custom_call_target="tpu_custom_call" | custom-call | tf_op jit(solution)/shard_map/join/pallas_call | solution.py:99
  25.4 16.2 %all-to-all-start = ((f32[32,1,640]{2,1,0:T(1,128)}), f32[32,1,640]{2,1,0:T(1,128)S(1)}, u32[]{:S(2)}, u32[]{:S(2)}) async-start(f32[32,1,640]{2,1,0:T(1,128)} %join.1), calls=%async_computation | async-start | bytes 163840 | tf_op jit(solution)/shard_map/all_to_all | solution.py:266
  41.6 0.0 copy-done.1
  41.7 2.8 %collective-permute-start.3 = (f32[4,8192]{1,0:T(4,128)S(1)}, f32[4,8192]{1,0:T(4,128)S(1)}, u32[]{:S(2)}, u32[]{:S(2)}) collective-permute-start(f32[4,8192]{1,0:T(4,128)S(1)} %get-tuple-element.15), channel_id=1, source_target_pairs={{1,0},{2,1},{3,2},{4,3},{5,4},{6,5},{7,6},{8,7},{9,8},{10,9},{11,1... | collective-permute-start | bytes 393224 | tf_op jit(solution)/shard_map/ppermute | solution.py:269
  44.5 3.0 %collective-permute-start.2 = (f32[4,8192]{1,0:T(4,128)S(1)}, f32[4,8192]{1,0:T(4,128)S(1)}, u32[]{:S(2)}, u32[]{:S(2)}) collective-permute-start(f32[4,8192]{1,0:T(4,128)S(1)} %get-tuple-element.16), channel_id=1, source_target_pairs={{0,1},{1,2},{2,3},{3,4},{4,5},{5,6},{6,7},{7,8},{8,9},{9,10},{10,1... | collective-permute-start | bytes 393224 | tf_op jit(solution)/shard_map/ppermute | solution.py:268
  47.5 7.3 %all-to-all-done.x_ref = f32[32,1,640]{2,1,0:T(1,128)S(1)} async-done(((f32[32,1,640]{2,1,0:T(1,128)}), f32[32,1,640]{2,1,0:T(1,128)S(1)}, u32[]{:S(2)}, u32[]{:S(2)}) %all-to-all-start) | async-done | bytes 81952 | tf_op jit(solution)/shard_map/all_to_all | solution.py:266
  54.9 0.1 gather.1.mine
  54.9 2.1 %collective-permute-start.1 = (f32[1,640]{1,0:T(1,128)S(1)}, f32[1,640]{1,0:T(1,128)S(1)}, u32[]{:S(2)}, u32[]{:S(2)}) collective-permute-start(f32[1,640]{1,0:T(1,128)S(1)} %gather.1.mine), channel_id=1, source_target_pairs={{0,1},{1,0},{2,3},{3,2},{4,5},{5,4},{6,7},{7,6},{8,9},{9,8},{10,11... | collective-permute-start | bytes 7688 | tf_op jit(solution)/shard_map/ppermute | solution.py:273
  57.0 0.0 collective-permute-done.3.below
  57.0 0.0 collective-permute-done.2.above
  57.0 2.4 %gradients.1 = (f32[16,8192]{1,0:T(8,128)S(1)}, f32[16,8192]{1,0:T(8,128)S(1)}, s32[16,8192]{1,0:T(8,128)S(1)}) custom-call(f32[4,8192]{1,0:T(4,128)S(1)} %collective-permute-done.2.above, f32[16,8192]{1,0:T(8,128)S(1)} %copy-done.1, f32[4,8192]{1,0:T(4,128)S(1)} %collective-permute-done.3.below), custom_call_target="tpu_custom_call" | custom-call | tf_op jit(solution)/shard_map/gradients/pallas_call | solution.py:163
  59.5 0.0 copy-start.2
  59.5 0.8 %copy-done.2 = f32[16,8192]{1,0:T(8,128)} copy-done((f32[16,8192]{1,0:T(8,128)}, f32[16,8192]{1,0:T(8,128)S(1)}, u32[]{:S(2)}) %copy-start.2) | copy-done | bytes 524312
  60.3 0.0 collective-permute-done.1.theirs
  60.3 0.0 copy-start.3
  60.3 1.0 %copy-done.3 = f32[16,8192]{1,0:T(8,128)S(1)} copy-done((f32[16,8192]{1,0:T(8,128)S(1)}, f32[16,8192]{1,0:T(8,128)}, u32[]{:S(2)}) %copy-start.3) | copy-done | bytes 524312
  61.3 2.8 %shade.1 = f32[16,8192]{1,0:T(8,128)} custom-call(f32[1,640]{1,0:T(1,128)S(1)} %gather.1.mine, f32[1,640]{1,0:T(1,128)S(1)} %collective-permute-done.1.theirs, s32[1]{0:T(128)} %bitcast.core_ref, s32[2]{0:T(128)} %ranks.1, s32[16,8192]{1,0:T(8,128)S(1)} %get-tuple-element.12.bins, f32[16,8192]{1,0:T(8,128)S(1)} %get-tuple-element.13.gx_ref, ...), custom_call_target="tpu_custom_call" | custom-call | tf_op jit(solution)/shard_map/shade/pallas_call | solution.py:240
  (1 shorter events, 0.0 us)
Async XLA Ops:
  0.0 1.0 %copy-start = (f32[16,8192]{1,0:T(8,128)S(1)}, f32[16,8192]{1,0:T(8,128)}, u32[]{:S(2)}) copy-start(f32[16,8192]{1,0:T(8,128)} %middle.1) | copy-start | bytes 1572868
  1.0 40.6 %copy-start.1 = (f32[16,8192]{1,0:T(8,128)S(1)}, f32[16,8192]{1,0:T(8,128)}, u32[]{:S(2)}) copy-start(f32[16,8192]{1,0:T(8,128)} %middle.1) | copy-start | bytes 1572868
  3.4 21.3 %collective-permute-start = (f32[1,640]{1,0:T(1,128)S(1)}, f32[1,640]{1,0:T(1,128)S(1)}, u32[]{:S(2)}, u32[]{:S(2)}) collective-permute-start(f32[1,640]{1,0:T(1,128)S(1)} %get-tuple-element.11), channel_id=1, source_target_pairs={{0,1},{1,0},{2,3},{3,2},{4,5},{5,4},{6,7},{7,6},{8,9},{9,8},{10,11... | collective-permute-start | bytes 7688 | tf_op jit(solution)/shard_map/ppermute | solution.py:264
  25.4 29.5 %all-to-all-start = ((f32[32,1,640]{2,1,0:T(1,128)}), f32[32,1,640]{2,1,0:T(1,128)S(1)}, u32[]{:S(2)}, u32[]{:S(2)}) async-start(f32[32,1,640]{2,1,0:T(1,128)} %join.1), calls=%async_computation | async-start | bytes 163840 | tf_op jit(solution)/shard_map/all_to_all | solution.py:266
  41.7 15.4 %collective-permute-start.3 = (f32[4,8192]{1,0:T(4,128)S(1)}, f32[4,8192]{1,0:T(4,128)S(1)}, u32[]{:S(2)}, u32[]{:S(2)}) collective-permute-start(f32[4,8192]{1,0:T(4,128)S(1)} %get-tuple-element.15), channel_id=1, source_target_pairs={{1,0},{2,1},{3,2},{4,3},{5,4},{6,5},{7,6},{8,7},{9,8},{10,9},{11,1... | collective-permute-start | bytes 393224 | tf_op jit(solution)/shard_map/ppermute | solution.py:269
  44.5 12.5 %collective-permute-start.2 = (f32[4,8192]{1,0:T(4,128)S(1)}, f32[4,8192]{1,0:T(4,128)S(1)}, u32[]{:S(2)}, u32[]{:S(2)}) collective-permute-start(f32[4,8192]{1,0:T(4,128)S(1)} %get-tuple-element.16), channel_id=1, source_target_pairs={{0,1},{1,2},{2,3},{3,4},{4,5},{5,6},{6,7},{7,8},{8,9},{9,10},{10,1... | collective-permute-start | bytes 393224 | tf_op jit(solution)/shard_map/ppermute | solution.py:268
  54.9 5.3 %collective-permute-start.1 = (f32[1,640]{1,0:T(1,128)S(1)}, f32[1,640]{1,0:T(1,128)S(1)}, u32[]{:S(2)}, u32[]{:S(2)}) collective-permute-start(f32[1,640]{1,0:T(1,128)S(1)} %gather.1.mine), channel_id=1, source_target_pairs={{0,1},{1,0},{2,3},{3,2},{4,5},{5,4},{6,7},{7,6},{8,9},{9,8},{10,11... | collective-permute-start | bytes 7688 | tf_op jit(solution)/shard_map/ppermute | solution.py:273
  59.5 0.8 %copy-start.2 = (f32[16,8192]{1,0:T(8,128)}, f32[16,8192]{1,0:T(8,128)S(1)}, u32[]{:S(2)}) copy-start(f32[16,8192]{1,0:T(8,128)S(1)} %get-tuple-element.14.gy_ref) | copy-start | bytes 1572868
  60.3 1.0 %copy-start.3 = (f32[16,8192]{1,0:T(8,128)S(1)}, f32[16,8192]{1,0:T(8,128)}, u32[]{:S(2)}) copy-start(f32[16,8192]{1,0:T(8,128)} %copy-done.2) | copy-start | bytes 1572868

commit v5 on v4

--- a/solution.py
+++ b/solution.py
@@ -74,6 +74,7 @@
 
 
 VMEM_SPEC = pl.BlockSpec(memory_space=pltpu.VMEM)
+SMALL = pltpu.CompilerParams(vmem_limit_bytes=16 * 2**20)
 SMEM_SPEC = pl.BlockSpec(memory_space=pltpu.SMEM)
 
 
@@ -86,23 +87,27 @@
         out_specs=(VMEM_SPEC,) * 2,
         scratch_shapes=[pltpu.VMEM(elevation.shape, jnp.float32)] * 2,
         name="count",
+        compiler_params=SMALL,
     )(elevation, core)
 
 
-def join_kernel(a_ref, b_ref, out_ref):
-    a, b = a_ref[...], b_ref[...]
-    both = jnp.where(iota(a.shape, 1) < HALF, a + b, jnp.maximum(a, b))
-    out_ref[...] = jnp.broadcast_to(both[None], out_ref.shape)
-
-
-def join(a, b, copies):
+def join_kernel(a_ref, b_ref, c_ref, d_ref, out_ref):
+    a, b, c, d = a_ref[...], b_ref[...], c_ref[...], d_ref[...]
+    added = (a + b) + (c + d)
+    largest = jnp.maximum(jnp.maximum(a, b), jnp.maximum(c, d))
+    joined = jnp.where(iota(a.shape, 1) < HALF, added, largest)
+    out_ref[...] = jnp.broadcast_to(joined[None], out_ref.shape)
+
+
+def join(a, b, c, d, copies):
     return pl.pallas_call(
         join_kernel,
         out_shape=pltpu.VMEM((copies, *a.shape), jnp.float32),
-        in_specs=[VMEM_SPEC] * 2,
+        in_specs=[VMEM_SPEC] * 4,
         out_specs=VMEM_SPEC,
         name="join",
-    )(a, b)
+        compiler_params=SMALL,
+    )(a, b, c, d)
 
 
 def gather_kernel(x_ref, out_ref):
@@ -118,10 +123,13 @@
         in_specs=[VMEM_SPEC],
         out_specs=VMEM_SPEC,
         name="gather",
+        compiler_params=SMALL,
     )(everyone)
 
 
-def gradient_kernel(above, middle, below, gx_ref, gy_ref, bin_ref, wide):
+def gradient_kernel(above, middle, below, ranks, gx_ref, gy_ref, bin_ref, rank_ref, wide):
+    rank_ref[:1] = jnp.full((1, LANES), ranks[0])
+    rank_ref[1:] = jnp.full((1, LANES), ranks[1] - ranks[0])
     rows, width = middle.shape
     halo = above.shape[0]
     edge = jnp.zeros((rows + 2 * halo, LANES), jnp.float32)
@@ -157,19 +165,25 @@
         gy_ref[:, c : c + chunk] = gy[:rows]
 
 
-def gradients(above, middle, below):
+def gradients(above, middle, below, ranks):
     rows, width = middle.shape
     shape = pltpu.VMEM(middle.shape, jnp.float32)
     return pl.pallas_call(
         gradient_kernel,
-        out_shape=(shape, shape, pltpu.VMEM(middle.shape, jnp.int32)),
-        in_specs=[VMEM_SPEC] * 3,
-        out_specs=(VMEM_SPEC,) * 3,
+        out_shape=(
+            shape,
+            shape,
+            pltpu.VMEM(middle.shape, jnp.int32),
+            pltpu.VMEM((2, LANES), jnp.int32),
+        ),
+        in_specs=[VMEM_SPEC] * 3 + [SMEM_SPEC],
+        out_specs=(VMEM_SPEC,) * 4,
         scratch_shapes=[
             pltpu.VMEM((rows + 2 * above.shape[0], width + 2 * LANES), jnp.float32)
         ],
         name="gradients",
-    )(above, middle, below)
+        compiler_params=SMALL,
+    )(above, middle, below, ranks)
 
 
 def prefix_sums(counts):
@@ -187,7 +201,7 @@
     return inside
 
 
-def shade_kernel(mine, theirs, core_ref, ranks, bins, gx_ref, gy_ref, out_ref, done, sems):
+def shade_kernel(mine, theirs, core_ref, limits, bins, gx_ref, gy_ref, out_ref, done, sems):
     first = core_ref[0] == 0
     a, b = mine[...], theirs[...]
     lower = jnp.where(first, a, b)
@@ -198,8 +212,7 @@
     parts += [upper[:, i * LANES : (i + 1) * LANES] for i in range(4)]
     cumulative = prefix_sums(jnp.concatenate(parts, axis=0)).astype(jnp.int32)
     table = jnp.clip(
-        (cumulative - ranks[0]).astype(jnp.float32)
-        / jnp.full(cumulative.shape, ranks[1] - ranks[0]).astype(jnp.float32),
+        (cumulative - limits[:1]).astype(jnp.float32) / limits[1:].astype(jnp.float32),
         0.0,
         1.0,
     )
@@ -236,18 +249,19 @@
         copy.wait()
 
 
-def shade(mine, theirs, core, ranks, bins, gx, gy):
+def shade(mine, theirs, core, limits, bins, gx, gy):
     return pl.pallas_call(
         shade_kernel,
         out_shape=jax.ShapeDtypeStruct(gx.shape, jnp.float32),
-        in_specs=[VMEM_SPEC, VMEM_SPEC, SMEM_SPEC, SMEM_SPEC, VMEM_SPEC, VMEM_SPEC, VMEM_SPEC],
+        in_specs=[VMEM_SPEC, VMEM_SPEC, SMEM_SPEC, VMEM_SPEC, VMEM_SPEC, VMEM_SPEC, VMEM_SPEC],
         out_specs=pl.BlockSpec(memory_space=pl.ANY),
         scratch_shapes=[
             pltpu.VMEM(gx.shape, jnp.float32),
-            pltpu.SemaphoreType.DMA((8,)),
+            pltpu.SemaphoreType.DMA((16,)),
         ],
         name="shade",
-    )(mine, theirs, core, ranks, bins, gx, gy)
+        compiler_params=SMALL,
+    )(mine, theirs, core, limits, bins, gx, gy)
 
 
 def body(elevation, ranks):
@@ -255,24 +269,30 @@
     core = lax.axis_index("row") & 1
     core = core.astype(jnp.int32).reshape(1)
     partner = [(i, i ^ 1) for i in range(size)]
-    chips = size // 2
-    begin = chips * 11 // 16
-    order = [(i + begin) % chips for i in range(chips)]
-    same_core = [[2 * i + c for i in order] for c in range(2)]
+    blocks = size // 4
+    begin = blocks * 3 // 4
+    order = [(i + begin) % blocks for i in range(blocks)]
+    alike = [[4 * i + place for i in order] for place in range(4)]
     local = in_vmem(elevation)
     keep, send = count(local, core)
     received = lax.ppermute(send, "row", partner)
-    spread = join(in_vmem(keep), in_vmem(received), chips)
-    everyone = lax.all_to_all(spread, "row", 0, 0, axis_index_groups=same_core, tiled=True)
+    beside = lax.ppermute(keep, "row", [(i, i ^ 2) for i in range(size)])
+    across = lax.ppermute(send, "row", [(i, i ^ 3) for i in range(size)])
+    spread = join(
+        in_vmem(keep), in_vmem(received), in_vmem(beside), in_vmem(across), blocks
+    )
+    everyone = lax.all_to_all(spread, "row", 0, 0, axis_index_groups=alike, tiled=True)
 
     above = lax.ppermute(elevation[-4:], "row", [(i, i + 1) for i in range(size - 1)])
     below = lax.ppermute(elevation[:4], "row", [(i + 1, i) for i in range(size - 1)])
-    gx, gy, bins = gradients(in_vmem(above), local, in_vmem(below))
+    gx, gy, bins, limits = gradients(
+        in_vmem(above), local, in_vmem(below), ranks
+    )
 
     mine = gather(in_vmem(everyone))
     theirs = lax.ppermute(mine, "row", partner)
     return shade(
-        in_vmem(mine), in_vmem(theirs), core, ranks, in_vmem(bins), in_vmem(gx), in_vmem(gy)
+        in_vmem(mine), in_vmem(theirs), core, in_vmem(limits), in_vmem(bins), in_vmem(gx), in_vmem(gy)
     )
 
 

time: 64.4 us -> 61.1 us (0.949)
  local copies, waits for them, and re-layouts: 2.92 us -> 1.1 us
  starting transfers between devices: 44.7 us -> 43.1 us
    ppermute x0 -> x2, starting transfers between devices: none -> 22.1 us  [the longest x1 19.4 us: body(): across = lax.ppermute(send, 'row', [(i, i ^ 3) for i in range(size)])]
    ppermute x1, starting transfers between devices: 20.5 us -> 0.01 us  [body(): received = lax.ppermute(send, 'row', partner)]
    all_to_all x1, starting transfers between devices: 16.2 us -> 12.8 us  [body(): lax.all_to_all(spread, 'row', 0, 0, axis_index_groups=alike, tiled=True)]
    unnamed x8 -> x6, local copies, waits for them, and re-layouts: 2.87 us -> 1.05 us
    ppermute x0 -> x2, waiting for transfers between devices: none -> 1.56 us  [the longest x1 1.56 us: body(): across = lax.ppermute(send, 'row', [(i, i ^ 3) for i in range(size)])]
    ppermute x1, waiting for transfers between devices: 0.82 us -> 0.01 us  [body(): received = lax.ppermute(send, 'row', partner)]
    ppermute x1, starting transfers between devices: 3.02 us -> 2.36 us  [body(): lax.ppermute(elevation[-4:], 'row', [(i, i + 1) for i in range(size - 1)])]
  transfers between devices with their start and end apart: 5 -> 7, of which waited for: 2 -> 2; matrix products, arithmetic and copies ran while one was open for 0% -> 0% of each run, Pallas kernels for 4% -> 5%
where the time goes in v5:
time: 61.1 us; the launch traced here: 60.8 us
  starting transfers between devices  43.1 us (71%)
  waiting for transfers between devices  8.42 us (14%)
  Pallas kernels  8.18 us (13%)
  local copies, waits for them, and re-layouts  1.1 us (2%)
    ppermute x1, starting transfers between devices, body(): across = lax.ppermute(send, 'row', [(i, i ^ 3) for i in range(size)])  19.4 us
    all_to_all x1, starting transfers between devices, body(): lax.all_to_all(spread, 'row', 0, 0, axis_index_groups=alike, tiled=True)  12.8 us
    all_to_all x1, waiting for transfers between devices, body(): lax.all_to_all(spread, 'row', 0, 0, axis_index_groups=alike, tiled=True)  6.85 us
    ppermute x1, starting transfers between devices, body(): lax.ppermute(elevation[:4], 'row', [(i + 1, i) for i in range(size - 1)])  3.39 us
    pallas_call x1, Pallas kernels, gradients(): pl.pallas_call(gradient_kernel, out_shape=(shape, shape, pltpu.VMEM(middl...  2.98 us
    ppermute x1, starting transfers between devices, body(): beside = lax.ppermute(keep, 'row', [(i, i ^ 2) for i in range(size)])  2.72 us
    ppermute x1, starting transfers between devices, body(): theirs = lax.ppermute(mine, 'row', partner)  2.43 us
    ppermute x1, starting transfers between devices, body(): lax.ppermute(elevation[-4:], 'row', [(i, i + 1) for i in range(size - 1)])  2.36 us
  transfers between devices with their start and end apart: 7, of which 2 were waited for; matrix products, arithmetic and copies ran while one was open for 0% of the time, Pallas kernels for 5%

profile of v5, /device:TPU:37, one launch (start us, length us, event | category | flops | bytes accessed | tf_op | source)
XLA Modules:
  0.0 60.8 jit_solution(17255982038062885457)
XLA Ops:
  0.0 0.0 copy-start
  0.0 1.0 %copy-done = f32[16,8192]{1,0:T(8,128)S(1)} copy-done((f32[16,8192]{1,0:T(8,128)S(1)}, f32[16,8192]{1,0:T(8,128)}, u32[]{:S(2)}) %copy-start) | copy-done | bytes 524312
  1.0 0.0 copy-start.1
  1.0 2.4 %count.1 = (f32[1,640]{1,0:T(1,128)S(1)}, f32[1,640]{1,0:T(1,128)S(1)}) custom-call(f32[16,8192]{1,0:T(8,128)S(1)} %copy-done, s32[1]{0:T(128)} %bitcast.core_ref), custom_call_target="tpu_custom_call" | custom-call | tf_op jit(solution)/shard_map/count/pallas_call | solution.py:83
  3.4 2.7 %collective-permute-start.1 = (f32[1,640]{1,0:T(1,128)S(1)}, f32[1,640]{1,0:T(1,128)S(1)}, u32[]{:S(2)}, u32[]{:S(2)}) collective-permute-start(f32[1,640]{1,0:T(1,128)S(1)} %get-tuple-element.11.a_ref), channel_id=1, source_target_pairs={{0,2},{1,3},{2,0},{3,1},{4,6},{5,7},{6,4},{7,5},{8,10},{9,11},{10,... | collective-permute-start | bytes 7688 | tf_op jit(solution)/shard_map/ppermute | solution.py:279
  6.1 19.4 %collective-permute-start.2 = (f32[1,640]{1,0:T(1,128)S(1)}, f32[1,640]{1,0:T(1,128)S(1)}, u32[]{:S(2)}, u32[]{:S(2)}) collective-permute-start(f32[1,640]{1,0:T(1,128)S(1)} %get-tuple-element.12), channel_id=1, source_target_pairs={{0,3},{1,2},{2,1},{3,0},{4,7},{5,6},{6,5},{7,4},{8,11},{9,10},{10,... | collective-permute-start | bytes 7688 | tf_op jit(solution)/shard_map/ppermute | solution.py:280
  25.5 0.0 collective-permute-start
  25.5 0.0 collective-permute-done.1.c_ref
  25.5 1.6 %collective-permute-done.2.d_ref = f32[1,640]{1,0:T(1,128)S(1)} collective-permute-done((f32[1,640]{1,0:T(1,128)S(1)}, f32[1,640]{1,0:T(1,128)S(1)}, u32[]{:S(2)}, u32[]{:S(2)}) %collective-permute-start.2) | collective-permute-done | bytes 2592 | tf_op jit(solution)/shard_map/ppermute | solution.py:280
  27.1 0.0 collective-permute-done.b_ref
  27.1 0.6 %join.1 = f32[16,1,640]{2,1,0:T(1,128)} custom-call(f32[1,640]{1,0:T(1,128)S(1)} %get-tuple-element.11.a_ref, f32[1,640]{1,0:T(1,128)S(1)} %collective-permute-done.b_ref, f32[1,640]{1,0:T(1,128)S(1)} %collective-permute-done.1.c_ref, f32[1,640]{1,0:T(1,128)S(1)} %collective-permute-done.2.d_ref), custom_call_target="tpu_custom_call" | custom-call | tf_op jit(solution)/shard_map/join/pallas_call | solution.py:103
  27.7 12.8 %all-to-all-start = ((f32[16,1,640]{2,1,0:T(1,128)}), f32[16,1,640]{2,1,0:T(1,128)S(1)}, u32[]{:S(2)}, u32[]{:S(2)}) async-start(f32[16,1,640]{2,1,0:T(1,128)} %join.1), calls=%async_computation | async-start | bytes 81920 | tf_op jit(solution)/shard_map/all_to_all | solution.py:284
  40.5 0.0 copy-done.1
  40.5 3.4 %collective-permute-start.5 = (f32[4,8192]{1,0:T(4,128)S(1)}, f32[4,8192]{1,0:T(4,128)S(1)}, u32[]{:S(2)}, u32[]{:S(2)}) collective-permute-start(f32[4,8192]{1,0:T(4,128)S(1)} %get-tuple-element.17), channel_id=1, source_target_pairs={{1,0},{2,1},{3,2},{4,3},{5,4},{6,5},{7,6},{8,7},{9,8},{10,9},{11,1... | collective-permute-start | bytes 393224 | tf_op jit(solution)/shard_map/ppermute | solution.py:287
  43.9 0.0 copy-start.2
  44.0 2.4 %collective-permute-start.4 = (f32[4,8192]{1,0:T(4,128)S(1)}, f32[4,8192]{1,0:T(4,128)S(1)}, u32[]{:S(2)}, u32[]{:S(2)}) collective-permute-start(f32[4,8192]{1,0:T(4,128)S(1)} %get-tuple-element.18), channel_id=1, source_target_pairs={{0,1},{1,2},{2,3},{3,4},{4,5},{5,6},{6,7},{7,8},{8,9},{9,10},{10,1... | collective-permute-start | bytes 393224 | tf_op jit(solution)/shard_map/ppermute | solution.py:286
  46.3 6.8 %all-to-all-done.x_ref = f32[16,1,640]{2,1,0:T(1,128)S(1)} async-done(((f32[16,1,640]{2,1,0:T(1,128)}), f32[16,1,640]{2,1,0:T(1,128)S(1)}, u32[]{:S(2)}, u32[]{:S(2)}) %all-to-all-start) | async-done | bytes 40992 | tf_op jit(solution)/shard_map/all_to_all | solution.py:284
  53.2 2.4 %collective-permute-start.3 = (f32[1,640]{1,0:T(1,128)S(1)}, f32[1,640]{1,0:T(1,128)S(1)}, u32[]{:S(2)}, u32[]{:S(2)}) collective-permute-start(f32[1,640]{1,0:T(1,128)S(1)} %gather.1.mine), channel_id=1, source_target_pairs={{0,1},{1,0},{2,3},{3,2},{4,5},{5,4},{6,7},{7,6},{8,9},{9,8},{10,11... | collective-permute-start | bytes 7688 | tf_op jit(solution)/shard_map/ppermute | solution.py:293
  55.6 0.0 collective-permute-done.5.below
  55.6 0.0 collective-permute-done.4.above
  55.6 0.0 copy-done.2
  55.6 3.0 %gradients.1 = (f32[16,8192]{1,0:T(8,128)S(1)}, f32[16,8192]{1,0:T(8,128)S(1)}, s32[16,8192]{1,0:T(8,128)S(1)}, s32[2,128]{1,0:T(2,128)S(1)}) custom-call(f32[4,8192]{1,0:T(4,128)S(1)} %collective-permute-done.4.above, f32[16,8192]{1,0:T(8,128)S(1)} %copy-done.1, f32[4,8192]{1,0:T(4,128)S(1)} %collective-permute-done.5.below, s32[2]{0:T(128)S(1)} %copy-done.2), custom_call_target="tpu_custom_call" | custom-call | tf_op jit(solution)/shard_map/gradients/pallas_call | solution.py:171
  58.6 0.0 collective-permute-done.3.theirs
  58.6 2.2 %shade.1 = f32[16,8192]{1,0:T(8,128)} custom-call(f32[1,640]{1,0:T(1,128)S(1)} %gather.1.mine, f32[1,640]{1,0:T(1,128)S(1)} %collective-permute-done.3.theirs, s32[1]{0:T(128)} %bitcast.core_ref, s32[2,128]{1,0:T(2,128)S(1)} %get-tuple-element.13.limits, s32[16,8192]{1,0:T(8,128)S(1)} %get-tuple-element.14.bins, f32[16,8192]{1,0:T(8,128)S(1)} %get-tuple-element.15.gx_ref, ...), custom_call_target="tpu_custom_call" | custom-call | tf_op jit(solution)/shard_map/shade/pallas_call | solution.py:253
  (2 shorter events, 0.1 us)
Async XLA Ops:
  0.0 1.0 %copy-start = (f32[16,8192]{1,0:T(8,128)S(1)}, f32[16,8192]{1,0:T(8,128)}, u32[]{:S(2)}) copy-start(f32[16,8192]{1,0:T(8,128)} %middle.1) | copy-start | bytes 1572868
  1.0 39.4 %copy-start.1 = (f32[16,8192]{1,0:T(8,128)S(1)}, f32[16,8192]{1,0:T(8,128)}, u32[]{:S(2)}) copy-start(f32[16,8192]{1,0:T(8,128)} %middle.1) | copy-start | bytes 1572868
  3.4 22.1 %collective-permute-start.1 = (f32[1,640]{1,0:T(1,128)S(1)}, f32[1,640]{1,0:T(1,128)S(1)}, u32[]{:S(2)}, u32[]{:S(2)}) collective-permute-start(f32[1,640]{1,0:T(1,128)S(1)} %get-tuple-element.11.a_ref), channel_id=1, source_target_pairs={{0,2},{1,3},{2,0},{3,1},{4,6},{5,7},{6,4},{7,5},{8,10},{9,11},{10,... | collective-permute-start | bytes 7688 | tf_op jit(solution)/shard_map/ppermute | solution.py:279
  6.1 20.9 %collective-permute-start.2 = (f32[1,640]{1,0:T(1,128)S(1)}, f32[1,640]{1,0:T(1,128)S(1)}, u32[]{:S(2)}, u32[]{:S(2)}) collective-permute-start(f32[1,640]{1,0:T(1,128)S(1)} %get-tuple-element.12), channel_id=1, source_target_pairs={{0,3},{1,2},{2,1},{3,0},{4,7},{5,6},{6,5},{7,4},{8,11},{9,10},{10,... | collective-permute-start | bytes 7688 | tf_op jit(solution)/shard_map/ppermute | solution.py:280
  25.5 1.6 %collective-permute-start = (f32[1,640]{1,0:T(1,128)S(1)}, f32[1,640]{1,0:T(1,128)S(1)}, u32[]{:S(2)}, u32[]{:S(2)}) collective-permute-start(f32[1,640]{1,0:T(1,128)S(1)} %get-tuple-element.12), channel_id=1, source_target_pairs={{0,1},{1,0},{2,3},{3,2},{4,5},{5,4},{6,7},{7,6},{8,9},{9,8},{10,11... | collective-permute-start | bytes 7688 | tf_op jit(solution)/shard_map/ppermute | solution.py:278
  27.7 25.5 %all-to-all-start = ((f32[16,1,640]{2,1,0:T(1,128)}), f32[16,1,640]{2,1,0:T(1,128)S(1)}, u32[]{:S(2)}, u32[]{:S(2)}) async-start(f32[16,1,640]{2,1,0:T(1,128)} %join.1), calls=%async_computation | async-start | bytes 81920 | tf_op jit(solution)/shard_map/all_to_all | solution.py:284
  40.5 15.1 %collective-permute-start.5 = (f32[4,8192]{1,0:T(4,128)S(1)}, f32[4,8192]{1,0:T(4,128)S(1)}, u32[]{:S(2)}, u32[]{:S(2)}) collective-permute-start(f32[4,8192]{1,0:T(4,128)S(1)} %get-tuple-element.17), channel_id=1, source_target_pairs={{1,0},{2,1},{3,2},{4,3},{5,4},{6,5},{7,6},{8,7},{9,8},{10,9},{11,1... | collective-permute-start | bytes 393224 | tf_op jit(solution)/shard_map/ppermute | solution.py:287
  43.9 11.7 %copy-start.2 = (s32[2]{0:T(128)S(1)}, s32[2]{0:T(128)}, u32[]{:S(2)}) copy-start(s32[2]{0:T(128)} %ranks.1) | copy-start | bytes 28
  44.0 11.7 %collective-permute-start.4 = (f32[4,8192]{1,0:T(4,128)S(1)}, f32[4,8192]{1,0:T(4,128)S(1)}, u32[]{:S(2)}, u32[]{:S(2)}) collective-permute-start(f32[4,8192]{1,0:T(4,128)S(1)} %get-tuple-element.18), channel_id=1, source_target_pairs={{0,1},{1,2},{2,3},{3,4},{4,5},{5,6},{6,7},{7,8},{8,9},{9,10},{10,1... | collective-permute-start | bytes 393224 | tf_op jit(solution)/shard_map/ppermute | solution.py:286
  53.2 5.4 %collective-permute-start.3 = (f32[1,640]{1,0:T(1,128)S(1)}, f32[1,640]{1,0:T(1,128)S(1)}, u32[]{:S(2)}, u32[]{:S(2)}) collective-permute-start(f32[1,640]{1,0:T(1,128)S(1)} %gather.1.mine), channel_id=1, source_target_pairs={{0,1},{1,0},{2,3},{3,2},{4,5},{5,4},{6,7},{7,6},{8,9},{9,8},{10,11... | collective-permute-start | bytes 7688 | tf_op jit(solution)/shard_map/ppermute | solution.py:293

commit v6 on v5

--- a/solution.py
+++ b/solution.py
@@ -32,7 +32,7 @@
     return pltpu.with_memory_space_constraint(x, pltpu.VMEM)
 
 
-def count_kernel(heights, core_ref, keep_ref, send_ref, upper, lower):
+def count_kernel(heights, keep_ref, send_ref, upper, lower):
     rows, width = heights.shape
     high_count = BINS // LOW
     bins = bin_of(heights[...])
@@ -64,7 +64,7 @@
     )
     highest = jnp.max(heights[...])
     neg_lowest = -jnp.min(heights[...])
-    first = core_ref[0] == 0
+    first = lax.axis_index("row") & 1 == 0
     for i in range(4):
         cols = slice(i * LANES, (i + 1) * LANES)
         keep_ref[:, cols] = jnp.where(first, flat[i : i + 1], flat[4 + i : 5 + i])
@@ -75,20 +75,19 @@
 
 VMEM_SPEC = pl.BlockSpec(memory_space=pltpu.VMEM)
 SMALL = pltpu.CompilerParams(vmem_limit_bytes=16 * 2**20)
-SMEM_SPEC = pl.BlockSpec(memory_space=pltpu.SMEM)
-
-
-def count(elevation, core):
+
+
+def count(elevation):
     shape = pltpu.VMEM((1, WIRE), jnp.float32)
     return pl.pallas_call(
         count_kernel,
         out_shape=(shape, shape),
-        in_specs=[VMEM_SPEC, SMEM_SPEC],
+        in_specs=[VMEM_SPEC],
         out_specs=(VMEM_SPEC,) * 2,
         scratch_shapes=[pltpu.VMEM(elevation.shape, jnp.float32)] * 2,
         name="count",
         compiler_params=SMALL,
-    )(elevation, core)
+    )(elevation)
 
 
 def join_kernel(a_ref, b_ref, c_ref, d_ref, out_ref):
@@ -128,8 +127,9 @@
 
 
 def gradient_kernel(above, middle, below, ranks, gx_ref, gy_ref, bin_ref, rank_ref, wide):
-    rank_ref[:1] = jnp.full((1, LANES), ranks[0])
-    rank_ref[1:] = jnp.full((1, LANES), ranks[1] - ranks[0])
+    low, high = ranks[:, :1], ranks[:, 1:]
+    rank_ref[:1] = jnp.broadcast_to(low, (1, LANES))
+    rank_ref[1:] = jnp.broadcast_to(high - low, (1, LANES))
     rows, width = middle.shape
     halo = above.shape[0]
     edge = jnp.zeros((rows + 2 * halo, LANES), jnp.float32)
@@ -176,7 +176,7 @@
             pltpu.VMEM(middle.shape, jnp.int32),
             pltpu.VMEM((2, LANES), jnp.int32),
         ),
-        in_specs=[VMEM_SPEC] * 3 + [SMEM_SPEC],
+        in_specs=[VMEM_SPEC] * 4,
         out_specs=(VMEM_SPEC,) * 4,
         scratch_shapes=[
             pltpu.VMEM((rows + 2 * above.shape[0], width + 2 * LANES), jnp.float32)
@@ -201,8 +201,8 @@
     return inside
 
 
-def shade_kernel(mine, theirs, core_ref, limits, bins, gx_ref, gy_ref, out_ref, done, sems):
-    first = core_ref[0] == 0
+def shade_kernel(mine, theirs, limits, bins, gx_ref, gy_ref, out_ref, done, sems):
+    first = lax.axis_index("row") & 1 == 0
     a, b = mine[...], theirs[...]
     lower = jnp.where(first, a, b)
     upper = jnp.where(first, b, a)
@@ -249,11 +249,11 @@
         copy.wait()
 
 
-def shade(mine, theirs, core, limits, bins, gx, gy):
+def shade(mine, theirs, limits, bins, gx, gy):
     return pl.pallas_call(
         shade_kernel,
         out_shape=jax.ShapeDtypeStruct(gx.shape, jnp.float32),
-        in_specs=[VMEM_SPEC, VMEM_SPEC, SMEM_SPEC, VMEM_SPEC, VMEM_SPEC, VMEM_SPEC, VMEM_SPEC],
+        in_specs=[VMEM_SPEC] * 6,
         out_specs=pl.BlockSpec(memory_space=pl.ANY),
         scratch_shapes=[
             pltpu.VMEM(gx.shape, jnp.float32),
@@ -261,20 +261,18 @@
         ],
         name="shade",
         compiler_params=SMALL,
-    )(mine, theirs, core, limits, bins, gx, gy)
+    )(mine, theirs, limits, bins, gx, gy)
 
 
 def body(elevation, ranks):
     size = lax.axis_size("row")
-    core = lax.axis_index("row") & 1
-    core = core.astype(jnp.int32).reshape(1)
     partner = [(i, i ^ 1) for i in range(size)]
     blocks = size // 4
     begin = blocks * 3 // 4
     order = [(i + begin) % blocks for i in range(blocks)]
     alike = [[4 * i + place for i in order] for place in range(4)]
     local = in_vmem(elevation)
-    keep, send = count(local, core)
+    keep, send = count(local)
     received = lax.ppermute(send, "row", partner)
     beside = lax.ppermute(keep, "row", [(i, i ^ 2) for i in range(size)])
     across = lax.ppermute(send, "row", [(i, i ^ 3) for i in range(size)])
@@ -286,13 +284,13 @@
     above = lax.ppermute(elevation[-4:], "row", [(i, i + 1) for i in range(size - 1)])
     below = lax.ppermute(elevation[:4], "row", [(i + 1, i) for i in range(size - 1)])
     gx, gy, bins, limits = gradients(
-        in_vmem(above), local, in_vmem(below), ranks
+        in_vmem(above), local, in_vmem(below), in_vmem(ranks.reshape(1, 2))
     )
 
     mine = gather(in_vmem(everyone))
     theirs = lax.ppermute(mine, "row", partner)
     return shade(
-        in_vmem(mine), in_vmem(theirs), core, in_vmem(limits), in_vmem(bins), in_vmem(gx), in_vmem(gy)
+        in_vmem(mine), in_vmem(theirs), in_vmem(limits), in_vmem(bins), in_vmem(gx), in_vmem(gy)
     )
 
 

time: 61.1 us -> 60.6 us (level)
  transfers between devices with their start and end apart: 7 -> 7, of which waited for: 2 -> 2; matrix products, arithmetic and copies ran while one was open for 0% -> 0% of each run, Pallas kernels for 5% -> 4%
where the time goes in v6:
time: 60.6 us; the launch traced here: 60.3 us
  starting transfers between devices  43.1 us (71%)
  waiting for transfers between devices  8.43 us (14%)
  Pallas kernels  7.68 us (13%)
  local copies, waits for them, and re-layouts  1.1 us (2%)
    ppermute x1, starting transfers between devices, body(): across = lax.ppermute(send, 'row', [(i, i ^ 3) for i in range(size)])  19.4 us
    all_to_all x1, starting transfers between devices, body(): lax.all_to_all(spread, 'row', 0, 0, axis_index_groups=alike, tiled=True)  12.8 us
    all_to_all x1, waiting for transfers between devices, body(): lax.all_to_all(spread, 'row', 0, 0, axis_index_groups=alike, tiled=True)  6.86 us
    ppermute x1, starting transfers between devices, body(): lax.ppermute(elevation[:4], 'row', [(i + 1, i) for i in range(size - 1)])  3.39 us
    ppermute x1, starting transfers between devices, body(): beside = lax.ppermute(keep, 'row', [(i, i ^ 2) for i in range(size)])  2.72 us
    pallas_call x1, Pallas kernels, gradients(): pl.pallas_call(gradient_kernel, out_shape=(shape, shape, pltpu.VMEM(middl...  2.45 us
    ppermute x1, starting transfers between devices, body(): theirs = lax.ppermute(mine, 'row', partner)  2.43 us
    ppermute x1, starting transfers between devices, body(): lax.ppermute(elevation[-4:], 'row', [(i, i + 1) for i in range(size - 1)])  2.36 us
  transfers between devices with their start and end apart: 7, of which 2 were waited for; matrix products, arithmetic and copies ran while one was open for 0% of the time, Pallas kernels for 4%

profile of v6, /device:TPU:37, one launch (start us, length us, event | category | flops | bytes accessed | tf_op | source)
XLA Modules:
  0.0 60.3 jit_solution(14155609940316383173)
XLA Ops:
  0.0 0.0 copy-start
  0.0 1.0 %copy-done = f32[16,8192]{1,0:T(8,128)S(1)} copy-done((f32[16,8192]{1,0:T(8,128)S(1)}, f32[16,8192]{1,0:T(8,128)}, u32[]{:S(2)}) %copy-start) | copy-done | bytes 524312
  1.0 0.0 copy-start.1
  1.0 2.4 %count.1 = (f32[1,640]{1,0:T(1,128)S(1)}, f32[1,640]{1,0:T(1,128)S(1)}) custom-call(f32[16,8192]{1,0:T(8,128)S(1)} %copy-done), custom_call_target="tpu_custom_call" | custom-call | tf_op jit(solution)/shard_map/count/pallas_call | solution.py:82
  3.4 2.7 %collective-permute-start.1 = (f32[1,640]{1,0:T(1,128)S(1)}, f32[1,640]{1,0:T(1,128)S(1)}, u32[]{:S(2)}, u32[]{:S(2)}) collective-permute-start(f32[1,640]{1,0:T(1,128)S(1)} %get-tuple-element.11.a_ref), channel_id=1, source_target_pairs={{0,2},{1,3},{2,0},{3,1},{4,6},{5,7},{6,4},{7,5},{8,10},{9,11},{10,... | collective-permute-start | bytes 7688 | tf_op jit(solution)/shard_map/ppermute | solution.py:277
  6.1 19.4 %collective-permute-start.2 = (f32[1,640]{1,0:T(1,128)S(1)}, f32[1,640]{1,0:T(1,128)S(1)}, u32[]{:S(2)}, u32[]{:S(2)}) collective-permute-start(f32[1,640]{1,0:T(1,128)S(1)} %get-tuple-element.12), channel_id=1, source_target_pairs={{0,3},{1,2},{2,1},{3,0},{4,7},{5,6},{6,5},{7,4},{8,11},{9,10},{10,... | collective-permute-start | bytes 7688 | tf_op jit(solution)/shard_map/ppermute | solution.py:278
  25.5 0.0 collective-permute-start
  25.5 0.0 collective-permute-done.1.c_ref
  25.5 1.6 %collective-permute-done.2.d_ref = f32[1,640]{1,0:T(1,128)S(1)} collective-permute-done((f32[1,640]{1,0:T(1,128)S(1)}, f32[1,640]{1,0:T(1,128)S(1)}, u32[]{:S(2)}, u32[]{:S(2)}) %collective-permute-start.2) | collective-permute-done | bytes 2592 | tf_op jit(solution)/shard_map/ppermute | solution.py:278
  27.1 0.0 collective-permute-done.b_ref
  27.1 0.6 %join.1 = f32[16,1,640]{2,1,0:T(1,128)} custom-call(f32[1,640]{1,0:T(1,128)S(1)} %get-tuple-element.11.a_ref, f32[1,640]{1,0:T(1,128)S(1)} %collective-permute-done.b_ref, f32[1,640]{1,0:T(1,128)S(1)} %collective-permute-done.1.c_ref, f32[1,640]{1,0:T(1,128)S(1)} %collective-permute-done.2.d_ref), custom_call_target="tpu_custom_call" | custom-call | tf_op jit(solution)/shard_map/join/pallas_call | solution.py:102
  27.7 12.8 %all-to-all-start = ((f32[16,1,640]{2,1,0:T(1,128)}), f32[16,1,640]{2,1,0:T(1,128)S(1)}, u32[]{:S(2)}, u32[]{:S(2)}) async-start(f32[16,1,640]{2,1,0:T(1,128)} %join.1), calls=%async_computation | async-start | bytes 81920 | tf_op jit(solution)/shard_map/all_to_all | solution.py:282
  40.5 0.0 copy-done.1
  40.5 3.4 %collective-permute-start.5 = (f32[4,8192]{1,0:T(4,128)S(1)}, f32[4,8192]{1,0:T(4,128)S(1)}, u32[]{:S(2)}, u32[]{:S(2)}) collective-permute-start(f32[4,8192]{1,0:T(4,128)S(1)} %get-tuple-element.17), channel_id=1, source_target_pairs={{1,0},{2,1},{3,2},{4,3},{5,4},{6,5},{7,6},{8,7},{9,8},{10,9},{11,1... | collective-permute-start | bytes 393224 | tf_op jit(solution)/shard_map/ppermute | solution.py:285
  43.9 2.4 %collective-permute-start.4 = (f32[4,8192]{1,0:T(4,128)S(1)}, f32[4,8192]{1,0:T(4,128)S(1)}, u32[]{:S(2)}, u32[]{:S(2)}) collective-permute-start(f32[4,8192]{1,0:T(4,128)S(1)} %get-tuple-element.18), channel_id=1, source_target_pairs={{0,1},{1,2},{2,3},{3,4},{4,5},{5,6},{6,7},{7,8},{8,9},{9,10},{10,1... | collective-permute-start | bytes 393224 | tf_op jit(solution)/shard_map/ppermute | solution.py:284
  46.3 6.9 %all-to-all-done.x_ref = f32[16,1,640]{2,1,0:T(1,128)S(1)} async-done(((f32[16,1,640]{2,1,0:T(1,128)}), f32[16,1,640]{2,1,0:T(1,128)S(1)}, u32[]{:S(2)}, u32[]{:S(2)}) %all-to-all-start) | async-done | bytes 40992 | tf_op jit(solution)/shard_map/all_to_all | solution.py:282
  53.2 0.0 copy-start.2
  53.2 2.4 %collective-permute-start.3 = (f32[1,640]{1,0:T(1,128)S(1)}, f32[1,640]{1,0:T(1,128)S(1)}, u32[]{:S(2)}, u32[]{:S(2)}) collective-permute-start(f32[1,640]{1,0:T(1,128)S(1)} %gather.1.mine), channel_id=1, source_target_pairs={{0,1},{1,0},{2,3},{3,2},{4,5},{5,4},{6,7},{7,6},{8,9},{9,8},{10,11... | collective-permute-start | bytes 7688 | tf_op jit(solution)/shard_map/ppermute | solution.py:291
  55.7 0.0 collective-permute-done.5.below
  55.7 0.0 collective-permute-done.4.above
  55.7 0.0 copy-done.2
  55.7 2.4 %gradients.1 = (f32[16,8192]{1,0:T(8,128)S(1)}, f32[16,8192]{1,0:T(8,128)S(1)}, s32[16,8192]{1,0:T(8,128)S(1)}, s32[2,128]{1,0:T(2,128)S(1)}) custom-call(f32[4,8192]{1,0:T(4,128)S(1)} %collective-permute-done.4.above, f32[16,8192]{1,0:T(8,128)S(1)} %copy-done.1, f32[4,8192]{1,0:T(4,128)S(1)} %collective-permute-done.5.below, s32[1,2]{1,0:T(1,128)S(1)} %bitcast.1), custom_call_target="tpu_custom_call" | custom-call | tf_op jit(solution)/shard_map/gradients/pallas_call | solution.py:171
  58.1 0.0 collective-permute-done.3.theirs
  58.1 2.2 %shade.1 = f32[16,8192]{1,0:T(8,128)} custom-call(f32[1,640]{1,0:T(1,128)S(1)} %gather.1.mine, f32[1,640]{1,0:T(1,128)S(1)} %collective-permute-done.3.theirs, s32[2,128]{1,0:T(2,128)S(1)} %get-tuple-element.13.limits, s32[16,8192]{1,0:T(8,128)S(1)} %get-tuple-element.14.bins, f32[16,8192]{1,0:T(8,128)S(1)} %get-tuple-element.15.gx_ref, ...), custom_call_target="tpu_custom_call" | custom-call | tf_op jit(solution)/shard_map/shade/pallas_call | solution.py:253
  (2 shorter events, 0.1 us)
Async XLA Ops:
  0.0 1.0 %copy-start = (f32[16,8192]{1,0:T(8,128)S(1)}, f32[16,8192]{1,0:T(8,128)}, u32[]{:S(2)}) copy-start(f32[16,8192]{1,0:T(8,128)} %middle.1) | copy-start | bytes 1572868
  1.0 39.4 %copy-start.1 = (f32[16,8192]{1,0:T(8,128)S(1)}, f32[16,8192]{1,0:T(8,128)}, u32[]{:S(2)}) copy-start(f32[16,8192]{1,0:T(8,128)} %middle.1) | copy-start | bytes 1572868
  3.4 22.1 %collective-permute-start.1 = (f32[1,640]{1,0:T(1,128)S(1)}, f32[1,640]{1,0:T(1,128)S(1)}, u32[]{:S(2)}, u32[]{:S(2)}) collective-permute-start(f32[1,640]{1,0:T(1,128)S(1)} %get-tuple-element.11.a_ref), channel_id=1, source_target_pairs={{0,2},{1,3},{2,0},{3,1},{4,6},{5,7},{6,4},{7,5},{8,10},{9,11},{10,... | collective-permute-start | bytes 7688 | tf_op jit(solution)/shard_map/ppermute | solution.py:277
  6.1 20.9 %collective-permute-start.2 = (f32[1,640]{1,0:T(1,128)S(1)}, f32[1,640]{1,0:T(1,128)S(1)}, u32[]{:S(2)}, u32[]{:S(2)}) collective-permute-start(f32[1,640]{1,0:T(1,128)S(1)} %get-tuple-element.12), channel_id=1, source_target_pairs={{0,3},{1,2},{2,1},{3,0},{4,7},{5,6},{6,5},{7,4},{8,11},{9,10},{10,... | collective-permute-start | bytes 7688 | tf_op jit(solution)/shard_map/ppermute | solution.py:278
  25.5 1.6 %collective-permute-start = (f32[1,640]{1,0:T(1,128)S(1)}, f32[1,640]{1,0:T(1,128)S(1)}, u32[]{:S(2)}, u32[]{:S(2)}) collective-permute-start(f32[1,640]{1,0:T(1,128)S(1)} %get-tuple-element.12), channel_id=1, source_target_pairs={{0,1},{1,0},{2,3},{3,2},{4,5},{5,4},{6,7},{7,6},{8,9},{9,8},{10,11... | collective-permute-start | bytes 7688 | tf_op jit(solution)/shard_map/ppermute | solution.py:276
  27.7 25.5 %all-to-all-start = ((f32[16,1,640]{2,1,0:T(1,128)}), f32[16,1,640]{2,1,0:T(1,128)S(1)}, u32[]{:S(2)}, u32[]{:S(2)}) async-start(f32[16,1,640]{2,1,0:T(1,128)} %join.1), calls=%async_computation | async-start | bytes 81920 | tf_op jit(solution)/shard_map/all_to_all | solution.py:282
  40.5 15.1 %collective-permute-start.5 = (f32[4,8192]{1,0:T(4,128)S(1)}, f32[4,8192]{1,0:T(4,128)S(1)}, u32[]{:S(2)}, u32[]{:S(2)}) collective-permute-start(f32[4,8192]{1,0:T(4,128)S(1)} %get-tuple-element.17), channel_id=1, source_target_pairs={{1,0},{2,1},{3,2},{4,3},{5,4},{6,5},{7,6},{8,7},{9,8},{10,9},{11,1... | collective-permute-start | bytes 393224 | tf_op jit(solution)/shard_map/ppermute | solution.py:285
  43.9 11.7 %collective-permute-start.4 = (f32[4,8192]{1,0:T(4,128)S(1)}, f32[4,8192]{1,0:T(4,128)S(1)}, u32[]{:S(2)}, u32[]{:S(2)}) collective-permute-start(f32[4,8192]{1,0:T(4,128)S(1)} %get-tuple-element.18), channel_id=1, source_target_pairs={{0,1},{1,2},{2,3},{3,4},{4,5},{5,6},{6,7},{7,8},{8,9},{9,10},{10,1... | collective-permute-start | bytes 393224 | tf_op jit(solution)/shard_map/ppermute | solution.py:284
  53.2 2.5 %copy-start.2 = (s32[2]{0:T(128)S(1)}, s32[2]{0:T(128)}, u32[]{:S(2)}) copy-start(s32[2]{0:T(128)} %param.4) | copy-start | bytes 28
  53.2 4.9 %collective-permute-start.3 = (f32[1,640]{1,0:T(1,128)S(1)}, f32[1,640]{1,0:T(1,128)S(1)}, u32[]{:S(2)}, u32[]{:S(2)}) collective-permute-start(f32[1,640]{1,0:T(1,128)S(1)} %gather.1.mine), channel_id=1, source_target_pairs={{0,1},{1,0},{2,3},{3,2},{4,5},{5,4},{6,7},{7,6},{8,9},{9,8},{10,11... | collective-permute-start | bytes 7688 | tf_op jit(solution)/shard_map/ppermute | solution.py:291

commit v7 on v6

--- a/solution.py
+++ b/solution.py
@@ -15,7 +15,6 @@
 cos_zenith = 0.70710678
 sin_zenith = 0.70710678
 light_y = 0.70710678
-HIGHEST = lax.Precision.HIGHEST
 HOT = jnp.float8_e4m3fn
 STEPS = 65535.0
 
@@ -32,8 +31,18 @@
     return pltpu.with_memory_space_constraint(x, pltpu.VMEM)
 
 
-def count_kernel(heights, keep_ref, send_ref, upper, lower):
+def count_kernel(source, keep_ref, send_ref, heights, upper, lower, sems):
     rows, width = heights.shape
+    part = width // sems.shape[0]
+    copies = []
+    for i in range(sems.shape[0]):
+        some = slice(i * part, (i + 1) * part)
+        copies.append(
+            pltpu.make_async_copy(source.at[:, some], heights.at[:, some], sems.at[i])
+        )
+        copies[-1].start()
+    for copy in copies:
+        copy.wait()
     high_count = BINS // LOW
     bins = bin_of(heights[...])
     up = jnp.floor(bins * (1.0 / LOW))
@@ -55,20 +64,19 @@
             (((1,), (1,)), ((), ())),
             preferred_element_type=jnp.float32,
         )
-    spread = (iota((LOW, LANES), 1) % LOW == iota((LOW, LANES), 0)).astype(jnp.float32)
-    tiled = jnp.dot(grid, spread, precision=HIGHEST, preferred_element_type=jnp.float32)
+    tiled = jnp.concatenate([grid] * (LANES // LOW), axis=1)
     quarter = iota((high_count, LANES), 1) // LOW == iota((high_count, LANES), 0) % 4
-    fold = (iota((8, high_count), 1) // 4 == iota((8, high_count), 0)).astype(jnp.float32)
-    flat = jnp.dot(
-        fold, jnp.where(quarter, tiled, 0.0), precision=HIGHEST, preferred_element_type=jnp.float32
-    )
+    flat = jnp.where(quarter, tiled, 0.0)
+    flat = flat + pltpu.roll(flat, high_count - 1, 0)
+    flat = flat + pltpu.roll(flat, high_count - 2, 0)
     highest = jnp.max(heights[...])
     neg_lowest = -jnp.min(heights[...])
     first = lax.axis_index("row") & 1 == 0
     for i in range(4):
         cols = slice(i * LANES, (i + 1) * LANES)
-        keep_ref[:, cols] = jnp.where(first, flat[i : i + 1], flat[4 + i : 5 + i])
-        send_ref[:, cols] = jnp.where(first, flat[4 + i : 5 + i], flat[i : i + 1])
+        lower_row, upper_row = (flat[j : j + 1] for j in (4 * i, 4 * i + 16))
+        keep_ref[:, cols] = jnp.where(first, lower_row, upper_row)
+        send_ref[:, cols] = jnp.where(first, upper_row, lower_row)
     keep_ref[:, HALF:] = jnp.full((1, LANES), jnp.where(first, highest, neg_lowest))
     send_ref[:, HALF:] = jnp.full((1, LANES), jnp.where(first, neg_lowest, highest))
 
@@ -81,10 +89,11 @@
     shape = pltpu.VMEM((1, WIRE), jnp.float32)
     return pl.pallas_call(
         count_kernel,
-        out_shape=(shape, shape),
-        in_specs=[VMEM_SPEC],
-        out_specs=(VMEM_SPEC,) * 2,
-        scratch_shapes=[pltpu.VMEM(elevation.shape, jnp.float32)] * 2,
+        out_shape=(shape, shape, pltpu.VMEM(elevation.shape, jnp.float32)),
+        in_specs=[pl.BlockSpec(memory_space=pltpu.HBM)],
+        out_specs=(VMEM_SPEC,) * 3,
+        scratch_shapes=[pltpu.VMEM(elevation.shape, jnp.float32)] * 2
+        + [pltpu.SemaphoreType.DMA((4,))],
         name="count",
         compiler_params=SMALL,
     )(elevation)
@@ -220,6 +229,14 @@
     words = steps[:4] | (steps[4:] << 16)
 
     rows, width = bins.shape
+    for c in range(width // LANES):
+        cols = slice(c * LANES, (c + 1) * LANES)
+        gx = gx_ref[:, cols] * scale
+        gy = gy_ref[:, cols] * scale
+        light = (cos_zenith - (sin_zenith * light_y) * (gy - gx)) * lax.rsqrt(
+            1.0 + gx * gx + gy * gy
+        )
+        done[:, cols] = 0.5 / STEPS + jnp.maximum(light, 0.0) * (1.0 / STEPS)
     tables = [jnp.broadcast_to(words[r : r + 1], (rows, LANES)) for r in range(4)]
     pieces = sems.shape[0]
     piece = width // pieces
@@ -232,12 +249,7 @@
         odd = (code & 128) != 0
         word = jnp.where((code & 256) != 0, jnp.where(odd, w[3], w[2]), jnp.where(odd, w[1], w[0]))
         stretch = ((word >> ((code >> 5) & 16)) & 65535).astype(jnp.float32)
-        gx = gx_ref[:, cols] * scale
-        gy = gy_ref[:, cols] * scale
-        light = (cos_zenith - (sin_zenith * light_y) * (gy - gx)) * lax.rsqrt(
-            1.0 + gx * gx + gy * gy
-        )
-        done[:, cols] = stretch * (0.5 / STEPS + jnp.maximum(light, 0.0) * (1.0 / STEPS))
+        done[:, cols] = stretch * done[:, cols]
         if (c + 1) * LANES % piece == 0:
             n = len(copies)
             span_cols = slice(n * piece, (n + 1) * piece)
@@ -271,8 +283,7 @@
     begin = blocks * 3 // 4
     order = [(i + begin) % blocks for i in range(blocks)]
     alike = [[4 * i + place for i in order] for place in range(4)]
-    local = in_vmem(elevation)
-    keep, send = count(local)
+    keep, send, local = count(pltpu.with_memory_space_constraint(elevation, pltpu.HBM))
     received = lax.ppermute(send, "row", partner)
     beside = lax.ppermute(keep, "row", [(i, i ^ 2) for i in range(size)])
     across = lax.ppermute(send, "row", [(i, i ^ 3) for i in range(size)])
@@ -281,10 +292,10 @@
     )
     everyone = lax.all_to_all(spread, "row", 0, 0, axis_index_groups=alike, tiled=True)
 
-    above = lax.ppermute(elevation[-4:], "row", [(i, i + 1) for i in range(size - 1)])
-    below = lax.ppermute(elevation[:4], "row", [(i + 1, i) for i in range(size - 1)])
+    above = lax.ppermute(local[-4:], "row", [(i, i + 1) for i in range(size - 1)])
+    below = lax.ppermute(local[:4], "row", [(i + 1, i) for i in range(size - 1)])
     gx, gy, bins, limits = gradients(
-        in_vmem(above), local, in_vmem(below), in_vmem(ranks.reshape(1, 2))
+        in_vmem(above), in_vmem(local), in_vmem(below), in_vmem(ranks.reshape(1, 2))
     )
 
     mine = gather(in_vmem(everyone))

time: 60.6 us -> 60.5 us (level)
  local copies, waits for them, and re-layouts: 1.1 us -> 0.05 us
  Pallas kernels: 7.68 us -> 8.59 us
    unnamed x6 -> x2, local copies, waits for them, and re-layouts: 1.05 us -> 0.01 us
    pallas_call x1, Pallas kernels: 2.36 us -> 3.28 us  [count(): pl.pallas_call(count_kernel, out_shape=(shape, shape, pltpu.VMEM(elevatio...]
where the time goes in v7:
time: 60.5 us; the launch traced here: 60.3 us
  starting transfers between devices  43.1 us (71%)
  Pallas kernels  8.59 us (14%)
  waiting for transfers between devices  8.44 us (14%)
    ppermute x1, starting transfers between devices, body(): across = lax.ppermute(send, 'row', [(i, i ^ 3) for i in range(size)])  19.4 us
    all_to_all x1, starting transfers between devices, body(): lax.all_to_all(spread, 'row', 0, 0, axis_index_groups=alike, tiled=True)  12.8 us
    all_to_all x1, waiting for transfers between devices, body(): lax.all_to_all(spread, 'row', 0, 0, axis_index_groups=alike, tiled=True)  6.87 us
    ppermute x1, starting transfers between devices, body(): lax.ppermute(local[:4], 'row', [(i + 1, i) for i in range(size - 1)])  3.39 us
    pallas_call x1, Pallas kernels, count(): pl.pallas_call(count_kernel, out_shape=(shape, shape, pltpu.VMEM(elevatio...  3.28 us
    ppermute x1, starting transfers between devices, body(): beside = lax.ppermute(keep, 'row', [(i, i ^ 2) for i in range(size)])  2.78 us
    pallas_call x1, Pallas kernels, gradients(): pl.pallas_call(gradient_kernel, out_shape=(shape, shape, pltpu.VMEM(middl...  2.45 us
    ppermute x1, starting transfers between devices, body(): theirs = lax.ppermute(mine, 'row', partner)  2.43 us
  transfers between devices with their start and end apart: 7, of which 2 were waited for; matrix products, arithmetic and copies ran while one was open for 0% of the time, Pallas kernels for 4%

profile of v7, /device:TPU:37, one launch (start us, length us, event | category | flops | bytes accessed | tf_op | source)
XLA Modules:
  0.0 60.3 jit_solution(18154527993703828402)
XLA Ops:
  0.0 3.3 %count.1 = (f32[1,640]{1,0:T(1,128)S(1)}, f32[1,640]{1,0:T(1,128)S(1)}, f32[16,8192]{1,0:T(8,128)S(1)}) custom-call(f32[16,8192]{1,0:T(8,128)} %source.1), custom_call_target="tpu_custom_call" | custom-call | tf_op jit(solution)/shard_map/count/pallas_call | solution.py:90
  3.3 2.8 %collective-permute-start.1 = (f32[1,640]{1,0:T(1,128)S(1)}, f32[1,640]{1,0:T(1,128)S(1)}, u32[]{:S(2)}, u32[]{:S(2)}) collective-permute-start(f32[1,640]{1,0:T(1,128)S(1)} %get-tuple-element.12.a_ref), channel_id=1, source_target_pairs={{0,2},{1,3},{2,0},{3,1},{4,6},{5,7},{6,4},{7,5},{8,10},{9,11},{10,... | collective-permute-start | bytes 7688 | tf_op jit(solution)/shard_map/ppermute | solution.py:288
  6.1 19.4 %collective-permute-start.2 = (f32[1,640]{1,0:T(1,128)S(1)}, f32[1,640]{1,0:T(1,128)S(1)}, u32[]{:S(2)}, u32[]{:S(2)}) collective-permute-start(f32[1,640]{1,0:T(1,128)S(1)} %get-tuple-element.13), channel_id=1, source_target_pairs={{0,3},{1,2},{2,1},{3,0},{4,7},{5,6},{6,5},{7,4},{8,11},{9,10},{10,... | collective-permute-start | bytes 7688 | tf_op jit(solution)/shard_map/ppermute | solution.py:289
  25.5 0.0 collective-permute-start
  25.5 0.0 collective-permute-done.1.c_ref
  25.5 1.6 %collective-permute-done.2.d_ref = f32[1,640]{1,0:T(1,128)S(1)} collective-permute-done((f32[1,640]{1,0:T(1,128)S(1)}, f32[1,640]{1,0:T(1,128)S(1)}, u32[]{:S(2)}, u32[]{:S(2)}) %collective-permute-start.2) | collective-permute-done | bytes 2592 | tf_op jit(solution)/shard_map/ppermute | solution.py:289
  27.0 0.0 collective-permute-done.b_ref
  27.0 0.6 %join.1 = f32[16,1,640]{2,1,0:T(1,128)} custom-call(f32[1,640]{1,0:T(1,128)S(1)} %get-tuple-element.12.a_ref, f32[1,640]{1,0:T(1,128)S(1)} %collective-permute-done.b_ref, f32[1,640]{1,0:T(1,128)S(1)} %collective-permute-done.1.c_ref, f32[1,640]{1,0:T(1,128)S(1)} %collective-permute-done.2.d_ref), custom_call_target="tpu_custom_call" | custom-call | tf_op jit(solution)/shard_map/join/pallas_call | solution.py:111
  27.7 12.8 %all-to-all-start = ((f32[16,1,640]{2,1,0:T(1,128)}), f32[16,1,640]{2,1,0:T(1,128)S(1)}, u32[]{:S(2)}, u32[]{:S(2)}) async-start(f32[16,1,640]{2,1,0:T(1,128)} %join.1), calls=%async_computation | async-start | bytes 81920 | tf_op jit(solution)/shard_map/all_to_all | solution.py:293
  40.5 3.4 %collective-permute-start.5 = (f32[4,8192]{1,0:T(4,128)S(1)}, f32[4,8192]{1,0:T(4,128)S(1)}, u32[]{:S(2)}, u32[]{:S(2)}) collective-permute-start(f32[4,8192]{1,0:T(4,128)S(1)} %get-tuple-element.19), channel_id=1, source_target_pairs={{1,0},{2,1},{3,2},{4,3},{5,4},{6,5},{7,6},{8,7},{9,8},{10,9},{11,1... | collective-permute-start | bytes 393224 | tf_op jit(solution)/shard_map/ppermute | solution.py:296
  43.9 2.4 %collective-permute-start.4 = (f32[4,8192]{1,0:T(4,128)S(1)}, f32[4,8192]{1,0:T(4,128)S(1)}, u32[]{:S(2)}, u32[]{:S(2)}) collective-permute-start(f32[4,8192]{1,0:T(4,128)S(1)} %get-tuple-element.20), channel_id=1, source_target_pairs={{0,1},{1,2},{2,3},{3,4},{4,5},{5,6},{6,7},{7,8},{8,9},{9,10},{10,1... | collective-permute-start | bytes 393224 | tf_op jit(solution)/shard_map/ppermute | solution.py:295
  46.2 6.9 %all-to-all-done.x_ref = f32[16,1,640]{2,1,0:T(1,128)S(1)} async-done(((f32[16,1,640]{2,1,0:T(1,128)}), f32[16,1,640]{2,1,0:T(1,128)S(1)}, u32[]{:S(2)}, u32[]{:S(2)}) %all-to-all-start) | async-done | bytes 40992 | tf_op jit(solution)/shard_map/all_to_all | solution.py:293
  53.1 0.0 copy-start
  53.2 2.4 %collective-permute-start.3 = (f32[1,640]{1,0:T(1,128)S(1)}, f32[1,640]{1,0:T(1,128)S(1)}, u32[]{:S(2)}, u32[]{:S(2)}) collective-permute-start(f32[1,640]{1,0:T(1,128)S(1)} %gather.1.mine), channel_id=1, source_target_pairs={{0,1},{1,0},{2,3},{3,2},{4,5},{5,4},{6,7},{7,6},{8,9},{9,8},{10,11... | collective-permute-start | bytes 7688 | tf_op jit(solution)/shard_map/ppermute | solution.py:302
  55.6 0.0 collective-permute-done.5.below
  55.6 0.0 collective-permute-done.4.above
  55.6 0.0 copy-done
  55.6 2.4 %gradients.1 = (f32[16,8192]{1,0:T(8,128)S(1)}, f32[16,8192]{1,0:T(8,128)S(1)}, s32[16,8192]{1,0:T(8,128)S(1)}, s32[2,128]{1,0:T(2,128)S(1)}) custom-call(f32[4,8192]{1,0:T(4,128)S(1)} %collective-permute-done.4.above, f32[16,8192]{1,0:T(8,128)S(1)} %get-tuple-element.14.middle, f32[4,8192]{1,0:T(4,128)S(1)} %collective-permute-done.5.below, s32[1,2]{1,0:T(1,128)S(1)} %bitcast.1), custom_call_target="tpu_custom_call" | custom-call | tf_op jit(solution)/shard_map/gradients/pallas_call | solution.py:180
  58.1 0.0 collective-permute-done.3.theirs
  58.1 2.2 %shade.1 = f32[16,8192]{1,0:T(8,128)} custom-call(f32[1,640]{1,0:T(1,128)S(1)} %gather.1.mine, f32[1,640]{1,0:T(1,128)S(1)} %collective-permute-done.3.theirs, s32[2,128]{1,0:T(2,128)S(1)} %get-tuple-element.15.limits, s32[16,8192]{1,0:T(8,128)S(1)} %get-tuple-element.16.bins, f32[16,8192]{1,0:T(8,128)S(1)} %get-tuple-element.17.gx_ref, ...), custom_call_target="tpu_custom_call" | custom-call | tf_op jit(solution)/shard_map/shade/pallas_call | solution.py:265
  (2 shorter events, 0.1 us)
Async XLA Ops:
  3.3 22.2 %collective-permute-start.1 = (f32[1,640]{1,0:T(1,128)S(1)}, f32[1,640]{1,0:T(1,128)S(1)}, u32[]{:S(2)}, u32[]{:S(2)}) collective-permute-start(f32[1,640]{1,0:T(1,128)S(1)} %get-tuple-element.12.a_ref), channel_id=1, source_target_pairs={{0,2},{1,3},{2,0},{3,1},{4,6},{5,7},{6,4},{7,5},{8,10},{9,11},{10,... | collective-permute-start | bytes 7688 | tf_op jit(solution)/shard_map/ppermute | solution.py:288
  6.1 21.0 %collective-permute-start.2 = (f32[1,640]{1,0:T(1,128)S(1)}, f32[1,640]{1,0:T(1,128)S(1)}, u32[]{:S(2)}, u32[]{:S(2)}) collective-permute-start(f32[1,640]{1,0:T(1,128)S(1)} %get-tuple-element.13), channel_id=1, source_target_pairs={{0,3},{1,2},{2,1},{3,0},{4,7},{5,6},{6,5},{7,4},{8,11},{9,10},{10,... | collective-permute-start | bytes 7688 | tf_op jit(solution)/shard_map/ppermute | solution.py:289
  25.5 1.6 %collective-permute-start = (f32[1,640]{1,0:T(1,128)S(1)}, f32[1,640]{1,0:T(1,128)S(1)}, u32[]{:S(2)}, u32[]{:S(2)}) collective-permute-start(f32[1,640]{1,0:T(1,128)S(1)} %get-tuple-element.13), channel_id=1, source_target_pairs={{0,1},{1,0},{2,3},{3,2},{4,5},{5,4},{6,7},{7,6},{8,9},{9,8},{10,11... | collective-permute-start | bytes 7688 | tf_op jit(solution)/shard_map/ppermute | solution.py:287
  27.7 25.5 %all-to-all-start = ((f32[16,1,640]{2,1,0:T(1,128)}), f32[16,1,640]{2,1,0:T(1,128)S(1)}, u32[]{:S(2)}, u32[]{:S(2)}) async-start(f32[16,1,640]{2,1,0:T(1,128)} %join.1), calls=%async_computation | async-start | bytes 81920 | tf_op jit(solution)/shard_map/all_to_all | solution.py:293
  40.5 15.1 %collective-permute-start.5 = (f32[4,8192]{1,0:T(4,128)S(1)}, f32[4,8192]{1,0:T(4,128)S(1)}, u32[]{:S(2)}, u32[]{:S(2)}) collective-permute-start(f32[4,8192]{1,0:T(4,128)S(1)} %get-tuple-element.19), channel_id=1, source_target_pairs={{1,0},{2,1},{3,2},{4,3},{5,4},{6,5},{7,6},{8,7},{9,8},{10,9},{11,1... | collective-permute-start | bytes 393224 | tf_op jit(solution)/shard_map/ppermute | solution.py:296
  43.9 11.7 %collective-permute-start.4 = (f32[4,8192]{1,0:T(4,128)S(1)}, f32[4,8192]{1,0:T(4,128)S(1)}, u32[]{:S(2)}, u32[]{:S(2)}) collective-permute-start(f32[4,8192]{1,0:T(4,128)S(1)} %get-tuple-element.20), channel_id=1, source_target_pairs={{0,1},{1,2},{2,3},{3,4},{4,5},{5,6},{6,7},{7,8},{8,9},{9,10},{10,1... | collective-permute-start | bytes 393224 | tf_op jit(solution)/shard_map/ppermute | solution.py:295
  53.1 2.5 %copy-start = (s32[2]{0:T(128)S(1)}, s32[2]{0:T(128)}, u32[]{:S(2)}) copy-start(s32[2]{0:T(128)} %param.4) | copy-start | bytes 28
  53.2 4.9 %collective-permute-start.3 = (f32[1,640]{1,0:T(1,128)S(1)}, f32[1,640]{1,0:T(1,128)S(1)}, u32[]{:S(2)}, u32[]{:S(2)}) collective-permute-start(f32[1,640]{1,0:T(1,128)S(1)} %gather.1.mine), channel_id=1, source_target_pairs={{0,1},{1,0},{2,3},{3,2},{4,5},{5,4},{6,7},{7,6},{8,9},{9,8},{10,11... | collective-permute-start | bytes 7688 | tf_op jit(solution)/shard_map/ppermute | solution.py:302

commit v8 on v7

--- a/solution.py
+++ b/solution.py
@@ -77,8 +77,9 @@
         lower_row, upper_row = (flat[j : j + 1] for j in (4 * i, 4 * i + 16))
         keep_ref[:, cols] = jnp.where(first, lower_row, upper_row)
         send_ref[:, cols] = jnp.where(first, upper_row, lower_row)
-    keep_ref[:, HALF:] = jnp.full((1, LANES), jnp.where(first, highest, neg_lowest))
-    send_ref[:, HALF:] = jnp.full((1, LANES), jnp.where(first, neg_lowest, highest))
+    ends = jnp.where(iota((1, LANES), 1) < LANES // 2, highest, neg_lowest)
+    keep_ref[:, HALF:] = ends
+    send_ref[:, HALF:] = ends
 
 
 VMEM_SPEC = pl.BlockSpec(memory_space=pltpu.VMEM)
@@ -210,13 +211,36 @@
     return inside
 
 
-def shade_kernel(mine, theirs, limits, bins, gx_ref, gy_ref, out_ref, done, sems):
+def light_kernel(mine, gx_ref, gy_ref, out_ref):
+    ends = mine[:, HALF:]
+    span = ends + pltpu.roll(ends, LANES // 2, 1)
+    scale = zfactor / (8.0 * span)
+    for c in range(out_ref.shape[1] // LANES):
+        cols = slice(c * LANES, (c + 1) * LANES)
+        gx = gx_ref[:, cols] * scale
+        gy = gy_ref[:, cols] * scale
+        light = (cos_zenith - (sin_zenith * light_y) * (gy - gx)) * lax.rsqrt(
+            1.0 + gx * gx + gy * gy
+        )
+        out_ref[:, cols] = 0.5 / STEPS + jnp.maximum(light, 0.0) * (1.0 / STEPS)
+
+
+def lights(mine, gx, gy):
+    return pl.pallas_call(
+        light_kernel,
+        out_shape=pltpu.VMEM(gx.shape, jnp.float32),
+        in_specs=[VMEM_SPEC] * 3,
+        out_specs=VMEM_SPEC,
+        name="lights",
+        compiler_params=SMALL,
+    )(mine, gx, gy)
+
+
+def shade_kernel(mine, theirs, limits, bins, lit, out_ref, done, sems):
     first = lax.axis_index("row") & 1 == 0
     a, b = mine[...], theirs[...]
     lower = jnp.where(first, a, b)
     upper = jnp.where(first, b, a)
-    span = lower[:, HALF:] + upper[:, HALF:]
-    scale = zfactor / (8.0 * span)
     parts = [lower[:, i * LANES : (i + 1) * LANES] for i in range(4)]
     parts += [upper[:, i * LANES : (i + 1) * LANES] for i in range(4)]
     cumulative = prefix_sums(jnp.concatenate(parts, axis=0)).astype(jnp.int32)
@@ -229,14 +253,6 @@
     words = steps[:4] | (steps[4:] << 16)
 
     rows, width = bins.shape
-    for c in range(width // LANES):
-        cols = slice(c * LANES, (c + 1) * LANES)
-        gx = gx_ref[:, cols] * scale
-        gy = gy_ref[:, cols] * scale
-        light = (cos_zenith - (sin_zenith * light_y) * (gy - gx)) * lax.rsqrt(
-            1.0 + gx * gx + gy * gy
-        )
-        done[:, cols] = 0.5 / STEPS + jnp.maximum(light, 0.0) * (1.0 / STEPS)
     tables = [jnp.broadcast_to(words[r : r + 1], (rows, LANES)) for r in range(4)]
     pieces = sems.shape[0]
     piece = width // pieces
@@ -249,7 +265,7 @@
         odd = (code & 128) != 0
         word = jnp.where((code & 256) != 0, jnp.where(odd, w[3], w[2]), jnp.where(odd, w[1], w[0]))
         stretch = ((word >> ((code >> 5) & 16)) & 65535).astype(jnp.float32)
-        done[:, cols] = stretch * done[:, cols]
+        done[:, cols] = stretch * lit[:, cols]
         if (c + 1) * LANES % piece == 0:
             n = len(copies)
             span_cols = slice(n * piece, (n + 1) * piece)
@@ -261,19 +277,19 @@
         copy.wait()
 
 
-def shade(mine, theirs, limits, bins, gx, gy):
+def shade(mine, theirs, limits, bins, lit):
     return pl.pallas_call(
         shade_kernel,
-        out_shape=jax.ShapeDtypeStruct(gx.shape, jnp.float32),
-        in_specs=[VMEM_SPEC] * 6,
+        out_shape=jax.ShapeDtypeStruct(lit.shape, jnp.float32),
+        in_specs=[VMEM_SPEC] * 5,
         out_specs=pl.BlockSpec(memory_space=pl.ANY),
         scratch_shapes=[
-            pltpu.VMEM(gx.shape, jnp.float32),
+            pltpu.VMEM(lit.shape, jnp.float32),
             pltpu.SemaphoreType.DMA((16,)),
         ],
         name="shade",
         compiler_params=SMALL,
-    )(mine, theirs, limits, bins, gx, gy)
+    )(mine, theirs, limits, bins, lit)
 
 
 def body(elevation, ranks):
@@ -300,8 +316,9 @@
 
     mine = gather(in_vmem(everyone))
     theirs = lax.ppermute(mine, "row", partner)
+    lit = lights(in_vmem(mine), in_vmem(gx), in_vmem(gy))
     return shade(
-        in_vmem(mine), in_vmem(theirs), in_vmem(limits), in_vmem(bins), in_vmem(gx), in_vmem(gy)
+        in_vmem(mine), in_vmem(theirs), in_vmem(limits), in_vmem(bins), in_vmem(lit)
     )
 
 

time: 60.5 us -> 60.8 us (level)
    pallas_call x1 -> x2, Pallas kernels: 2.2 us -> 2.51 us  [the longest x1 2.19 us: shade(): pl.pallas_call(shade_kernel, out_shape=jax.ShapeDtypeStruct(lit.shape, jn...]
  transfers between devices with their start and end apart: 7 -> 7, of which waited for: 2 -> 2; matrix products, arithmetic and copies ran while one was open for 0% -> 0% of each run, Pallas kernels for 4% -> 5%
where the time goes in v8:
time: 60.8 us; the launch traced here: 60.6 us
  starting transfers between devices  43.1 us (71%)
  Pallas kernels  8.9 us (15%)
  waiting for transfers between devices  8.44 us (14%)
    ppermute x1, starting transfers between devices, body(): across = lax.ppermute(send, 'row', [(i, i ^ 3) for i in range(size)])  19.4 us
    all_to_all x1, starting transfers between devices, body(): lax.all_to_all(spread, 'row', 0, 0, axis_index_groups=alike, tiled=True)  12.8 us
    all_to_all x1, waiting for transfers between devices, body(): lax.all_to_all(spread, 'row', 0, 0, axis_index_groups=alike, tiled=True)  6.87 us
    ppermute x1, starting transfers between devices, body(): lax.ppermute(local[:4], 'row', [(i + 1, i) for i in range(size - 1)])  3.39 us
    pallas_call x1, Pallas kernels, count(): pl.pallas_call(count_kernel, out_shape=(shape, shape, pltpu.VMEM(elevatio...  3.28 us
    ppermute x1, starting transfers between devices, body(): beside = lax.ppermute(keep, 'row', [(i, i ^ 2) for i in range(size)])  2.78 us
    pallas_call x1, Pallas kernels, gradients(): pl.pallas_call(gradient_kernel, out_shape=(shape, shape, pltpu.VMEM(middl...  2.45 us
    ppermute x1, starting transfers between devices, body(): theirs = lax.ppermute(mine, 'row', partner)  2.43 us
  transfers between devices with their start and end apart: 7, of which 2 were waited for; matrix products, arithmetic and copies ran while one was open for 0% of the time, Pallas kernels for 5%

profile of v8, /device:TPU:37, one launch (start us, length us, event | category | flops | bytes accessed | tf_op | source)
XLA Modules:
  0.0 60.6 jit_solution(15544234330058698872)
XLA Ops:
  0.0 3.3 %count.1 = (f32[1,640]{1,0:T(1,128)S(1)}, f32[1,640]{1,0:T(1,128)S(1)}, f32[16,8192]{1,0:T(8,128)S(1)}) custom-call(f32[16,8192]{1,0:T(8,128)} %source.1), custom_call_target="tpu_custom_call" | custom-call | tf_op jit(solution)/shard_map/count/pallas_call | solution.py:91
  3.3 2.8 %collective-permute-start.1 = (f32[1,640]{1,0:T(1,128)S(1)}, f32[1,640]{1,0:T(1,128)S(1)}, u32[]{:S(2)}, u32[]{:S(2)}) collective-permute-start(f32[1,640]{1,0:T(1,128)S(1)} %get-tuple-element.12.a_ref), channel_id=1, source_target_pairs={{0,2},{1,3},{2,0},{3,1},{4,6},{5,7},{6,4},{7,5},{8,10},{9,11},{10,... | collective-permute-start | bytes 7688 | tf_op jit(solution)/shard_map/ppermute | solution.py:304
  6.1 19.4 %collective-permute-start.2 = (f32[1,640]{1,0:T(1,128)S(1)}, f32[1,640]{1,0:T(1,128)S(1)}, u32[]{:S(2)}, u32[]{:S(2)}) collective-permute-start(f32[1,640]{1,0:T(1,128)S(1)} %get-tuple-element.13), channel_id=1, source_target_pairs={{0,3},{1,2},{2,1},{3,0},{4,7},{5,6},{6,5},{7,4},{8,11},{9,10},{10,... | collective-permute-start | bytes 7688 | tf_op jit(solution)/shard_map/ppermute | solution.py:305
  25.5 0.0 collective-permute-start
  25.5 0.0 collective-permute-done.1.c_ref
  25.5 1.6 %collective-permute-done.2.d_ref = f32[1,640]{1,0:T(1,128)S(1)} collective-permute-done((f32[1,640]{1,0:T(1,128)S(1)}, f32[1,640]{1,0:T(1,128)S(1)}, u32[]{:S(2)}, u32[]{:S(2)}) %collective-permute-start.2) | collective-permute-done | bytes 2592 | tf_op jit(solution)/shard_map/ppermute | solution.py:305
  27.0 0.0 collective-permute-done.b_ref
  27.0 0.6 %join.1 = f32[16,1,640]{2,1,0:T(1,128)} custom-call(f32[1,640]{1,0:T(1,128)S(1)} %get-tuple-element.12.a_ref, f32[1,640]{1,0:T(1,128)S(1)} %collective-permute-done.b_ref, f32[1,640]{1,0:T(1,128)S(1)} %collective-permute-done.1.c_ref, f32[1,640]{1,0:T(1,128)S(1)} %collective-permute-done.2.d_ref), custom_call_target="tpu_custom_call" | custom-call | tf_op jit(solution)/shard_map/join/pallas_call | solution.py:112
  27.7 12.8 %all-to-all-start = ((f32[16,1,640]{2,1,0:T(1,128)}), f32[16,1,640]{2,1,0:T(1,128)S(1)}, u32[]{:S(2)}, u32[]{:S(2)}) async-start(f32[16,1,640]{2,1,0:T(1,128)} %join.1), calls=%async_computation | async-start | bytes 81920 | tf_op jit(solution)/shard_map/all_to_all | solution.py:309
  40.5 3.4 %collective-permute-start.5 = (f32[4,8192]{1,0:T(4,128)S(1)}, f32[4,8192]{1,0:T(4,128)S(1)}, u32[]{:S(2)}, u32[]{:S(2)}) collective-permute-start(f32[4,8192]{1,0:T(4,128)S(1)} %get-tuple-element.19), channel_id=1, source_target_pairs={{1,0},{2,1},{3,2},{4,3},{5,4},{6,5},{7,6},{8,7},{9,8},{10,9},{11,1... | collective-permute-start | bytes 393224 | tf_op jit(solution)/shard_map/ppermute | solution.py:312
  43.9 2.4 %collective-permute-start.4 = (f32[4,8192]{1,0:T(4,128)S(1)}, f32[4,8192]{1,0:T(4,128)S(1)}, u32[]{:S(2)}, u32[]{:S(2)}) collective-permute-start(f32[4,8192]{1,0:T(4,128)S(1)} %get-tuple-element.20), channel_id=1, source_target_pairs={{0,1},{1,2},{2,3},{3,4},{4,5},{5,6},{6,7},{7,8},{8,9},{9,10},{10,1... | collective-permute-start | bytes 393224 | tf_op jit(solution)/shard_map/ppermute | solution.py:311
  46.2 6.9 %all-to-all-done.x_ref = f32[16,1,640]{2,1,0:T(1,128)S(1)} async-done(((f32[16,1,640]{2,1,0:T(1,128)}), f32[16,1,640]{2,1,0:T(1,128)S(1)}, u32[]{:S(2)}, u32[]{:S(2)}) %all-to-all-start) | async-done | bytes 40992 | tf_op jit(solution)/shard_map/all_to_all | solution.py:309
  53.1 0.0 copy-start
  53.2 2.4 %collective-permute-start.3 = (f32[1,640]{1,0:T(1,128)S(1)}, f32[1,640]{1,0:T(1,128)S(1)}, u32[]{:S(2)}, u32[]{:S(2)}) collective-permute-start(f32[1,640]{1,0:T(1,128)S(1)} %gather.1.mine), channel_id=1, source_target_pairs={{0,1},{1,0},{2,3},{3,2},{4,5},{5,4},{6,7},{7,6},{8,9},{9,8},{10,11... | collective-permute-start | bytes 7688 | tf_op jit(solution)/shard_map/ppermute | solution.py:318
  55.6 0.0 collective-permute-done.5.below
  55.6 0.0 collective-permute-done.4.above
  55.6 0.0 copy-done
  55.6 2.4 %gradients.1 = (f32[16,8192]{1,0:T(8,128)S(1)}, f32[16,8192]{1,0:T(8,128)S(1)}, s32[16,8192]{1,0:T(8,128)S(1)}, s32[2,128]{1,0:T(2,128)S(1)}) custom-call(f32[4,8192]{1,0:T(4,128)S(1)} %collective-permute-done.4.above, f32[16,8192]{1,0:T(8,128)S(1)} %get-tuple-element.14.middle, f32[4,8192]{1,0:T(4,128)S(1)} %collective-permute-done.5.below, s32[1,2]{1,0:T(1,128)S(1)} %bitcast.1), custom_call_target="tpu_custom_call" | custom-call | tf_op jit(solution)/shard_map/gradients/pallas_call | solution.py:181
  58.1 0.3 lights.1.lit
  58.4 0.0 collective-permute-done.3.theirs
  58.4 2.2 %shade.1 = f32[16,8192]{1,0:T(8,128)} custom-call(f32[1,640]{1,0:T(1,128)S(1)} %gather.1.mine, f32[1,640]{1,0:T(1,128)S(1)} %collective-permute-done.3.theirs, s32[2,128]{1,0:T(2,128)S(1)} %get-tuple-element.15.limits, s32[16,8192]{1,0:T(8,128)S(1)} %get-tuple-element.16.bins, f32[16,8192]{1,0:T(8,128)S(1)} %lights.1.lit), custom_call_target="tpu_custom_call" | custom-call | tf_op jit(solution)/shard_map/shade/pallas_call | solution.py:281
  (2 shorter events, 0.1 us)
Async XLA Ops:
  3.3 22.2 %collective-permute-start.1 = (f32[1,640]{1,0:T(1,128)S(1)}, f32[1,640]{1,0:T(1,128)S(1)}, u32[]{:S(2)}, u32[]{:S(2)}) collective-permute-start(f32[1,640]{1,0:T(1,128)S(1)} %get-tuple-element.12.a_ref), channel_id=1, source_target_pairs={{0,2},{1,3},{2,0},{3,1},{4,6},{5,7},{6,4},{7,5},{8,10},{9,11},{10,... | collective-permute-start | bytes 7688 | tf_op jit(solution)/shard_map/ppermute | solution.py:304
  6.1 21.0 %collective-permute-start.2 = (f32[1,640]{1,0:T(1,128)S(1)}, f32[1,640]{1,0:T(1,128)S(1)}, u32[]{:S(2)}, u32[]{:S(2)}) collective-permute-start(f32[1,640]{1,0:T(1,128)S(1)} %get-tuple-element.13), channel_id=1, source_target_pairs={{0,3},{1,2},{2,1},{3,0},{4,7},{5,6},{6,5},{7,4},{8,11},{9,10},{10,... | collective-permute-start | bytes 7688 | tf_op jit(solution)/shard_map/ppermute | solution.py:305
  25.5 1.6 %collective-permute-start = (f32[1,640]{1,0:T(1,128)S(1)}, f32[1,640]{1,0:T(1,128)S(1)}, u32[]{:S(2)}, u32[]{:S(2)}) collective-permute-start(f32[1,640]{1,0:T(1,128)S(1)} %get-tuple-element.13), channel_id=1, source_target_pairs={{0,1},{1,0},{2,3},{3,2},{4,5},{5,4},{6,7},{7,6},{8,9},{9,8},{10,11... | collective-permute-start | bytes 7688 | tf_op jit(solution)/shard_map/ppermute | solution.py:303
  27.7 25.5 %all-to-all-start = ((f32[16,1,640]{2,1,0:T(1,128)}), f32[16,1,640]{2,1,0:T(1,128)S(1)}, u32[]{:S(2)}, u32[]{:S(2)}) async-start(f32[16,1,640]{2,1,0:T(1,128)} %join.1), calls=%async_computation | async-start | bytes 81920 | tf_op jit(solution)/shard_map/all_to_all | solution.py:309
  40.5 15.1 %collective-permute-start.5 = (f32[4,8192]{1,0:T(4,128)S(1)}, f32[4,8192]{1,0:T(4,128)S(1)}, u32[]{:S(2)}, u32[]{:S(2)}) collective-permute-start(f32[4,8192]{1,0:T(4,128)S(1)} %get-tuple-element.19), channel_id=1, source_target_pairs={{1,0},{2,1},{3,2},{4,3},{5,4},{6,5},{7,6},{8,7},{9,8},{10,9},{11,1... | collective-permute-start | bytes 393224 | tf_op jit(solution)/shard_map/ppermute | solution.py:312
  43.9 11.7 %collective-permute-start.4 = (f32[4,8192]{1,0:T(4,128)S(1)}, f32[4,8192]{1,0:T(4,128)S(1)}, u32[]{:S(2)}, u32[]{:S(2)}) collective-permute-start(f32[4,8192]{1,0:T(4,128)S(1)} %get-tuple-element.20), channel_id=1, source_target_pairs={{0,1},{1,2},{2,3},{3,4},{4,5},{5,6},{6,7},{7,8},{8,9},{9,10},{10,1... | collective-permute-start | bytes 393224 | tf_op jit(solution)/shard_map/ppermute | solution.py:311
  53.1 2.5 %copy-start = (s32[2]{0:T(128)S(1)}, s32[2]{0:T(128)}, u32[]{:S(2)}) copy-start(s32[2]{0:T(128)} %param.4) | copy-start | bytes 28
  53.2 5.2 %collective-permute-start.3 = (f32[1,640]{1,0:T(1,128)S(1)}, f32[1,640]{1,0:T(1,128)S(1)}, u32[]{:S(2)}, u32[]{:S(2)}) collective-permute-start(f32[1,640]{1,0:T(1,128)S(1)} %gather.1.mine), channel_id=1, source_target_pairs={{0,1},{1,0},{2,3},{3,2},{4,5},{5,4},{6,7},{7,6},{8,9},{9,8},{10,11... | collective-permute-start | bytes 7688 | tf_op jit(solution)/shard_map/ppermute | solution.py:318

commit v9 on v8

--- a/solution.py
+++ b/solution.py
@@ -16,7 +16,7 @@
 sin_zenith = 0.70710678
 light_y = 0.70710678
 HOT = jnp.float8_e4m3fn
-STEPS = 65535.0
+STEPS = 1023.0
 
 
 def bin_of(height):
@@ -170,7 +170,11 @@
         both = s4 + 8.0 * s3 + 28.0 * s2 + 56.0 * s1 + 70.0 * x[:, LANES : LANES + chunk]
         gx = east + pltpu.roll(east, tall - 1, 0)
         gy = pltpu.roll(both, tall - 1, 0) - both
-        bin_ref[:, c : c + chunk] = bin_of(middle[:, c : c + chunk]).astype(jnp.int32)
+        bins = bin_of(middle[:, c : c + chunk]).astype(jnp.int32)
+        row = bins >> 7
+        word = jnp.where(row >= 6, 2, jnp.where(row >= 3, 1, 0))
+        shift = (row - 3 * word) * 10
+        bin_ref[:, c : c + chunk] = (bins & (LANES - 1)) | (word << 7) | (shift << 9)
         gx_ref[:, c : c + chunk] = gx[:rows]
         gy_ref[:, c : c + chunk] = gy[:rows]
 
@@ -250,10 +254,14 @@
         1.0,
     )
     steps = jnp.floor(table * STEPS + 0.5).astype(jnp.int32)
-    words = steps[:4] | (steps[4:] << 16)
+    words = [
+        steps[0:1] | (steps[1:2] << 10) | (steps[2:3] << 20),
+        steps[3:4] | (steps[4:5] << 10) | (steps[5:6] << 20),
+        steps[6:7] | (steps[7:8] << 10),
+    ]
 
     rows, width = bins.shape
-    tables = [jnp.broadcast_to(words[r : r + 1], (rows, LANES)) for r in range(4)]
+    tables = [jnp.broadcast_to(word, (rows, LANES)) for word in words]
     pieces = sems.shape[0]
     piece = width // pieces
     copies = []
@@ -262,9 +270,8 @@
         code = bins[:, cols]
         low = code & (LANES - 1)
         w = [jnp.take_along_axis(t, low, axis=1, mode="promise_in_bounds") for t in tables]
-        odd = (code & 128) != 0
-        word = jnp.where((code & 256) != 0, jnp.where(odd, w[3], w[2]), jnp.where(odd, w[1], w[0]))
-        stretch = ((word >> ((code >> 5) & 16)) & 65535).astype(jnp.float32)
+        word = jnp.where((code & 256) != 0, w[2], jnp.where((code & 128) != 0, w[1], w[0]))
+        stretch = ((word >> (code >> 9)) & 1023).astype(jnp.float32)
         done[:, cols] = stretch * lit[:, cols]
         if (c + 1) * LANES % piece == 0:
             n = len(copies)
@@ -296,7 +303,7 @@
     size = lax.axis_size("row")
     partner = [(i, i ^ 1) for i in range(size)]
     blocks = size // 4
-    begin = blocks * 3 // 4
+    begin = blocks * 11 // 16
     order = [(i + begin) % blocks for i in range(blocks)]
     alike = [[4 * i + place for i in order] for place in range(4)]
     keep, send, local = count(pltpu.with_memory_space_constraint(elevation, pltpu.HBM))

time: 60.8 us -> 60.3 us (level)
  waiting for transfers between devices: 8.44 us -> 5.71 us
  starting transfers between devices: 43.1 us -> 45.4 us
    all_to_all x1, waiting for transfers between devices: 6.87 us -> 4.14 us  [body(): lax.all_to_all(spread, 'row', 0, 0, axis_index_groups=alike, tiled=True)]
    all_to_all x1, starting transfers between devices: 12.8 us -> 15.4 us  [body(): lax.all_to_all(spread, 'row', 0, 0, axis_index_groups=alike, tiled=True)]
where the time goes in v9:
time: 60.3 us; the launch traced here: 60.1 us
  starting transfers between devices  45.4 us (75%)
  Pallas kernels  8.84 us (15%)
  waiting for transfers between devices  5.71 us (9%)
    ppermute x1, starting transfers between devices, body(): across = lax.ppermute(send, 'row', [(i, i ^ 3) for i in range(size)])  19.4 us
    all_to_all x1, starting transfers between devices, body(): lax.all_to_all(spread, 'row', 0, 0, axis_index_groups=alike, tiled=True)  15.4 us
    all_to_all x1, waiting for transfers between devices, body(): lax.all_to_all(spread, 'row', 0, 0, axis_index_groups=alike, tiled=True)  4.14 us
    ppermute x1, starting transfers between devices, body(): lax.ppermute(local[:4], 'row', [(i + 1, i) for i in range(size - 1)])  3.39 us
    pallas_call x1, Pallas kernels, count(): pl.pallas_call(count_kernel, out_shape=(shape, shape, pltpu.VMEM(elevatio...  3.28 us
    ppermute x1, starting transfers between devices, body(): beside = lax.ppermute(keep, 'row', [(i, i ^ 2) for i in range(size)])  2.78 us
    pallas_call x1, Pallas kernels, gradients(): pl.pallas_call(gradient_kernel, out_shape=(shape, shape, pltpu.VMEM(middl...  2.7 us
    ppermute x1, starting transfers between devices, body(): lax.ppermute(local[-4:], 'row', [(i, i + 1) for i in range(size - 1)])  2.36 us
  transfers between devices with their start and end apart: 7, of which 2 were waited for; matrix products, arithmetic and copies ran while one was open for 0% of the time, Pallas kernels for 5%

profile of v9, /device:TPU:37, one launch (start us, length us, event | category | flops | bytes accessed | tf_op | source)
XLA Modules:
  0.0 60.1 jit_solution(12278112658559615064)
XLA Ops:
  0.0 3.3 %count.1 = (f32[1,640]{1,0:T(1,128)S(1)}, f32[1,640]{1,0:T(1,128)S(1)}, f32[16,8192]{1,0:T(8,128)S(1)}) custom-call(f32[16,8192]{1,0:T(8,128)} %source.1), custom_call_target="tpu_custom_call" | custom-call | tf_op jit(solution)/shard_map/count/pallas_call | solution.py:91
  3.3 2.8 %collective-permute-start.1 = (f32[1,640]{1,0:T(1,128)S(1)}, f32[1,640]{1,0:T(1,128)S(1)}, u32[]{:S(2)}, u32[]{:S(2)}) collective-permute-start(f32[1,640]{1,0:T(1,128)S(1)} %get-tuple-element.12.a_ref), channel_id=1, source_target_pairs={{0,2},{1,3},{2,0},{3,1},{4,6},{5,7},{6,4},{7,5},{8,10},{9,11},{10,... | collective-permute-start | bytes 7688 | tf_op jit(solution)/shard_map/ppermute | solution.py:311
  6.1 19.4 %collective-permute-start.2 = (f32[1,640]{1,0:T(1,128)S(1)}, f32[1,640]{1,0:T(1,128)S(1)}, u32[]{:S(2)}, u32[]{:S(2)}) collective-permute-start(f32[1,640]{1,0:T(1,128)S(1)} %get-tuple-element.13), channel_id=1, source_target_pairs={{0,3},{1,2},{2,1},{3,0},{4,7},{5,6},{6,5},{7,4},{8,11},{9,10},{10,... | collective-permute-start | bytes 7688 | tf_op jit(solution)/shard_map/ppermute | solution.py:312
  25.5 0.0 collective-permute-start
  25.5 0.0 collective-permute-done.1.c_ref
  25.5 1.6 %collective-permute-done.2.d_ref = f32[1,640]{1,0:T(1,128)S(1)} collective-permute-done((f32[1,640]{1,0:T(1,128)S(1)}, f32[1,640]{1,0:T(1,128)S(1)}, u32[]{:S(2)}, u32[]{:S(2)}) %collective-permute-start.2) | collective-permute-done | bytes 2592 | tf_op jit(solution)/shard_map/ppermute | solution.py:312
  27.0 0.0 collective-permute-done.b_ref
  27.0 0.6 %join.1 = f32[16,1,640]{2,1,0:T(1,128)} custom-call(f32[1,640]{1,0:T(1,128)S(1)} %get-tuple-element.12.a_ref, f32[1,640]{1,0:T(1,128)S(1)} %collective-permute-done.b_ref, f32[1,640]{1,0:T(1,128)S(1)} %collective-permute-done.1.c_ref, f32[1,640]{1,0:T(1,128)S(1)} %collective-permute-done.2.d_ref), custom_call_target="tpu_custom_call" | custom-call | tf_op jit(solution)/shard_map/join/pallas_call | solution.py:112
  27.7 15.4 %all-to-all-start = ((f32[16,1,640]{2,1,0:T(1,128)}), f32[16,1,640]{2,1,0:T(1,128)S(1)}, u32[]{:S(2)}, u32[]{:S(2)}) async-start(f32[16,1,640]{2,1,0:T(1,128)} %join.1), calls=%async_computation | async-start | bytes 81920 | tf_op jit(solution)/shard_map/all_to_all | solution.py:316
  43.1 3.4 %collective-permute-start.5 = (f32[4,8192]{1,0:T(4,128)S(1)}, f32[4,8192]{1,0:T(4,128)S(1)}, u32[]{:S(2)}, u32[]{:S(2)}) collective-permute-start(f32[4,8192]{1,0:T(4,128)S(1)} %get-tuple-element.19), channel_id=1, source_target_pairs={{1,0},{2,1},{3,2},{4,3},{5,4},{6,5},{7,6},{8,7},{9,8},{10,9},{11,1... | collective-permute-start | bytes 393224 | tf_op jit(solution)/shard_map/ppermute | solution.py:319
  46.5 2.4 %collective-permute-start.4 = (f32[4,8192]{1,0:T(4,128)S(1)}, f32[4,8192]{1,0:T(4,128)S(1)}, u32[]{:S(2)}, u32[]{:S(2)}) collective-permute-start(f32[4,8192]{1,0:T(4,128)S(1)} %get-tuple-element.20), channel_id=1, source_target_pairs={{0,1},{1,2},{2,3},{3,4},{4,5},{5,6},{6,7},{7,8},{8,9},{9,10},{10,1... | collective-permute-start | bytes 393224 | tf_op jit(solution)/shard_map/ppermute | solution.py:318
  48.8 4.1 %all-to-all-done.x_ref = f32[16,1,640]{2,1,0:T(1,128)S(1)} async-done(((f32[16,1,640]{2,1,0:T(1,128)}), f32[16,1,640]{2,1,0:T(1,128)S(1)}, u32[]{:S(2)}, u32[]{:S(2)}) %all-to-all-start) | async-done | bytes 40992 | tf_op jit(solution)/shard_map/all_to_all | solution.py:316
  53.0 0.0 copy-start
  53.0 2.1 %collective-permute-start.3 = (f32[1,640]{1,0:T(1,128)S(1)}, f32[1,640]{1,0:T(1,128)S(1)}, u32[]{:S(2)}, u32[]{:S(2)}) collective-permute-start(f32[1,640]{1,0:T(1,128)S(1)} %gather.1.mine), channel_id=1, source_target_pairs={{0,1},{1,0},{2,3},{3,2},{4,5},{5,4},{6,7},{7,6},{8,9},{9,8},{10,11... | collective-permute-start | bytes 7688 | tf_op jit(solution)/shard_map/ppermute | solution.py:325
  55.2 0.0 collective-permute-done.5.below
  55.2 0.0 collective-permute-done.4.above
  55.2 0.0 copy-done
  55.2 2.7 %gradients.1 = (f32[16,8192]{1,0:T(8,128)S(1)}, f32[16,8192]{1,0:T(8,128)S(1)}, s32[16,8192]{1,0:T(8,128)S(1)}, s32[2,128]{1,0:T(2,128)S(1)}) custom-call(f32[4,8192]{1,0:T(4,128)S(1)} %collective-permute-done.4.above, f32[16,8192]{1,0:T(8,128)S(1)} %get-tuple-element.14.middle, f32[4,8192]{1,0:T(4,128)S(1)} %collective-permute-done.5.below, s32[1,2]{1,0:T(1,128)S(1)} %bitcast.1), custom_call_target="tpu_custom_call" | custom-call | tf_op jit(solution)/shard_map/gradients/pallas_call | solution.py:185
  57.9 0.3 lights.1.lit
  58.2 0.0 collective-permute-done.3.theirs
  58.2 1.9 %shade.1 = f32[16,8192]{1,0:T(8,128)} custom-call(f32[1,640]{1,0:T(1,128)S(1)} %gather.1.mine, f32[1,640]{1,0:T(1,128)S(1)} %collective-permute-done.3.theirs, s32[2,128]{1,0:T(2,128)S(1)} %get-tuple-element.15.limits, s32[16,8192]{1,0:T(8,128)S(1)} %get-tuple-element.16.bins, f32[16,8192]{1,0:T(8,128)S(1)} %lights.1.lit), custom_call_target="tpu_custom_call" | custom-call | tf_op jit(solution)/shard_map/shade/pallas_call | solution.py:288
  (2 shorter events, 0.1 us)
Async XLA Ops:
  3.3 22.2 %collective-permute-start.1 = (f32[1,640]{1,0:T(1,128)S(1)}, f32[1,640]{1,0:T(1,128)S(1)}, u32[]{:S(2)}, u32[]{:S(2)}) collective-permute-start(f32[1,640]{1,0:T(1,128)S(1)} %get-tuple-element.12.a_ref), channel_id=1, source_target_pairs={{0,2},{1,3},{2,0},{3,1},{4,6},{5,7},{6,4},{7,5},{8,10},{9,11},{10,... | collective-permute-start | bytes 7688 | tf_op jit(solution)/shard_map/ppermute | solution.py:311
  6.1 21.0 %collective-permute-start.2 = (f32[1,640]{1,0:T(1,128)S(1)}, f32[1,640]{1,0:T(1,128)S(1)}, u32[]{:S(2)}, u32[]{:S(2)}) collective-permute-start(f32[1,640]{1,0:T(1,128)S(1)} %get-tuple-element.13), channel_id=1, source_target_pairs={{0,3},{1,2},{2,1},{3,0},{4,7},{5,6},{6,5},{7,4},{8,11},{9,10},{10,... | collective-permute-start | bytes 7688 | tf_op jit(solution)/shard_map/ppermute | solution.py:312
  25.5 1.6 %collective-permute-start = (f32[1,640]{1,0:T(1,128)S(1)}, f32[1,640]{1,0:T(1,128)S(1)}, u32[]{:S(2)}, u32[]{:S(2)}) collective-permute-start(f32[1,640]{1,0:T(1,128)S(1)} %get-tuple-element.13), channel_id=1, source_target_pairs={{0,1},{1,0},{2,3},{3,2},{4,5},{5,4},{6,7},{7,6},{8,9},{9,8},{10,11... | collective-permute-start | bytes 7688 | tf_op jit(solution)/shard_map/ppermute | solution.py:310
  27.7 25.3 %all-to-all-start = ((f32[16,1,640]{2,1,0:T(1,128)}), f32[16,1,640]{2,1,0:T(1,128)S(1)}, u32[]{:S(2)}, u32[]{:S(2)}) async-start(f32[16,1,640]{2,1,0:T(1,128)} %join.1), calls=%async_computation | async-start | bytes 81920 | tf_op jit(solution)/shard_map/all_to_all | solution.py:316
  43.1 12.1 %collective-permute-start.5 = (f32[4,8192]{1,0:T(4,128)S(1)}, f32[4,8192]{1,0:T(4,128)S(1)}, u32[]{:S(2)}, u32[]{:S(2)}) collective-permute-start(f32[4,8192]{1,0:T(4,128)S(1)} %get-tuple-element.19), channel_id=1, source_target_pairs={{1,0},{2,1},{3,2},{4,3},{5,4},{6,5},{7,6},{8,7},{9,8},{10,9},{11,1... | collective-permute-start | bytes 393224 | tf_op jit(solution)/shard_map/ppermute | solution.py:319
  46.5 8.7 %collective-permute-start.4 = (f32[4,8192]{1,0:T(4,128)S(1)}, f32[4,8192]{1,0:T(4,128)S(1)}, u32[]{:S(2)}, u32[]{:S(2)}) collective-permute-start(f32[4,8192]{1,0:T(4,128)S(1)} %get-tuple-element.20), channel_id=1, source_target_pairs={{0,1},{1,2},{2,3},{3,4},{4,5},{5,6},{6,7},{7,8},{8,9},{9,10},{10,1... | collective-permute-start | bytes 393224 | tf_op jit(solution)/shard_map/ppermute | solution.py:318
  53.0 2.2 %copy-start = (s32[2]{0:T(128)S(1)}, s32[2]{0:T(128)}, u32[]{:S(2)}) copy-start(s32[2]{0:T(128)} %param.4) | copy-start | bytes 28
  53.0 5.2 %collective-permute-start.3 = (f32[1,640]{1,0:T(1,128)S(1)}, f32[1,640]{1,0:T(1,128)S(1)}, u32[]{:S(2)}, u32[]{:S(2)}) collective-permute-start(f32[1,640]{1,0:T(1,128)S(1)} %gather.1.mine), channel_id=1, source_target_pairs={{0,1},{1,0},{2,3},{3,2},{4,5},{5,4},{6,7},{7,6},{8,9},{9,8},{10,11... | collective-permute-start | bytes 7688 | tf_op jit(solution)/shard_map/ppermute | solution.py:325
